TPU v7x, 32 devices: a whole 2x2x4 slice. The times are simulated.
32 devices in a mesh: rep: 8 (over y, x, core), shard: 4 (over z).
Axes of the slice: x: 2, y: 2, z: 4, core: 2. Of those that a mesh axis runs over, the one named last changes fastest.
Arguments:
- activations: bfloat16 [6, 4096, 2048], P(None, ('rep', 'shard')), may hold values from -50 to 50
- cotangents: bfloat16 [6, 4096, 512], P(None, ('rep', 'shard')), may hold values from -120 to 120
- momentum: float32 [12, 256, 2048], P(None, None, 'shard'), may hold values from -6 to 6
- owners: int32 [12], replicated, may hold values from 0 to 3, as said below
- bucket_starts: int32 [2], replicated, may hold values from 1 to 11, as said below
Outputs:
- momentum_out: float32 [12, 256, 2048], P(None, None, 'shard')
- update: float32 [12, 256, 2048], P(None, None, 'shard')
- owned: bfloat16 [16, 256, 2048], P('shard')
Inputs may be any that keep to these rules, and one draw needn't show every extreme that they name: `owners`: no owner is named more than 4 times, and some owner exactly 4 times. `bucket_starts`: strictly increasing.
All inputs are finite; a program needn't handle non-finite values.
Results may differ from a plain program's by a relative error of at most 0.033.
Values may be sent and summed in bfloat16 or wider, within the bound.
No kernel may reach another device: no remote copies, remote signals or barrier semaphores. Data moves between devices by JAX's collectives and lax.ppermute only.
A program may use at most 128 MiB of HBM per device.

v0:
```python
import math

import jax
import jax.numpy as jnp
from jax import lax
from jax.sharding import PartitionSpec as P

D = 2048
KV = 256
ITERS = 5
MATS = 12


coef_a = 3.4445
coef_b = -4.775
coef_c = 2.0315
momentum_rate = 0.95
clip_level = 0.5
epsilon = 1e-06


def orthogonal_batch(matrices):
    values = matrices.astype(jnp.float32)
    frobenius = jnp.sqrt(jnp.sum(values * values, axis=(1, 2), keepdims=True))
    matrix = (values / (frobenius + epsilon)).astype(jnp.bfloat16)
    for iteration in range(ITERS):
        gram_matrix = jnp.einsum(
            "skd,sjd->skj", matrix, matrix, preferred_element_type=jnp.float32
        ).astype(jnp.bfloat16)
        square = jnp.einsum(
            "skj,sji->ski", gram_matrix, gram_matrix, preferred_element_type=jnp.float32
        )
        mixing = (coef_b * gram_matrix.astype(jnp.float32) + coef_c * square).astype(jnp.bfloat16)
        product = jnp.einsum("skj,sjd->skd", mixing, matrix, preferred_element_type=jnp.float32)
        matrix = (coef_a * matrix.astype(jnp.float32) + product).astype(jnp.bfloat16)
    return matrix


def clip_factors(square_sums, bucket_starts):
    indices = jnp.arange(MATS, dtype=jnp.int32)
    buckets = jnp.sum((indices[:, None] >= bucket_starts[None, :]).astype(jnp.int32), axis=1)
    together = (buckets[:, None] == buckets[None, :]).astype(jnp.float32)
    totals = jnp.sum(together * square_sums[None, :], axis=1)
    members = jnp.sum(together, axis=1)
    root_mean = jnp.sqrt(totals / (members * KV * D) + epsilon)
    return jnp.minimum(1.0, clip_level / root_mean)


def slot_numbers(owners):
    indices = jnp.arange(MATS, dtype=jnp.int32)
    earlier = (indices[None, :] < indices[:, None]) & (owners[None, :] == owners[:, None])
    return jnp.sum(earlier.astype(jnp.int32), axis=1)


def selector(owner_of, slot_of, shard_count, slot_count):
    holders = lax.broadcasted_iota(jnp.int32, (shard_count, slot_count, 1), 0)
    places = lax.broadcasted_iota(jnp.int32, (shard_count, slot_count, 1), 1)
    chosen = (holders == owner_of[None, None, :]) & (places == slot_of[None, None, :])
    return chosen.astype(jnp.bfloat16)


def pack_slots(shards, chooser):
    return jnp.einsum("psm,mkd->skpd", chooser, shards, preferred_element_type=jnp.float32).astype(
        jnp.bfloat16
    )


def unpack_slots(received, chooser):
    return jnp.einsum("psm,skpd->mkd", chooser, received, preferred_element_type=jnp.float32)


def per_device(activations, cotangents, momentum, owners, bucket_starts):
    shard_count = lax.axis_size("shard")
    replica_count = lax.axis_size("rep")
    layers, tok_rows, width = activations.shape
    token_total = tok_rows * shard_count * replica_count
    columns = width // shard_count
    slot_count = -(-MATS // shard_count) + 1
    update_scale = math.sqrt(max(KV, D))
    partial_terms = jnp.einsum(
        "ltk,ltd->lkd", cotangents, activations, preferred_element_type=jnp.float32
    ).reshape(MATS, KV, width)
    shard_part = lax.psum_scatter(
        partial_terms.astype(jnp.bfloat16), "shard", scatter_dimension=2, tiled=True
    )
    summed = lax.psum(shard_part, "rep").astype(jnp.float32)
    gradient = summed / jnp.sqrt(jnp.float32(token_total))
    square_sums = lax.psum(jnp.sum(gradient * gradient, axis=(1, 2)), "shard")
    factors = clip_factors(square_sums, bucket_starts)
    momentum_out = momentum_rate * momentum + factors[:, None, None] * gradient
    nesterov = (factors[:, None, None] * gradient + momentum_rate * momentum_out).astype(
        jnp.bfloat16
    )
    slot_of = slot_numbers(owners)
    chooser = selector(owners, slot_of, shard_count, slot_count)
    received = lax.all_to_all(
        pack_slots(nesterov, chooser), "shard", split_axis=2, concat_axis=2, tiled=True
    )
    item_count = received.shape[0]
    result = orthogonal_batch(received.reshape(item_count, KV, width))
    scaled = (update_scale * result.astype(jnp.float32)).astype(jnp.bfloat16)
    returned_part = lax.all_to_all(
        result.reshape(item_count, KV, shard_count, columns),
        "shard",
        split_axis=2,
        concat_axis=2,
        tiled=True,
    )
    update = update_scale * unpack_slots(returned_part, chooser)
    return (momentum_out, update, scaled)


def solution(mesh):
    placed = (
        P(None, ("rep", "shard"), None),
        P(None, ("rep", "shard"), None),
        P(None, None, "shard"),
        P(),
        P(),
    )
    return jax.shard_map(
        per_device,
        mesh=mesh,
        in_specs=placed,
        out_specs=(P(None, None, "shard"), P(None, None, "shard"), P("shard", None, None)),
        check_vma=False,
    )
```

profile of v0, /device:TPU:0, one launch (start us, length us, event | category | flops | bytes accessed | tf_op | source)
XLA Modules:
  0.0 628.7 jit_solution(7850183555704222649)
XLA Ops:
  7.2 0.0 copy-start
  7.2 0.0 reduce-scatter.2.cloned.1.call-start
  7.2 1.8 copy-done
  9.1 7.5 %convolution_convert_fusion = bf16[6,512,2048]{2,1,0:T(8,128)(2,1)} fusion(bf16[6,128,512]{2,1,0:T(8,128)(2,1)} %param.6, bf16[6,128,2048]{2,1,0:T(8,128)(2,1)S(1)} %copy-done), kind=kOutput, calls=%fused_computation.13 | convolution fusion | flops 1616904192 | bytes 16515072 | tf_op jit(solution)/shard_map/ltk,ltd->lkd/dot_general | solution.py:80
  16.6 0.0 copy-start.3
  16.6 0.0 reduce-scatter.2.cloned.1.call-update
  16.6 0.0 copy-start.4
  16.6 0.0 all-reduce.2.cloned.1.call-start
  16.7 214.7 %reduce-scatter.2.cloned.1.call-done = bf16[12,256,512]{2,1,0:T(8,128)(2,1)} async-done(((bf16[12,256,2048]{2,1,0:T(8,128)(2,1)}), bf16[12,256,512]{2,1,0:T(8,128)(2,1)}) %reduce-scatter.2.cloned.1.call-update) | async-done | bytes 3145744 | tf_op jit(solution)/shard_map/reduce_scatter | solution.py:83
  231.4 0.0 all-reduce.2.cloned.1.call-update
  231.4 0.0 copy-done.3
  231.4 0.2 convert_reduce_fusion
  231.6 73.4 %all-reduce.2.cloned.1.call-done = bf16[12,256,512]{2,1,0:T(8,128)(2,1)} async-done(((bf16[12,256,512]{2,1,0:T(8,128)(2,1)}), bf16[12,256,512]{2,1,0:T(8,128)(2,1)}) %all-reduce.2.cloned.1.call-update) | async-done | bytes 3145744 | tf_op jit(solution)/shard_map/psum | solution.py:86
  305.0 2.9 fusion.4
  307.9 0.0 copy-done.4
  307.9 0.1 fusion.46
  308.0 11.7 %psum.15 = f32[12]{0:T(128)S(1)} all-reduce(f32[12]{0:T(128)S(1)} %fusion.4), channel_id=1, replica_groups=mesh['rep'=8,'shard'=4] {'shard'}, use_global_device_ids=true, to_apply=%region_4.0 | all-reduce | flops 12 | bytes 96 | tf_op jit(solution)/shard_map/psum | solution.py:88
  319.7 0.2 fusion.41
  319.9 8.1 %fusion.9 = (bf16[12,256,512,1]{2,1,0,3:T(8,128)(2,1)S(1)}, f32[12,256,512]{2,1,0:T(8,128)}) fusion(bf16[12,256,512]{2,1,0:T(8,128)(2,1)} %all-reduce.2.cloned.1.call-done, f32[12]{0:T(128)S(1)} %minimum_multiply_fusion, f32[12,256,512]{2,1,0:T(8,128)} %param.7), kind=kLoop, calls=%fused_computation.20 | loop fusion | flops 11010048 | bytes 18874416 | tf_op jit(solution)/shard_map/convert_element_type | solution.py:91
  327.9 2.8 fusion.6
  330.7 1.4 copy.28
  332.2 94.6 %all_to_all.10 = bf16[4,256,4,512]{3,0,1,2:T(4,128)(2,1)} all-to-all(bf16[4,256,4,512]{3,0,1,2:T(4,128)(2,1)S(1)} %copy.28), channel_id=1, replica_groups=mesh['rep'=8,'shard'=4] {'shard'}, dimensions={2} | all-to-all | bytes 8388608 | tf_op jit(solution)/shard_map/all_to_all | solution.py:96
  426.8 7.5 %copy.29 = bf16[4,256,4,512]{1,3,2,0:T(8,128)(2,1)} copy(bf16[4,256,4,512]{3,0,1,2:T(4,128)(2,1)} %all_to_all.10) | data formatting | bytes 8388608 | tf_op jit(solution)/shard_map/all_to_all | solution.py:96
  434.3 3.4 multiply_reduce_fusion
  437.6 6.9 %copy.30 = f32[4,256,2048]{2,1,0:T(8,128)} copy(bf16[4,256,2048]{1,2,0:T(8,128)(2,1)} %bitcast.48) | data formatting | bytes 12582912 | tf_op jit(solution)/shard_map/convert_element_type | solution.py:23
  444.6 4.6 divide_convert_fusion
  449.2 0.0 copy-start.2
  449.2 2.0 copy-done.2
  451.2 1.3 convolution_convert_fusion.6
  452.5 6.3 add_convert_fusion.4
  458.7 4.7 convolution_convert_fusion.5
  463.5 6.3 add_convert_fusion.3
  469.7 4.8 convolution_convert_fusion.4
  474.5 6.3 add_convert_fusion.2
  480.8 4.7 convolution_convert_fusion.3
  485.5 6.3 add_convert_fusion.1
  491.8 4.7 convolution_convert_fusion.2
  496.6 7.7 %multiply_convert_fusion = (bf16[4,256,2048]{2,1,0:T(8,128)(2,1)}, bf16[4,256,2048]{2,1,0:T(8,128)(2,1)}) fusion(bf16[4,256,2048]{2,1,0:T(8,128)(2,1)} %add_convert_fusion.1, bf16[4,256,256]{2,1,0:T(8,128)(2,1)S(1)} %convolution_convert_fusion.2), kind=kOutput, calls=%fused_computation.1 | convolution fusion | flops 1223950336 | bytes 13107200 | tf_op jit(solution)/shard_map/skj,sjd->skd/dot_general | solution.py:34
  504.3 7.8 %reshape.38 = bf16[4,256,4,512]{3,2,1,0:T(4,128)(2,1)} reshape(bf16[4,256,2048]{2,1,0:T(8,128)(2,1)} %get-tuple-element.20) | data formatting | bytes 8388608 | tf_op jit(solution)/shard_map/reshape | solution.py:103
  512.1 5.4 copy.31
  517.5 94.6 %all_to_all.11 = bf16[4,256,4,512]{3,0,1,2:T(4,128)(2,1)S(1)} all-to-all(bf16[4,256,4,512]{3,0,1,2:T(4,128)(2,1)S(1)} %copy.31), channel_id=1, replica_groups=mesh['rep'=8,'shard'=4] {'shard'}, dimensions={2} | all-to-all | bytes 8388608 | tf_op jit(solution)/shard_map/all_to_all | solution.py:102
  612.2 0.0 copy-start.1
  612.2 3.4 bitcast_multiply_fusion
  615.5 6.3 %copy.33 = f32[12,256,512]{2,1,0:T(8,128)} copy(f32[12,256,512]{2,0,1:T(8,128)S(1)} %bitcast_multiply_fusion) | data formatting | bytes 12582912
  621.9 0.0 copy-done.1
  (2 shorter events, 0.0 us)
Async XLA Ops:
  7.2 1.9 copy-start
  7.2 224.2 %reduce-scatter.2.cloned.1.call-start = ((), (), s32[]{:S(2)}) async-start(), calls=%async_computation.3 | async-start | bytes 15728640 | tf_op jit(solution)/shard_map/reduce_scatter | solution.py:83
  16.6 214.8 %copy-start.3 = (s32[12]{0:T(128)S(1)}, s32[12]{0:T(128)}, u32[]{:S(2)}) copy-start(s32[12]{0:T(128)} %param.8) | copy-start | bytes 148
  16.6 291.3 %copy-start.4 = (s32[2]{0:T(128)S(1)}, s32[2]{0:T(128)}, u32[]{:S(2)}) copy-start(s32[2]{0:T(128)} %param.9) | copy-start | bytes 28
  16.6 288.4 %all-reduce.2.cloned.1.call-start = ((), (), s32[]{:S(2)}) async-start(), calls=%async_computation.4 | async-start | bytes 6291456 | tf_op jit(solution)/shard_map/psum | solution.py:86
  449.2 2.0 copy-start.2
  612.2 9.7 %copy-start.1 = (bf16[6,128,2048]{2,1,0:T(8,128)(2,1)S(1)}, bf16[6,128,2048]{2,1,0:T(8,128)(2,1)}, u32[]{:S(2)}) copy-start(bf16[6,128,2048]{2,1,0:T(8,128)(2,1)} %param.5) | copy-start | bytes 9437188
Sparse Core Ops, SparseCore 0:
  16.7 214.6 reduce-scatter.1
  234.7 70.3 all-reduce.1
where the time goes:
time: 630 us; the launch traced here: 629 us
  waiting for transfers between devices  288 us (46%)
  blocking collectives  201 us (32%)
  matrix products  66.7 us (11%)
  local copies, waits for them, and re-layouts  39.3 us (6%)
  other arithmetic  19.4 us (3%)
  between operations  14.1 us (2%)
    reduce_scatter x1, waiting for transfers between devices, per_device(): lax.psum_scatter(partial_terms.astype(jnp.bfloat16), 'shard', scatter_dim...  215 us
    all_to_all x1, blocking collectives, per_device(): lax.all_to_all(result.reshape(item_count, KV, shard_count, columns), 'sha...  94.6 us
    all_to_all x1, blocking collectives, per_device(): lax.all_to_all(pack_slots(nesterov, chooser), 'shard', split_axis=2, conc...  94.6 us
    psum x1, waiting for transfers between devices, per_device(): summed = lax.psum(shard_part, 'rep').astype(jnp.float32)  73.4 us
    dot_general x5, matrix products, orthogonal_batch(): jnp.einsum('skj,sjd->skd', mixing, matrix, preferred_element_type=jnp.flo...  32.7 us
    dot_general x5, matrix products, orthogonal_batch(): jnp.einsum('skd,sjd->skj', matrix, matrix, preferred_element_type=jnp.flo...  20.3 us
    reshape x2, local copies, waits for them, and re-layouts, per_device(): result.reshape(item_count, KV, shard_count, columns)  13.2 us
  transfers between devices with their start and end apart: 2, of which 2 were waited for; matrix products, arithmetic and copies ran while one was open for 0% of the time, Pallas kernels for 0%

commit v1 on v0

v1 whole, which is shorter than its diff:
```python
import functools
import math

import jax
import jax.numpy as jnp
from jax import lax
from jax.experimental import pallas as pl
from jax.experimental.pallas import tpu as pltpu
from jax.sharding import PartitionSpec as P

ITERS = 5

coef_a = 3.4445
coef_b = -4.775
coef_c = 2.0315
momentum_rate = 0.95
clip_level = 0.5
epsilon = 1e-06


F32 = jnp.float32
BF16 = jnp.bfloat16
NT = (((1,), (1,)), ((), ()))
NN = (((1,), (0,)), ((), ()))

CORE, BIT_X, BIT_Y = 1, 2, 4
CHIPS = 4
GROUPS = 3


def dot(a, b, dims):
    return lax.dot_general(a, b, dims, preferred_element_type=F32)


def swap_rep(value, bit):
    count = lax.axis_size("rep")
    return lax.ppermute(value, "rep", [(i, i ^ bit) for i in range(count)])


def swap_shard(value, bit, wanted=lambda source, target: True):
    count = lax.axis_size("shard")
    pairs = [(i, i ^ bit) for i in range(count) if wanted(i, i ^ bit)]
    return lax.ppermute(value, "shard", pairs)


def pick(value, index, axis=0):
    return lax.dynamic_index_in_dim(value, index, axis, keepdims=False)


def add(a, b):
    return (a.astype(F32) + b.astype(F32)).astype(BF16)


VMEM = pl.BlockSpec(memory_space=pltpu.VMEM)
ANY = pl.BlockSpec(memory_space=pl.ANY)
SMEM = pl.BlockSpec(memory_space=pltpu.SMEM)

AT_CORE, AT_X, AT_Y, AT_Z, AT_CHIP, AT_SHARD, AT_PLACE, AT_LOW, AT_LISTS = range(9)


def unit_of(matrix):
    return matrix // CHIPS


def chip_of(matrix):
    place = matrix % CHIPS
    turned = 2 * (place % 2) + place // 2
    if isinstance(matrix, int):
        return turned if matrix < CHIPS else place
    return jnp.where(matrix < CHIPS, turned, place)


def matrix_of(table, unit):
    chip = table[AT_CHIP]
    if isinstance(unit, int):
        return CHIPS * unit + chip if unit else 2 * table[AT_X] + table[AT_Y]
    return jnp.where(unit == 0, 2 * table[AT_X] + table[AT_Y], CHIPS * unit + chip)


def load_kernel(table, activations, cotangents, *rest):
    outs, sems = rest[:-1], rest[-1]
    width = activations.shape[2]
    copies = []
    for group, out in enumerate(outs):
        layer = table[group]
        copies.append(
            pltpu.make_async_copy(activations.at[layer], out.at[:, :width], sems.at[2 * group])
        )
        copies.append(
            pltpu.make_async_copy(cotangents.at[layer], out.at[:, width:], sems.at[2 * group + 1])
        )
    for copy in copies:
        copy.start()
    for copy in copies:
        copy.wait()


def load_layers(layers, activations, cotangents):
    _, tokens, width = activations.shape
    terms = cotangents.shape[2]
    return pl.pallas_call(
        load_kernel,
        in_specs=[SMEM, ANY, ANY],
        out_specs=[VMEM] * GROUPS,
        out_shape=[jax.ShapeDtypeStruct((tokens, width + terms), BF16)] * GROUPS,
        scratch_shapes=[pltpu.SemaphoreType.DMA((2 * GROUPS,))],
        cost_estimate=pl.CostEstimate(
            flops=GROUPS * tokens * width * 100, bytes_accessed=4 * GROUPS * tokens * (width + terms),
            transcendentals=0,
        ),
        name="load_layers",
    )(jnp.stack(layers), activations, cotangents)


def gradient_rows(table, group, width, half, sources, turned):
    for source, ref in enumerate(sources):
        tokens = ref.shape[0]
        for part in range(2):
            kind = part
            if group == 0:
                kind = 1 - table[AT_Y] if part else table[AT_Y]
            at = pl.multiple_of(width + (2 * kind + table[AT_CORE]) * half, half)
            turned[part * half:(part + 1) * half, source * tokens:(source + 1) * tokens] = ref[
                :, pl.ds(at, half)
            ].T


def local_kernel(width, blocks, table, mine0, mine1, mine2, sib0, sib1, sib2, out0, out1, out2, turned):
    half = turned.shape[1] // 2
    columns = width // blocks
    for group, (mine, sib, out) in enumerate(((mine0, sib0, out0), (mine1, sib1, out1), (mine2, sib2, out2))):
        sources = (mine, sib)
        gradient_rows(table, group, width, half, sources, turned.at[group])
        for block in range(blocks):
            span = slice(block * columns, (block + 1) * columns)
            values = jnp.concatenate([ref[:, span] for ref in sources], axis=0)
            out[:, span] = dot(turned[group], values, NN)


def gradient_kernel(group, width, blocks, table, local, got, fwd, keep, send, turned):
    half = turned.shape[0] // 2
    columns = width // blocks
    sources = (got, fwd)
    gradient_rows(table, group, width, half, sources, turned)
    for block in range(blocks):
        span = slice(block * columns, (block + 1) * columns)
        values = jnp.concatenate([ref[:, span] for ref in sources], axis=0)
        terms = (local[:, span] + dot(turned[...], values, NN)).astype(BF16)
        if group == 0:
            keep[block] = terms[:half]
            send[block] = terms[half:]
            continue
        if group == 1:
            bit, value, at = table[AT_Z], block % 2, block // 2
        else:
            bit, value, at = table[AT_LOW], block // (blocks // 2), block % (blocks // 2)

        @pl.when(bit == value)
        def _():
            keep[0, at] = terms[:half]
            keep[1, at] = terms[half:]

        @pl.when(bit != value)
        def _():
            send[0, at] = terms[:half]
            send[1, at] = terms[half:]


def local_gradients(table, mine, sib, width, blocks, half):
    tokens = mine[0].shape[0]
    return pl.pallas_call(
        functools.partial(local_kernel, width, blocks),
        in_specs=[SMEM] + [VMEM] * 6,
        out_specs=[VMEM] * GROUPS,
        out_shape=[jax.ShapeDtypeStruct((2 * half, width), F32)] * GROUPS,
        scratch_shapes=[pltpu.VMEM((GROUPS, 2 * half, 2 * tokens), BF16)],
        cost_estimate=pl.CostEstimate(
            flops=GROUPS * 2 * 2 * tokens * 2 * half * width, bytes_accessed=GROUPS * 12 * tokens * width,
            transcendentals=0,
        ),
        name="local_gradients",
    )(table, *mine, *sib)


def layer_gradient(group, table, local, got, fwd, width, blocks, half):
    columns = width // blocks
    tokens = got.shape[0]
    shape = (blocks, half, columns) if group == 0 else (2, blocks // 2, half, columns)
    return pl.pallas_call(
        functools.partial(gradient_kernel, group, width, blocks),
        in_specs=[SMEM] + [VMEM] * 3,
        out_specs=[VMEM] * 2,
        out_shape=[jax.ShapeDtypeStruct(shape, BF16)] * 2,
        scratch_shapes=[pltpu.VMEM((2 * half, 2 * tokens), BF16)],
        cost_estimate=pl.CostEstimate(
            flops=2 * 2 * tokens * 2 * half * width, bytes_accessed=12 * tokens * width, transcendentals=0
        ),
        name="layer_gradient",
    )(table, local, got, fwd)


def finish_kernel(scale, table, keep, got, keep_last, got_last, out, last, sums):
    lane = lax.broadcasted_iota(jnp.int32, sums.shape, 1)
    held = (
        matrix_of(table, 0),
        matrix_of(table, 1),
        2 * CHIPS + 2 * table[AT_Z] + table[AT_X],
    )
    total = jnp.zeros(sums.shape, F32)
    for unit in range(GROUPS):
        if unit < GROUPS - 1:
            values = keep[unit, table[AT_LOW]].astype(F32) + got[unit].astype(F32)
        else:
            values = keep_last[...].astype(F32) + got_last[...].astype(F32)
        values = (values * scale).astype(BF16)
        if unit < GROUPS - 1:
            out[unit] = values
        else:
            last[...] = values
        wide = values.astype(F32)
        total = total + jnp.where(lane == held[unit], jnp.sum(wide * wide), 0.0)
    sums[...] = total


def finish(scale, table, keep, got, keep_last, got_last):
    return pl.pallas_call(
        functools.partial(finish_kernel, scale),
        in_specs=[SMEM] + [VMEM] * 4,
        out_specs=[VMEM] * 3,
        out_shape=[
            jax.ShapeDtypeStruct(got.shape, BF16),
            jax.ShapeDtypeStruct(got_last.shape, BF16),
            jax.ShapeDtypeStruct((1, 128), F32),
        ],
        cost_estimate=pl.CostEstimate(flops=1000 * got.size, bytes_accessed=8 * got.size, transcendentals=0),
        name="finish",
    )(table, keep, got, keep_last, got_last)


def momentum_kernel(table, factors, own, sib, momentum, momentum_out, nesterov, buffer, came, left):
    core, chip = table[AT_CORE], table[AT_CHIP]
    half = own.shape[2]
    mats = buffer.shape[0]
    ins = [pltpu.make_async_copy(momentum.at[m], buffer.at[m], came.at[m]) for m in range(mats)]
    outs = [pltpu.make_async_copy(buffer.at[m], momentum_out.at[m], left.at[m]) for m in range(mats)]
    for copy in ins:
        copy.start()
    for matrix in range(mats):
        ins[matrix].wait()
        factor = factors[matrix]
        place, unit = chip_of(matrix) ^ chip, unit_of(matrix)
        for part, ref in ((core, own), (1 - core, sib)):
            rows = pl.ds(pl.multiple_of(part * half, half), half)
            step = factor * ref[place, unit].astype(F32)
            fresh = momentum_rate * buffer[matrix, rows, :] + step
            buffer[matrix, rows, :] = fresh
            nesterov[matrix, rows, :] = (step + momentum_rate * fresh).astype(BF16)
        outs[matrix].start()
    for copy in outs:
        copy.wait()


def momentum_step(table, factors, own, sib, momentum):
    mats, rows, columns = momentum.shape
    return pl.pallas_call(
        momentum_kernel,
        in_specs=[SMEM, SMEM, VMEM, VMEM, ANY],
        out_specs=[ANY, VMEM],
        out_shape=[
            jax.ShapeDtypeStruct(momentum.shape, F32),
            jax.ShapeDtypeStruct(momentum.shape, BF16),
        ],
        scratch_shapes=[
            pltpu.VMEM(momentum.shape, F32), pltpu.SemaphoreType.DMA((mats,)), pltpu.SemaphoreType.DMA((mats,))
        ],
        cost_estimate=pl.CostEstimate(
            flops=mats * rows * columns * 400, bytes_accessed=12 * mats * rows * columns, transcendentals=0
        ),
        name="momentum_step",
    )(table, factors, own, sib, momentum)


def rows_kernel(table, factors, gradient, old, *outs):
    for k, out in enumerate(outs):
        unit = jnp.minimum(table[AT_SHARD] ^ k, GROUPS - 1)
        step = factors[matrix_of(table, unit)] * gradient[unit].astype(F32)
        fresh = momentum_rate * old[unit] + step
        out[...] = (step + momentum_rate * fresh).astype(BF16)


def newton_rows(table, factors, gradient, old, shard_count):
    _, half, columns = gradient.shape
    return pl.pallas_call(
        rows_kernel,
        in_specs=[SMEM, SMEM, VMEM, VMEM],
        out_specs=[VMEM] * shard_count,
        out_shape=[jax.ShapeDtypeStruct((half, columns), BF16)] * shard_count,
        cost_estimate=pl.CostEstimate(
            flops=shard_count * half * columns * 100, bytes_accessed=8 * shard_count * half * columns,
            transcendentals=0,
        ),
        name="newton_rows",
    )(table, factors, gradient, old)


def carried_kernel(targets, table, factors, own, *rest):
    refs, outs, sems = rest[0], rest[1:-2], rest[-2:]
    buffer, sem = sems
    core, chip, shard = table[AT_CORE], table[AT_CHIP], table[AT_SHARD]
    half = own.shape[2]
    matrices = [table[AT_LISTS + (shard ^ k)] for k in targets]
    copies = []
    for i, matrix in enumerate(matrices):
        rows = pl.ds(pl.multiple_of(core * half, half), half)
        copies.append(pltpu.make_async_copy(refs.at[matrix, rows, :], buffer.at[i], sem.at[i]))
        copies[-1].start()
    for i, matrix in enumerate(matrices):
        copies[i].wait()
        step = factors[matrix] * own[chip_of(matrix) ^ chip, unit_of(matrix)].astype(F32)
        fresh = momentum_rate * buffer[i] + step
        outs[i][...] = (step + momentum_rate * fresh).astype(BF16)


def carried_rows(table, factors, own, momentum, shard_count):
    half, columns = own.shape[2:]
    targets = tuple(range(1, shard_count))
    count = len(targets)
    return pl.pallas_call(
        functools.partial(carried_kernel, targets),
        in_specs=[SMEM, SMEM, VMEM, ANY],
        out_specs=[VMEM] * count,
        out_shape=[jax.ShapeDtypeStruct((half, columns), BF16)] * count,
        scratch_shapes=[pltpu.VMEM((count, half, columns), F32), pltpu.SemaphoreType.DMA((count,))],
        cost_estimate=pl.CostEstimate(
            flops=count * half * columns * 100, bytes_accessed=8 * count * half * columns, transcendentals=0
        ),
        name="carried_rows",
    )(table, factors, own, momentum)


def newton_kernel(table, own, sib, out, x, mix):
    core = table[AT_CORE]
    parts, half, columns = own.shape
    spans = [slice(p * columns, (p + 1) * columns) for p in range(parts)]
    total = jnp.zeros((1, 1), F32)
    for part, ref in ((core, own), (1 - core, sib)):
        rows = pl.ds(pl.multiple_of(part * half, half), half)
        for p, span in enumerate(spans):
            x[rows, span] = ref[p]
            wide = ref[p].astype(F32)
            total = total + jnp.sum(wide * wide)
    inverse = 1.0 / (jnp.sqrt(total) + epsilon)
    for span in spans:
        x[:, span] = (x[:, span].astype(F32) * inverse).astype(BF16)
    size = 2 * half
    diagonal = lax.broadcasted_iota(jnp.int32, (size, size), 0) == lax.broadcasted_iota(
        jnp.int32, (size, size), 1
    )
    for iteration in range(ITERS):
        gram = dot(x[...], x[...], NT).astype(BF16)
        square = dot(gram, gram, NN)
        mixing = (coef_b * gram.astype(F32) + coef_c * square).astype(BF16)
        if iteration < ITERS - 1:
            for span in spans:
                block = x[:, span]
                x[:, span] = (coef_a * block.astype(F32) + dot(mixing, block, NN)).astype(BF16)
        if iteration == 0:
            mix[...] = jnp.where(diagonal, coef_a, 0.0) + mixing.astype(F32)
        else:
            product = mix[...]
            high = product.astype(BF16)
            low = (product - high.astype(F32)).astype(BF16)
            mix[...] = coef_a * product + (dot(mixing, high, NN) + dot(mixing, low, NN))
    out[...] = (mix[pl.ds(pl.multiple_of(core * half, half), half), :] * inverse).astype(BF16)


def newton(table, own, sib):
    parts, half, columns = own.shape
    size = 2 * half
    return pl.pallas_call(
        newton_kernel,
        in_specs=[SMEM, VMEM, VMEM],
        out_specs=VMEM,
        scratch_shapes=[pltpu.VMEM((size, parts * columns), BF16), pltpu.VMEM((size, size), F32)],
        out_shape=jax.ShapeDtypeStruct((half, size), BF16),
        cost_estimate=pl.CostEstimate(
            flops=ITERS * 2 * size * size * (2 * parts * columns + 3 * size),
            bytes_accessed=8 * size * parts * columns, transcendentals=0,
        ),
        name="newton",
    )(table, own, sib)


def gather_rows(core, own, sib, out):
    half = own.shape[0]
    for part, block in ((core, own), (1 - core, sib)):
        out[pl.ds(pl.multiple_of(part * half, half), half), :] = block


def apply_kernel(scale, first, table, own, sib, values, own_rows, sib_rows, update, owned,
                 mix, rows, whole, held, sems):
    core, chip, shard = table[AT_CORE], table[AT_CHIP], table[AT_SHARD]
    mats = values.shape[0]
    slots, others, _, columns = own_rows.shape
    copies = []

    def leave(source, target):
        copies.append(pltpu.make_async_copy(source, target, sems.at[len(copies)]))
        copies[-1].start()

    for slot in range(slots):
        matrix = table[first + slot]
        filled = table[first + slots + slot] > 0
        place, unit = chip_of(matrix) ^ chip, unit_of(matrix)
        gather_rows(core, own[place, unit], sib[place, unit], mix.at[slot])
        at = table[AT_PLACE] ^ slot
        for k in range(others + 1):
            if k == 0:
                block = values[matrix]
            else:
                gather_rows(core, own_rows[at, k - 1], sib_rows[at, k - 1], rows.at[k - 1])
                block = rows[k - 1]
            result = scale * dot(mix[slot], block, NN).astype(BF16).astype(F32)
            span = pl.ds(pl.multiple_of((shard ^ k) * columns, columns), columns)
            held[slot, :, span] = jnp.where(filled, result, 0.0).astype(BF16)
        leave(held.at[slot], owned.at[slot])
    for matrix in range(mats):
        place, unit = chip_of(matrix) ^ chip, unit_of(matrix)
        gather_rows(core, own[place, unit], sib[place, unit], mix.at[slots + matrix])
        whole[matrix] = scale * dot(mix[slots + matrix], values[matrix], NN).astype(BF16).astype(F32)
        leave(whole.at[matrix], update.at[matrix])
    for copy in copies:
        copy.wait()


def apply_step(scale, table, own, sib, values, own_rows, sib_rows, shard_count):
    mats, rows, columns = values.shape
    slots, others, _, _ = own_rows.shape
    width = (others + 1) * columns
    return pl.pallas_call(
        functools.partial(apply_kernel, scale, AT_LISTS + shard_count),
        in_specs=[SMEM] + [VMEM] * 5,
        out_specs=[ANY, ANY],
        out_shape=[
            jax.ShapeDtypeStruct(values.shape, F32),
            jax.ShapeDtypeStruct((slots, rows, width), BF16),
        ],
        scratch_shapes=[
            pltpu.VMEM((slots + mats, rows, rows), BF16),
            pltpu.VMEM((others, rows, columns), BF16),
            pltpu.VMEM(values.shape, F32),
            pltpu.VMEM((slots, rows, width), BF16),
            pltpu.SemaphoreType.DMA((slots + mats,)),
        ],
        cost_estimate=pl.CostEstimate(
            flops=2 * rows * rows * (mats * columns + slots * width),
            bytes_accessed=6 * mats * rows * columns + 2 * slots * rows * width, transcendentals=0,
        ),
        name="apply_step",
    )(table, own, sib, values, own_rows, sib_rows)


def clip_factors(square_sums, bucket_starts, elements):
    mats = square_sums.shape[0]
    indices = jnp.arange(mats, dtype=jnp.int32)
    buckets = jnp.sum((indices[:, None] >= bucket_starts[None, :]).astype(jnp.int32), axis=1)
    together = (buckets[:, None] == buckets[None, :]).astype(F32)
    totals = jnp.sum(together * square_sums[None, :], axis=1)
    members = jnp.sum(together, axis=1)
    root_mean = jnp.sqrt(totals / (members * elements) + epsilon)
    return jnp.minimum(1.0, clip_level / root_mean)


def slot_numbers(owners):
    indices = jnp.arange(owners.shape[0], dtype=jnp.int32)
    earlier = (indices[None, :] < indices[:, None]) & (owners[None, :] == owners[:, None])
    return jnp.sum(earlier.astype(jnp.int32), axis=1)


def over_chips(value):
    return jnp.stack([value] + [swap_rep(value, BIT_X * k) for k in range(1, CHIPS)])


def small_table(owners, scalars, shard, place, shard_count, slot_count):
    indices = jnp.arange(owners.shape[0], dtype=jnp.int32)
    slot_of = slot_numbers(owners)
    holders = jnp.arange(shard_count, dtype=jnp.int32)
    places = jnp.arange(slot_count, dtype=jnp.int32)
    of_place = (holders[:, None] == owners[None, :]) & (slot_of == place)[None, :]
    of_shard = (places[:, None] == slot_of[None, :]) & (owners == shard)[None, :]
    return jnp.concatenate(
        [
            jnp.stack(scalars),
            jnp.sum(jnp.where(of_place, indices[None, :], 0), axis=1),
            jnp.sum(jnp.where(of_shard, indices[None, :], 0), axis=1),
            jnp.sum(of_shard.astype(jnp.int32), axis=1),
        ]
    )


def step(activations, cotangents, momentum, owners, bucket_starts):
    shard_count = lax.axis_size("shard")
    replica_count = lax.axis_size("rep")
    shard = lax.axis_index("shard")
    replica = lax.axis_index("rep")
    _, tokens, width = activations.shape
    mats, rows, columns = momentum.shape
    half = rows // 2
    token_total = tokens * shard_count * replica_count
    slot_count = -(-mats // shard_count) + 1
    update_scale = math.sqrt(max(rows, width))
    core = replica & 1
    bit_x = (replica >> 1) & 1
    bit_y = (replica >> 2) & 1
    bit_z = shard & 1
    chip = (replica >> 1) & (CHIPS - 1)
    place = chip % slot_count
    swaps = (
        lambda v: swap_rep(v, BIT_X),
        lambda v: swap_rep(v, BIT_Y),
        lambda v: swap_shard(v, 1),
    )
    chosen = (bit_x, bit_y, bit_z)

    def loaded(other):
        layers = [2 * group + (1 - chosen[group] if other else chosen[group]) for group in range(GROUPS)]
        return load_layers(layers, activations, cotangents)

    gots = [swaps[group](value) for group, value in enumerate(loaded(True))]
    mine = loaded(False)
    sib = [swap_rep(value, CORE) for value in mine]
    fwds = [swap_rep(got, CORE) for got in gots]
    top = shard_count // 2
    low = (shard // top) & 1
    table = small_table(
        owners, [core, bit_x, bit_y, bit_z, chip, shard, place, low], shard, place, shard_count, slot_count
    )
    local = local_gradients(table, mine, sib, width, shard_count, half)
    (first, first_sent), (second, second_sent), (third, third_sent) = [
        layer_gradient(group, table, local[group], gots[group], fwds[group], width, shard_count, half)
        for group in range(GROUPS)
    ]

    def over_middle(values):
        bit = 2
        while bit < top:
            at = (shard // bit) & 1
            values = values.reshape(values.shape[0], -1, 2, half, columns)
            values = add(pick(values, at, 2), swap_shard(pick(values, 1 - at, 2), bit))
            bit *= 2
        bit = BIT_Y * 2
        while bit < replica_count:
            values = add(values, swap_rep(values, bit))
            bit *= 2
        return values

    first_got, second_got, third_got = (
        swaps[1](first_sent), swaps[2](second_sent), swap_shard(third_sent, top)
    )
    first = add(first, first_got).reshape(shard_count // 2, 2, half, columns)
    second = add(second, second_got)
    first_got = swaps[2](pick(first, 1 - bit_z, 1))
    second_got = swaps[0](pick(second, 1 - bit_x))
    third = add(third, third_got)
    third_got = swaps[0](pick(third, 1 - bit_x))
    first = add(pick(first, bit_z, 1), first_got)
    second = add(pick(second, bit_x), second_got)
    terms = jnp.stack([first, second]).reshape(2, 2, shard_count // 4, half, columns)
    terms = over_middle(terms.reshape(4, shard_count // 4, half, columns)).reshape(2, 2, half, columns)
    got = swap_shard(pick(terms, 1 - low, 1), top)
    third = add(pick(third, bit_x), third_got).reshape(shard_count // 4, 2, half, columns)
    third = over_middle(jnp.swapaxes(third, 0, 1)).reshape(2, half, columns)
    third_got = swaps[1](pick(third, 1 - bit_y))
    terms, last, sums = finish(
        1.0 / math.sqrt(token_total), table, terms, got, pick(third, bit_y), third_got
    )

    turned = [
        (r * shard_count + s, (r ^ BIT_Y) * shard_count + (s ^ 1))
        for r in range(replica_count)
        for s in range(shard_count)
        if ((r // BIT_Y) & 1) != (s & 1)
    ]
    moved = lax.ppermute(last, ("rep", "shard"), turned)
    last = jnp.where(bit_y == bit_z, last, moved)
    gradient = jnp.concatenate([terms, last[None]])

    for bit in (CORE, BIT_X, BIT_Y):
        sums = sums + swap_rep(sums, bit)
    bit = 1
    while bit < shard_count:
        sums = sums + swap_shard(sums, bit)
        bit *= 2
    factors = clip_factors(sums[0, :mats], bucket_starts, rows * width)

    old = jnp.stack(
        [
            lax.dynamic_slice(momentum, (matrix, core * half, 0), (1, half, columns)).reshape(half, columns)
            for matrix in (2 * bit_x + bit_y, CHIPS + chip, 2 * CHIPS + chip)
        ]
    )
    whole = newton_rows(table, factors, gradient, old, shard_count)
    whole = jnp.stack(
        [whole[0]]
        + [
            swap_shard(whole[k], k, lambda source, target: target < GROUPS)
            for k in range(1, shard_count)
        ]
    )
    whole_sib = swap_rep(whole, CORE)
    mixing = newton(table, whole, whole_sib)
    products = mixing[None]
    bit = 1
    while bit < shard_count:
        products = jnp.concatenate([products, swap_shard(products, bit)])
        bit *= 2
    products = jnp.stack([pick(products, shard ^ unit) for unit in range(GROUPS)])
    all_products = over_chips(products)
    all_products_sib = swap_rep(all_products, CORE)

    all_gradient = over_chips(gradient)
    all_gradient_sib = swap_rep(all_gradient, CORE)
    momentum_out, nesterov = momentum_step(table, factors, all_gradient, all_gradient_sib, momentum)

    carried = carried_rows(table, factors, all_gradient, momentum, shard_count)
    slot_rows = jnp.stack([swap_shard(carried[k - 1], k) for k in range(1, shard_count)])
    slot_rows = jnp.stack(
        [slot_rows] + [swap_rep(slot_rows, BIT_X * k) for k in range(1, slot_count)]
    )
    slot_rows_sib = swap_rep(slot_rows, CORE)

    update, owned = apply_step(
        update_scale, table, all_products, all_products_sib, nesterov, slot_rows, slot_rows_sib,
        shard_count,
    )
    return (momentum_out, update, owned)


def solution(mesh):
    placed = (
        P(None, ("rep", "shard"), None),
        P(None, ("rep", "shard"), None),
        P(None, None, "shard"),
        P(),
        P(),
    )
    return jax.shard_map(
        step,
        mesh=mesh,
        in_specs=placed,
        out_specs=(P(None, None, "shard"), P(None, None, "shard"), P("shard", None, None)),
        check_vma=False,
    )
```

time: 630 us -> 212 us (0.34)
  waiting for transfers between devices: 288 us -> 84.4 us
  blocking collectives: 201 us -> 0 us
  matrix products: 66.7 us -> 0 us
  Pallas kernels: 0 us -> 56 us
  starting transfers between devices: 0.08 us -> 52.1 us
  local copies, waits for them, and re-layouts: 39.3 us -> 4.23 us
  between operations: 14.1 us -> 1.23 us
    reduce_scatter x1 -> x0, waiting for transfers between devices: 215 us -> none  [per_device(): lax.psum_scatter(partial_terms.astype(jnp.bfloat16), 'shard', scatter_dim...]
    all_to_all x2 -> x0, blocking collectives: 189 us -> none  [the longest x1 94.6 us: per_device(): lax.all_to_all(result.reshape(item_count, KV, shard_count, columns), 'sha...]
    ppermute x0 -> x44, waiting for transfers between devices: none -> 84.4 us  [the longest x15 49.5 us: swap_shard(): return lax.ppermute(value, 'shard', pairs)]
    psum x1 -> x0, waiting for transfers between devices: 73.4 us -> none  [per_device(): summed = lax.psum(shard_part, 'rep').astype(jnp.float32)]
    dot_general x13 -> x0, matrix products: 66.7 us -> none  [the longest x5 32.7 us: orthogonal_batch(): jnp.einsum('skj,sjd->skd', mixing, matrix, preferred_element_type=jnp.flo...]
    pallas_call x0 -> x12, Pallas kernels: none -> 56 us  [the longest x3 11.3 us: layer_gradient(): pl.pallas_call(functools.partial(gradient_kernel, group, width, blocks),...]
    ppermute x0 -> x44, starting transfers between devices: none -> 52.1 us  [the longest x15 29.4 us: swap_shard(): return lax.ppermute(value, 'shard', pairs)]
    reshape x2 -> x0, local copies, waits for them, and re-layouts: 13.2 us -> none  [per_device(): result.reshape(item_count, KV, shard_count, columns)]
  transfers between devices with their start and end apart: 2 -> 44, of which waited for: 2 -> 23; matrix products, arithmetic and copies ran while one was open for 0% -> 7% of each run, Pallas kernels for 0% -> 19%
where the time goes in v1:
time: 212 us
  waiting for transfers between devices  84.4 us (40%)
  Pallas kernels  56 us (26%)
  starting transfers between devices  52.1 us (25%)
  other arithmetic  13.9 us (7%)
  local copies, waits for them, and re-layouts  4.23 us (2%)
    ppermute x15, waiting for transfers between devices, swap_shard(): return lax.ppermute(value, 'shard', pairs)  49.5 us
    ppermute x28, waiting for transfers between devices, swap_rep(): return lax.ppermute(value, 'rep', [(i, i ^ bit) for i in range(count)])  34.9 us
    ppermute x15, starting transfers between devices, swap_shard(): return lax.ppermute(value, 'shard', pairs)  29.4 us
    ppermute x28, starting transfers between devices, swap_rep(): return lax.ppermute(value, 'rep', [(i, i ^ bit) for i in range(count)])  22 us
    pallas_call x3, Pallas kernels, layer_gradient(): pl.pallas_call(functools.partial(gradient_kernel, group, width, blocks),...  11.3 us
    pallas_call x1, Pallas kernels, momentum_step(): pl.pallas_call(momentum_kernel, in_specs=[SMEM, SMEM, VMEM, VMEM, ANY], o...  9.1 us
    pallas_call x1, Pallas kernels, apply_step(): pl.pallas_call(functools.partial(apply_kernel, scale, AT_LISTS + shard_co...  7.84 us
    pallas_call x1, Pallas kernels, newton(): pl.pallas_call(newton_kernel, in_specs=[SMEM, VMEM, VMEM], out_specs=VMEM...  7.8 us
  transfers between devices with their start and end apart: 44, of which 23 were waited for; matrix products, arithmetic and copies ran while one was open for 7% of the time, Pallas kernels for 19%

profile of v1, /device:TPU:0, one launch (start us, length us, event | category | flops | bytes accessed | tf_op | source)
XLA Modules:
  0.0 211.8 jit_solution(5738357978727412238)
XLA Ops:
  1.3 3.5 %load_layers.2 = (bf16[128,2560]{1,0:T(8,128)(2,1)}, bf16[128,2560]{1,0:T(8,128)(2,1)}, bf16[128,2560]{1,0:T(8,128)(2,1)}) custom-call(s32[3]{0:T(128)} %get-tuple-element.79.table, bf16[6,128,2048]{2,1,0:T(8,128)(2,1)} %activations.3, bf16[6,128,512]{2,1,0:T(8,128)(2,1)} %cotangents.3), custom_call_target="tpu_custom_call" | custom-call | flops 78643200 | bytes 3932160 | tf_op jit(solution)/shard_map/load_layers/pallas_call | solution.py:101
  5.3 3.6 %load_layers.3 = (bf16[128,2560]{1,0:T(8,128)(2,1)}, bf16[128,2560]{1,0:T(8,128)(2,1)}, bf16[128,2560]{1,0:T(8,128)(2,1)}) custom-call(s32[3]{0:T(128)} %get-tuple-element.80.table, bf16[6,128,2048]{2,1,0:T(8,128)(2,1)} %activations.3, bf16[6,128,512]{2,1,0:T(8,128)(2,1)} %cotangents.3), custom_call_target="tpu_custom_call" | custom-call | flops 78643200 | bytes 3932160 | tf_op jit(solution)/shard_map/load_layers/pallas_call | solution.py:101
  8.9 2.6 %collective-permute-start.3 = (bf16[128,2560]{1,0:T(8,128)(2,1)}, bf16[128,2560]{1,0:T(8,128)(2,1)}, u32[]{:S(2)}, u32[]{:S(2)}) collective-permute-start(bf16[128,2560]{1,0:T(8,128)(2,1)} %get-tuple-element.36), channel_id=1, source_target_pairs={{0,8},{4,12},{8,0},{12,4},{16,24},{20,28},{24,16},{28,20},{1,9},{5... | collective-permute-start | bytes 1966088 | tf_op jit(solution)/shard_map/ppermute | solution.py:37
  11.5 1.5 collective-permute-start.7
  13.5 1.6 collective-permute-start.12
  15.1 12.1 %collective-permute-done.3.got = bf16[128,2560]{1,0:T(8,128)(2,1)} collective-permute-done((bf16[128,2560]{1,0:T(8,128)(2,1)}, bf16[128,2560]{1,0:T(8,128)(2,1)}, u32[]{:S(2)}, u32[]{:S(2)}) %collective-permute-start.3) | collective-permute-done | bytes 655392 | tf_op jit(solution)/shard_map/ppermute | solution.py:37
  28.7 1.8 collective-permute-done.12.got
  31.3 5.3 %local_gradients.1 = (f32[256,2048]{1,0:T(8,128)}, f32[256,2048]{1,0:T(8,128)}, f32[256,2048]{1,0:T(8,128)}) custom-call(s32[20]{0:T(128)} %concatenate.13.table, bf16[128,2560]{1,0:T(8,128)(2,1)} %get-tuple-element.32.mine0, bf16[128,2560]{1,0:T(8,128)(2,1)} %get-tuple-element.33.mine1, bf16[128,2560]{1,0:T(8,128)(2,1)} %get-tuple-element.34.mine2, ...), custom_call_target="tpu_custom_call" | custom-call | flops 805306368 | bytes 9437184 | tf_op jit(solution)/shard_map/local_gradients/pallas_call | solution.py:171
  36.6 3.4 %layer_gradient.3 = (bf16[4,128,512]{2,1,0:T(8,128)(2,1)}, bf16[4,128,512]{2,1,0:T(8,128)(2,1)}) custom-call(s32[20]{0:T(128)} %concatenate.13.table, f32[256,2048]{1,0:T(8,128)} %get-tuple-element.35.local, bf16[128,2560]{1,0:T(8,128)(2,1)} %collective-permute-done.3.got, bf16[128,2560]{1,0:T(8,128)(2,1)} %collective-permute-done.4.fwd), custom_call_target="tpu_custom_call" | custom-call | flops 268435456 | bytes 3145728 | tf_op jit(solution)/shard_map/layer_gradient/pallas_call | solution.py:189
  40.4 4.0 %layer_gradient.4 = (bf16[2,2,128,512]{3,2,1,0:T(8,128)(2,1)}, bf16[2,2,128,512]{3,2,1,0:T(8,128)(2,1)}) custom-call(s32[20]{0:T(128)} %concatenate.13.table, f32[256,2048]{1,0:T(8,128)} %get-tuple-element.39.local, bf16[128,2560]{1,0:T(8,128)(2,1)} %copy-done.3, bf16[128,2560]{1,0:T(8,128)(2,1)} %collective-permute-done.8.fwd), custom_call_target="tpu_custom_call" | custom-call | flops 268435456 | bytes 3145728 | tf_op jit(solution)/shard_map/layer_gradient/pallas_call | solution.py:189
  44.4 1.6 collective-permute-start.9
  46.0 4.0 %layer_gradient.5 = (bf16[2,2,128,512]{3,2,1,0:T(8,128)(2,1)}, bf16[2,2,128,512]{3,2,1,0:T(8,128)(2,1)}) custom-call(s32[20]{0:T(128)} %concatenate.13.table, f32[256,2048]{1,0:T(8,128)} %get-tuple-element.43.local, bf16[128,2560]{1,0:T(8,128)(2,1)} %copy-done.2, bf16[128,2560]{1,0:T(8,128)(2,1)} %collective-permute-done.13.fwd), custom_call_target="tpu_custom_call" | custom-call | flops 268435456 | bytes 3145728 | tf_op jit(solution)/shard_map/layer_gradient/pallas_call | solution.py:189
  50.0 2.6 %collective-permute-start.14 = (bf16[2,2,128,512]{3,2,1,0:T(8,128)(2,1)}, bf16[2,2,128,512]{3,2,1,0:T(8,128)(2,1)S(1)}, u32[]{:S(2)}, u32[]{:S(2)}) collective-permute-start(bf16[2,2,128,512]{3,2,1,0:T(8,128)(2,1)} %get-tuple-element.46), channel_id=1, source_target_pairs={{0,2},{1,3},{2,0},{3,1},{4,6},{5,7},{6,4},{7,5},{8,10},{9,11},{10,... | collective-permute-start | bytes 1572872 | tf_op jit(solution)/shard_map/ppermute | solution.py:43
  52.6 1.9 collective-permute-done.5
  54.7 1.6 collective-permute-start.6
  56.3 10.2 %collective-permute-done.9 = bf16[2,2,128,512]{3,2,1,0:T(8,128)(2,1)S(1)} collective-permute-done((bf16[2,2,128,512]{3,2,1,0:T(8,128)(2,1)}, bf16[2,2,128,512]{3,2,1,0:T(8,128)(2,1)S(1)}, u32[]{:S(2)}, u32[]{:S(2)}) %collective-permute-start.9) | collective-permute-done | bytes 524320 | tf_op jit(solution)/shard_map/ppermute | solution.py:43
  67.2 8.9 %collective-permute-done.14 = bf16[2,2,128,512]{3,2,1,0:T(8,128)(2,1)S(1)} collective-permute-done((bf16[2,2,128,512]{3,2,1,0:T(8,128)(2,1)}, bf16[2,2,128,512]{3,2,1,0:T(8,128)(2,1)S(1)}, u32[]{:S(2)}, u32[]{:S(2)}) %collective-permute-start.14) | collective-permute-done | bytes 524320 | tf_op jit(solution)/shard_map/ppermute | solution.py:43
  78.4 5.4 %collective-permute-done.15 = bf16[2,128,512]{2,1,0:T(8,128)(2,1)S(1)} collective-permute-done((bf16[2,128,512]{2,1,0:T(8,128)(2,1)S(1)}, bf16[2,128,512]{2,1,0:T(8,128)(2,1)S(1)}, u32[]{:S(2)}, u32[]{:S(2)}) %collective-permute-start.15) | collective-permute-done | bytes 262176 | tf_op jit(solution)/shard_map/ppermute | solution.py:37
  84.5 1.5 collective-permute-start.16
  86.9 2.6 %collective-permute-done.16.got_last = bf16[128,512]{1,0:T(8,128)(2,1)S(1)} collective-permute-done((bf16[128,512]{1,0:T(8,128)(2,1)S(1)}, bf16[128,512]{1,0:T(8,128)(2,1)S(1)}, u32[]{:S(2)}, u32[]{:S(2)}) %collective-permute-start.16) | collective-permute-done | bytes 131104 | tf_op jit(solution)/shard_map/ppermute | solution.py:37
  91.5 2.2 %finish.1 = (bf16[2,128,512]{2,1,0:T(8,128)(2,1)}, bf16[128,512]{1,0:T(8,128)(2,1)}, f32[1,128]{1,0:T(1,128)}) custom-call(s32[20]{0:T(128)} %concatenate.13.table, bf16[2,2,128,512]{3,2,1,0:T(8,128)(2,1)} %pad_maximum_fusion.4.keep, bf16[2,128,512]{2,1,0:T(8,128)(2,1)} %copy-done.14, bf16[128,512]{1,0:T(8,128)(2,1)} %get-tuple-element.76.keep_last, ...), custom_call_target="tpu_custom_call" | custom-call | flops 131072000 | bytes 1048576 | tf_op jit(solution)/shard_map/finish/pallas_call | solution.py:226
  97.0 2.2 %collective-permute-done.18 = f32[1,128]{1,0:T(1,128)S(1)} collective-permute-done((f32[1,128]{1,0:T(1,128)S(1)}, f32[1,128]{1,0:T(1,128)S(1)}, u32[]{:S(2)}, u32[]{:S(2)}) %collective-permute-start.18) | collective-permute-done | bytes 544 | tf_op jit(solution)/shard_map/ppermute | solution.py:37
  99.3 1.5 collective-permute-start.19
  103.9 2.6 %collective-permute-done.20 = f32[1,128]{1,0:T(1,128)S(1)} collective-permute-done((f32[1,128]{1,0:T(1,128)S(1)}, f32[1,128]{1,0:T(1,128)S(1)}, u32[]{:S(2)}, u32[]{:S(2)}) %collective-permute-start.20) | collective-permute-done | bytes 544 | tf_op jit(solution)/shard_map/ppermute | solution.py:43
  108.3 2.7 %collective-permute-done.21 = f32[1,128]{1,0:T(1,128)S(1)} collective-permute-done((f32[1,128]{1,0:T(1,128)S(1)}, f32[1,128]{1,0:T(1,128)S(1)}, u32[]{:S(2)}, u32[]{:S(2)}) %collective-permute-start.21) | collective-permute-done | bytes 544 | tf_op jit(solution)/shard_map/ppermute | solution.py:43
  112.5 2.1 %newton_rows.1 = (bf16[128,512]{1,0:T(8,128)(2,1)}, bf16[128,512]{1,0:T(8,128)(2,1)}, bf16[128,512]{1,0:T(8,128)(2,1)}, bf16[128,512]{1,0:T(8,128)(2,1)}) custom-call(s32[20]{0:T(128)} %concatenate.13.table, f32[12]{0:T(128)} %multiply_minimum_fusion.factors, bf16[3,128,512]{2,1,0:T(8,128)(2,1)} %get-tuple-element.71.gradient, ...), custom_call_target="tpu_custom_call" | custom-call | flops 26214400 | bytes 2097152 | tf_op jit(solution)/shard_map/newton_rows/pallas_call | solution.py:293
  114.7 7.6 %collective-permute-start.27 = (bf16[128,512]{1,0:T(8,128)(2,1)}, bf16[128,512]{1,0:T(8,128)(2,1)S(1)}, u32[]{:S(2)}, u32[]{:S(2)}) collective-permute-start(bf16[128,512]{1,0:T(8,128)(2,1)} %get-tuple-element.52), channel_id=1, source_target_pairs={{0,1},{1,0},{3,2},{4,5},{5,4},{7,6},{8,9},{9,8},{11,10},{12,13},{1... | collective-permute-start | bytes 393224 | tf_op jit(solution)/shard_map/ppermute | solution.py:43
  122.3 2.1 collective-permute-start.24
  125.8 1.9 collective-permute-start.28
  127.7 1.5 collective-permute-start.29
  129.2 5.4 %collective-permute-done.28 = bf16[128,512]{1,0:T(8,128)(2,1)S(1)} collective-permute-done((bf16[128,512]{1,0:T(8,128)(2,1)}, bf16[128,512]{1,0:T(8,128)(2,1)S(1)}, u32[]{:S(2)}, u32[]{:S(2)}) %collective-permute-start.28) | collective-permute-done | bytes 131104 | tf_op jit(solution)/shard_map/ppermute | solution.py:43
  134.6 2.1 collective-permute-done.29
  139.2 3.3 %carried_rows.1 = (bf16[128,512]{1,0:T(8,128)(2,1)}, bf16[128,512]{1,0:T(8,128)(2,1)}, bf16[128,512]{1,0:T(8,128)(2,1)}) custom-call(s32[20]{0:T(128)} %concatenate.13.table, f32[12]{0:T(128)} %multiply_minimum_fusion.factors, bf16[4,3,128,512]{3,2,1,0:T(8,128)(2,1)} %pad_maximum_fusion.own, f32[12,256,512]{2,1,0:T(8,128)} %rest_0_.1), custom_call_target="tpu_custom_call" | custom-call | flops 19660800 | bytes 1572864 | tf_op jit(solution)/shard_map/carried_rows/pallas_call | solution.py:328
  144.6 2.3 %collective-permute-start.39 = (bf16[128,512]{1,0:T(8,128)(2,1)}, bf16[128,512]{1,0:T(8,128)(2,1)S(1)}, u32[]{:S(2)}, u32[]{:S(2)}) collective-permute-start(bf16[128,512]{1,0:T(8,128)(2,1)} %get-tuple-element.58), channel_id=1, source_target_pairs={{0,3},{1,2},{2,1},{3,0},{4,7},{5,6},{6,5},{7,4},{8,11},{9,10},{10,... | collective-permute-start | bytes 393224 | tf_op jit(solution)/shard_map/ppermute | solution.py:43
  146.9 3.2 %collective-permute-done.37 = bf16[128,512]{1,0:T(8,128)(2,1)S(1)} collective-permute-done((bf16[128,512]{1,0:T(8,128)(2,1)}, bf16[128,512]{1,0:T(8,128)(2,1)S(1)}, u32[]{:S(2)}, u32[]{:S(2)}) %collective-permute-start.37) | collective-permute-done | bytes 131104 | tf_op jit(solution)/shard_map/ppermute | solution.py:43
  150.1 6.8 %collective-permute-done.38 = bf16[128,512]{1,0:T(8,128)(2,1)S(1)} collective-permute-done((bf16[128,512]{1,0:T(8,128)(2,1)}, bf16[128,512]{1,0:T(8,128)(2,1)S(1)}, u32[]{:S(2)}, u32[]{:S(2)}) %collective-permute-start.38) | collective-permute-done | bytes 131104 | tf_op jit(solution)/shard_map/ppermute | solution.py:43
  159.0 2.2 %collective-permute-start.42 = (bf16[3,128,512]{2,1,0:T(8,128)(2,1)}, bf16[3,128,512]{2,1,0:T(8,128)(2,1)}, u32[]{:S(2)}, u32[]{:S(2)}) collective-permute-start(bf16[3,128,512]{2,1,0:T(8,128)(2,1)} %get-tuple-element.69), channel_id=1, source_target_pairs={{0,24},{4,28},{8,16},{12,20},{16,8},{20,12},{24,0},{28,4},{1,25},{... | collective-permute-start | bytes 1179656 | tf_op jit(solution)/shard_map/ppermute | solution.py:37
  161.2 7.8 %newton.1 = bf16[128,256]{1,0:T(8,128)(2,1)} custom-call(s32[20]{0:T(128)} %concatenate.13.table, bf16[4,128,512]{2,1,0:T(8,128)(2,1)} %copy-done.10, bf16[4,128,512]{2,1,0:T(8,128)(2,1)} %collective-permute-done.30.sib), custom_call_target="tpu_custom_call" | custom-call | flops 3187671040 | bytes 4194304 | tf_op jit(solution)/shard_map/newton/pallas_call | solution.py:380
  169.0 2.6 %collective-permute-start.31 = (bf16[1,128,256]{2,1,0:T(8,128)(2,1)}, bf16[1,128,256]{2,1,0:T(8,128)(2,1)S(1)}, u32[]{:S(2)}, u32[]{:S(2)}) collective-permute-start(bf16[1,128,256]{2,1,0:T(8,128)(2,1)} %bitcast.75), channel_id=1, source_target_pairs={{0,1},{1,0},{2,3},{3,2},{4,5},{5,4},{6,7},{7,6},{8,9},{9,8},{10,11... | collective-permute-start | bytes 196616 | tf_op jit(solution)/shard_map/ppermute | solution.py:43
  171.6 2.4 %collective-permute-done.31 = bf16[1,128,256]{2,1,0:T(8,128)(2,1)S(1)} collective-permute-done((bf16[1,128,256]{2,1,0:T(8,128)(2,1)}, bf16[1,128,256]{2,1,0:T(8,128)(2,1)S(1)}, u32[]{:S(2)}, u32[]{:S(2)}) %collective-permute-start.31) | collective-permute-done | bytes 65568 | tf_op jit(solution)/shard_map/ppermute | solution.py:43
  174.1 1.5 pad_maximum_fusion.10
  175.6 1.8 collective-permute-start.32
  179.8 2.0 collective-permute-done.32
  184.1 2.3 %collective-permute-start.35 = (bf16[3,128,256]{2,1,0:T(8,128)(2,1)S(1)}, bf16[3,128,256]{2,1,0:T(8,128)(2,1)S(1)}, u32[]{:S(2)}, u32[]{:S(2)}) collective-permute-start(bf16[3,128,256]{2,1,0:T(8,128)(2,1)S(1)} %get-tuple-element.78), channel_id=1, source_target_pairs={{0,24},{4,28},{8,16},{12,20},{16,8},{20,12},{24,0},{28,4},{1,25},{... | collective-permute-start | bytes 589832 | tf_op jit(solution)/shard_map/ppermute | solution.py:37
  186.4 4.1 %collective-permute-done.34 = bf16[3,128,256]{2,1,0:T(8,128)(2,1)S(1)} collective-permute-done((bf16[3,128,256]{2,1,0:T(8,128)(2,1)S(1)}, bf16[3,128,256]{2,1,0:T(8,128)(2,1)S(1)}, u32[]{:S(2)}, u32[]{:S(2)}) %collective-permute-start.34) | collective-permute-done | bytes 196640 | tf_op jit(solution)/shard_map/ppermute | solution.py:37
  191.0 2.7 %collective-permute-done.35 = bf16[3,128,256]{2,1,0:T(8,128)(2,1)S(1)} collective-permute-done((bf16[3,128,256]{2,1,0:T(8,128)(2,1)S(1)}, bf16[3,128,256]{2,1,0:T(8,128)(2,1)S(1)}, u32[]{:S(2)}, u32[]{:S(2)}) %collective-permute-start.35) | collective-permute-done | bytes 196640 | tf_op jit(solution)/shard_map/ppermute | solution.py:37
  194.7 9.1 %momentum_step.1 = (f32[12,256,512]{2,1,0:T(8,128)}, bf16[12,256,512]{2,1,0:T(8,128)(2,1)}) custom-call(s32[20]{0:T(128)} %concatenate.13.table, f32[12]{0:T(128)} %multiply_minimum_fusion.factors, bf16[4,3,128,512]{3,2,1,0:T(8,128)(2,1)} %pad_maximum_fusion.own, bf16[4,3,128,512]{3,2,1,0:T(8,128)(2,1)} %collective-permute-done.26.sib, f32[12,256,512]{2,1,0:T(8,128)} %rest_0_.1), custom_call_target="tpu_custom_call" | custom-call | flops 629145600 | bytes 18874368 | tf_op jit(solution)/shard_map/momentum_step/pallas_call | solution.py:265
  203.8 7.8 %apply_step.1 = (f32[12,256,512]{2,1,0:T(8,128)}, bf16[4,256,2048]{2,1,0:T(8,128)(2,1)}) custom-call(s32[20]{0:T(128)} %concatenate.13.table, bf16[4,3,128,256]{3,2,1,0:T(8,128)(2,1)} %pad_maximum_fusion.3.own, bf16[4,3,128,256]{3,2,1,0:T(8,128)(2,1)} %collective-permute-done.36.sib, bf16[12,256,512]{2,1,0:T(8,128)(2,1)} %get-tuple-element.55.values, ...), custom_call_target="tpu_custom_call" | custom-call | flops 1879048192 | bytes 13631488 | tf_op jit(solution)/shard_map/apply_step/pallas_call | solution.py:440
  (133 shorter events, 35.2 us)
Async XLA Ops:
  4.7 8.8 %collective-permute-start = (bf16[128,2560]{1,0:T(8,128)(2,1)}, bf16[128,2560]{1,0:T(8,128)(2,1)S(1)}, u32[]{:S(2)}, u32[]{:S(2)}) collective-permute-start(bf16[128,2560]{1,0:T(8,128)(2,1)} %get-tuple-element.32.mine0), channel_id=1, source_target_pairs={{0,4},{4,0},{8,12},{12,8},{16,20},{20,16},{24,28},{28,24},{1,5},{5... | collective-permute-start | bytes 1966088 | tf_op jit(solution)/shard_map/ppermute | solution.py:37
  5.3 21.9 %copy-start.18 = (s32[12]{0:T(128)S(1)}, s32[12]{0:T(128)}, u32[]{:S(2)}) copy-start(s32[12]{0:T(128)} %param.8) | copy-start | bytes 148
  8.9 18.3 %collective-permute-start.3 = (bf16[128,2560]{1,0:T(8,128)(2,1)}, bf16[128,2560]{1,0:T(8,128)(2,1)}, u32[]{:S(2)}, u32[]{:S(2)}) collective-permute-start(bf16[128,2560]{1,0:T(8,128)(2,1)} %get-tuple-element.36), channel_id=1, source_target_pairs={{0,8},{4,12},{8,0},{12,4},{16,24},{20,28},{24,16},{28,20},{1,9},{5... | collective-permute-start | bytes 1966088 | tf_op jit(solution)/shard_map/ppermute | solution.py:37
  11.5 17.0 %collective-permute-start.7 = (bf16[128,2560]{1,0:T(8,128)(2,1)}, bf16[128,2560]{1,0:T(8,128)(2,1)S(1)}, u32[]{:S(2)}, u32[]{:S(2)}) collective-permute-start(bf16[128,2560]{1,0:T(8,128)(2,1)} %get-tuple-element.40), channel_id=1, source_target_pairs={{0,16},{4,20},{8,24},{12,28},{16,0},{20,4},{24,8},{28,12},{1,17},{... | collective-permute-start | bytes 1966088 | tf_op jit(solution)/shard_map/ppermute | solution.py:37
  13.0 18.3 %collective-permute-start.1 = (bf16[128,2560]{1,0:T(8,128)(2,1)S(1)}, bf16[128,2560]{1,0:T(8,128)(2,1)}, u32[]{:S(2)}, u32[]{:S(2)}) collective-permute-start(bf16[128,2560]{1,0:T(8,128)(2,1)S(1)} %copy-done.4), channel_id=1, source_target_pairs={{0,4},{4,0},{8,12},{12,8},{16,20},{20,16},{24,28},{28,24},{1,5},{5... | collective-permute-start | bytes 1966088 | tf_op jit(solution)/shard_map/ppermute | solution.py:37
  13.0 18.3 %collective-permute-start.2 = (bf16[128,2560]{1,0:T(8,128)(2,1)S(1)}, bf16[128,2560]{1,0:T(8,128)(2,1)}, u32[]{:S(2)}, u32[]{:S(2)}) collective-permute-start(bf16[128,2560]{1,0:T(8,128)(2,1)S(1)} %copy-done.5), channel_id=1, source_target_pairs={{0,4},{4,0},{8,12},{12,8},{16,20},{20,16},{24,28},{28,24},{1,5},{5... | collective-permute-start | bytes 1966088 | tf_op jit(solution)/shard_map/ppermute | solution.py:37
  13.5 17.7 %copy-start.6 = (bf16[128,2560]{1,0:T(8,128)(2,1)}, bf16[128,2560]{1,0:T(8,128)(2,1)S(1)}, u32[]{:S(2)}) copy-start(bf16[128,2560]{1,0:T(8,128)(2,1)S(1)} %collective-permute-done.sib0) | copy-start | bytes 1966084
  13.5 16.9 %collective-permute-start.12 = (bf16[128,2560]{1,0:T(8,128)(2,1)}, bf16[128,2560]{1,0:T(8,128)(2,1)S(1)}, u32[]{:S(2)}, u32[]{:S(2)}) collective-permute-start(bf16[128,2560]{1,0:T(8,128)(2,1)} %get-tuple-element.44), channel_id=1, source_target_pairs={{0,1},{1,0},{2,3},{3,2},{4,5},{5,4},{6,7},{7,6},{8,9},{9,8},{10,11... | collective-permute-start | bytes 1966088 | tf_op jit(solution)/shard_map/ppermute | solution.py:43
  27.2 9.4 %collective-permute-start.4 = (bf16[128,2560]{1,0:T(8,128)(2,1)}, bf16[128,2560]{1,0:T(8,128)(2,1)}, u32[]{:S(2)}, u32[]{:S(2)}) collective-permute-start(bf16[128,2560]{1,0:T(8,128)(2,1)} %collective-permute-done.3.got), channel_id=1, source_target_pairs={{0,4},{4,0},{8,12},{12,8},{16,20},{20,16},{24,28},{28,24},{1,5},{5... | collective-permute-start | bytes 1966088 | tf_op jit(solution)/shard_map/ppermute | solution.py:37
  28.5 11.9 %collective-permute-start.8 = (bf16[128,2560]{1,0:T(8,128)(2,1)S(1)}, bf16[128,2560]{1,0:T(8,128)(2,1)}, u32[]{:S(2)}, u32[]{:S(2)}) collective-permute-start(bf16[128,2560]{1,0:T(8,128)(2,1)S(1)} %collective-permute-done.7.got), channel_id=1, source_target_pairs={{0,4},{4,0},{8,12},{12,8},{16,20},{20,16},{24,28},{28,24},{1,5},{5... | collective-permute-start | bytes 1966088 | tf_op jit(solution)/shard_map/ppermute | solution.py:37
  30.5 15.5 %collective-permute-start.13 = (bf16[128,2560]{1,0:T(8,128)(2,1)S(1)}, bf16[128,2560]{1,0:T(8,128)(2,1)}, u32[]{:S(2)}, u32[]{:S(2)}) collective-permute-start(bf16[128,2560]{1,0:T(8,128)(2,1)S(1)} %collective-permute-done.12.got), channel_id=1, source_target_pairs={{0,4},{4,0},{8,12},{12,8},{16,20},{20,16},{24,28},{28,24},{1,5},{5... | collective-permute-start | bytes 1966088 | tf_op jit(solution)/shard_map/ppermute | solution.py:37
  39.9 14.5 %collective-permute-start.5 = (bf16[4,128,512]{2,1,0:T(8,128)(2,1)}, bf16[4,128,512]{2,1,0:T(8,128)(2,1)S(1)}, u32[]{:S(2)}, u32[]{:S(2)}) collective-permute-start(bf16[4,128,512]{2,1,0:T(8,128)(2,1)} %get-tuple-element.38), channel_id=1, source_target_pairs={{0,16},{4,20},{8,24},{12,28},{16,0},{20,4},{24,8},{28,12},{1,17},{... | collective-permute-start | bytes 1572872 | tf_op jit(solution)/shard_map/ppermute | solution.py:37
  44.4 22.1 %collective-permute-start.9 = (bf16[2,2,128,512]{3,2,1,0:T(8,128)(2,1)}, bf16[2,2,128,512]{3,2,1,0:T(8,128)(2,1)S(1)}, u32[]{:S(2)}, u32[]{:S(2)}) collective-permute-start(bf16[2,2,128,512]{3,2,1,0:T(8,128)(2,1)} %get-tuple-element.42), channel_id=1, source_target_pairs={{0,1},{1,0},{2,3},{3,2},{4,5},{5,4},{6,7},{7,6},{8,9},{9,8},{10,11... | collective-permute-start | bytes 1572872 | tf_op jit(solution)/shard_map/ppermute | solution.py:43
  50.0 26.2 %collective-permute-start.14 = (bf16[2,2,128,512]{3,2,1,0:T(8,128)(2,1)}, bf16[2,2,128,512]{3,2,1,0:T(8,128)(2,1)S(1)}, u32[]{:S(2)}, u32[]{:S(2)}) collective-permute-start(bf16[2,2,128,512]{3,2,1,0:T(8,128)(2,1)} %get-tuple-element.46), channel_id=1, source_target_pairs={{0,2},{1,3},{2,0},{3,1},{4,6},{5,7},{6,4},{7,5},{8,10},{9,11},{10,... | collective-permute-start | bytes 1572872 | tf_op jit(solution)/shard_map/ppermute | solution.py:43
  54.6 21.5 %copy-start.9 = (bf16[2,2,128,512]{3,2,1,0:T(8,128)(2,1)S(1)}, bf16[2,2,128,512]{3,2,1,0:T(8,128)(2,1)}, u32[]{:S(2)}) copy-start(bf16[2,2,128,512]{3,2,1,0:T(8,128)(2,1)} %get-tuple-element.45) | copy-start | bytes 1572868
  54.7 22.3 %collective-permute-start.6 = (bf16[2,128,512]{2,1,0:T(8,128)(2,1)S(1)}, bf16[2,128,512]{2,1,0:T(8,128)(2,1)S(1)}, u32[]{:S(2)}, u32[]{:S(2)}) collective-permute-start(bf16[2,128,512]{2,1,0:T(8,128)(2,1)S(1)} %dynamic-slice_bitcast_fusion.2), channel_id=1, source_target_pairs={{0,1},{1,0},{2,3},{3,2},{4,5},{5,4},{6,7},{7,6},{8,9},{9,8},{10,11... | collective-permute-start | bytes 786440 | tf_op jit(solution)/shard_map/ppermute | solution.py:43
  66.6 10.4 %collective-permute-start.10 = (bf16[2,128,512]{2,1,0:T(8,128)(2,1)S(1)}, bf16[2,128,512]{2,1,0:T(8,128)(2,1)S(1)}, u32[]{:S(2)}, u32[]{:S(2)}) collective-permute-start(bf16[2,128,512]{2,1,0:T(8,128)(2,1)S(1)} %dynamic-slice_bitcast_fusion.1), channel_id=1, source_target_pairs={{0,8},{4,12},{8,0},{12,4},{16,24},{20,28},{24,16},{28,20},{1,9},{5... | collective-permute-start | bytes 786440 | tf_op jit(solution)/shard_map/ppermute | solution.py:37
  76.3 7.4 %collective-permute-start.15 = (bf16[2,128,512]{2,1,0:T(8,128)(2,1)S(1)}, bf16[2,128,512]{2,1,0:T(8,128)(2,1)S(1)}, u32[]{:S(2)}, u32[]{:S(2)}) collective-permute-start(bf16[2,128,512]{2,1,0:T(8,128)(2,1)S(1)} %dynamic-slice_bitcast_fusion), channel_id=1, source_target_pairs={{0,8},{4,12},{8,0},{12,4},{16,24},{20,28},{24,16},{28,20},{1,9},{5... | collective-permute-start | bytes 786440 | tf_op jit(solution)/shard_map/ppermute | solution.py:37
  77.2 13.7 %collective-permute-start.11 = (bf16[2,128,512]{2,1,0:T(8,128)(2,1)S(1)}, bf16[2,128,512]{2,1,0:T(8,128)(2,1)S(1)}, u32[]{:S(2)}, u32[]{:S(2)}) collective-permute-start(bf16[2,128,512]{2,1,0:T(8,128)(2,1)S(1)} %fusion.6), channel_id=1, source_target_pairs={{0,2},{1,3},{2,0},{3,1},{4,6},{5,7},{6,4},{7,5},{8,10},{9,11},{10,... | collective-permute-start | bytes 786440 | tf_op jit(solution)/shard_map/ppermute | solution.py:43
  84.5 5.0 %collective-permute-start.16 = (bf16[128,512]{1,0:T(8,128)(2,1)S(1)}, bf16[128,512]{1,0:T(8,128)(2,1)S(1)}, u32[]{:S(2)}, u32[]{:S(2)}) collective-permute-start(bf16[128,512]{1,0:T(8,128)(2,1)S(1)} %get-tuple-element.75), channel_id=1, source_target_pairs={{0,16},{4,20},{8,24},{12,28},{16,0},{20,4},{24,8},{28,12},{1,17},{... | collective-permute-start | bytes 393224 | tf_op jit(solution)/shard_map/ppermute | solution.py:37
  93.7 1.4 collective-permute-start.17
  95.7 3.6 %collective-permute-start.18 = (f32[1,128]{1,0:T(1,128)S(1)}, f32[1,128]{1,0:T(1,128)S(1)}, u32[]{:S(2)}, u32[]{:S(2)}) collective-permute-start(f32[1,128]{1,0:T(1,128)S(1)} %add.130), channel_id=1, source_target_pairs={{0,8},{4,12},{8,0},{12,4},{16,24},{20,28},{24,16},{28,20},{1,9},{5... | collective-permute-start | bytes 1544 | tf_op jit(solution)/shard_map/ppermute | solution.py:37
  99.3 3.6 %collective-permute-start.19 = (f32[1,128]{1,0:T(1,128)S(1)}, f32[1,128]{1,0:T(1,128)S(1)}, u32[]{:S(2)}, u32[]{:S(2)}) collective-permute-start(f32[1,128]{1,0:T(1,128)S(1)} %add.131), channel_id=1, source_target_pairs={{0,16},{4,20},{8,24},{12,28},{16,0},{20,4},{24,8},{28,12},{1,17},{... | collective-permute-start | bytes 1544 | tf_op jit(solution)/shard_map/ppermute | solution.py:37
  102.9 3.6 %collective-permute-start.20 = (f32[1,128]{1,0:T(1,128)S(1)}, f32[1,128]{1,0:T(1,128)S(1)}, u32[]{:S(2)}, u32[]{:S(2)}) collective-permute-start(f32[1,128]{1,0:T(1,128)S(1)} %add.132), channel_id=1, source_target_pairs={{0,1},{1,0},{2,3},{3,2},{4,5},{5,4},{6,7},{7,6},{8,9},{9,8},{10,11... | collective-permute-start | bytes 1544 | tf_op jit(solution)/shard_map/ppermute | solution.py:43
  106.5 4.5 %collective-permute-start.21 = (f32[1,128]{1,0:T(1,128)S(1)}, f32[1,128]{1,0:T(1,128)S(1)}, u32[]{:S(2)}, u32[]{:S(2)}) collective-permute-start(f32[1,128]{1,0:T(1,128)S(1)} %add.133), channel_id=1, source_target_pairs={{0,2},{1,3},{2,0},{3,1},{4,6},{5,7},{6,4},{7,5},{8,10},{9,11},{10,... | collective-permute-start | bytes 1544 | tf_op jit(solution)/shard_map/ppermute | solution.py:43
  107.6 4.1 %collective-permute-start.22 = (bf16[128,512]{1,0:T(8,128)(2,1)S(1)}, bf16[128,512]{1,0:T(8,128)(2,1)S(1)}, u32[]{:S(2)}, u32[]{:S(2)}) collective-permute-start(bf16[128,512]{1,0:T(8,128)(2,1)S(1)} %copy-done.16), channel_id=1, source_target_pairs={{1,16},{3,18},{5,20},{7,22},{9,24},{11,26},{13,28},{15,30},{16,1},... | collective-permute-start | bytes 393224 | tf_op jit(solution)/shard_map/ppermute | solution.py:584
  114.7 13.1 %collective-permute-start.27 = (bf16[128,512]{1,0:T(8,128)(2,1)}, bf16[128,512]{1,0:T(8,128)(2,1)S(1)}, u32[]{:S(2)}, u32[]{:S(2)}) collective-permute-start(bf16[128,512]{1,0:T(8,128)(2,1)} %get-tuple-element.52), channel_id=1, source_target_pairs={{0,1},{1,0},{3,2},{4,5},{5,4},{7,6},{8,9},{9,8},{11,10},{12,13},{1... | collective-permute-start | bytes 393224 | tf_op jit(solution)/shard_map/ppermute | solution.py:43
  122.3 15.5 %collective-permute-start.25 = (bf16[3,128,512]{2,1,0:T(8,128)(2,1)}, bf16[3,128,512]{2,1,0:T(8,128)(2,1)S(1)}, u32[]{:S(2)}, u32[]{:S(2)}) collective-permute-start(bf16[3,128,512]{2,1,0:T(8,128)(2,1)} %get-tuple-element.71.gradient), channel_id=1, source_target_pairs={{0,24},{4,28},{8,16},{12,20},{16,8},{20,12},{24,0},{28,4},{1,25},{... | collective-permute-start | bytes 1179656 | tf_op jit(solution)/shard_map/ppermute | solution.py:37
  122.3 15.5 %collective-permute-start.24 = (bf16[3,128,512]{2,1,0:T(8,128)(2,1)}, bf16[3,128,512]{2,1,0:T(8,128)(2,1)S(1)}, u32[]{:S(2)}, u32[]{:S(2)}) collective-permute-start(bf16[3,128,512]{2,1,0:T(8,128)(2,1)} %get-tuple-element.71.gradient), channel_id=1, source_target_pairs={{0,16},{4,20},{8,24},{12,28},{16,0},{20,4},{24,8},{28,12},{1,17},{... | collective-permute-start | bytes 1179656 | tf_op jit(solution)/shard_map/ppermute | solution.py:37
  124.4 13.4 %collective-permute-start.23 = (bf16[3,128,512]{2,1,0:T(8,128)(2,1)}, bf16[3,128,512]{2,1,0:T(8,128)(2,1)S(1)}, u32[]{:S(2)}, u32[]{:S(2)}) collective-permute-start(bf16[3,128,512]{2,1,0:T(8,128)(2,1)} %get-tuple-element.71.gradient), channel_id=1, source_target_pairs={{0,8},{4,12},{8,0},{12,4},{16,24},{20,28},{24,16},{28,20},{1,9},{5... | collective-permute-start | bytes 1179656 | tf_op jit(solution)/shard_map/ppermute | solution.py:37
  125.8 8.8 %collective-permute-start.28 = (bf16[128,512]{1,0:T(8,128)(2,1)}, bf16[128,512]{1,0:T(8,128)(2,1)S(1)}, u32[]{:S(2)}, u32[]{:S(2)}) collective-permute-start(bf16[128,512]{1,0:T(8,128)(2,1)} %get-tuple-element.53), channel_id=1, source_target_pairs={{0,2},{2,0},{3,1},{4,6},{6,4},{7,5},{8,10},{10,8},{11,9},{12,14},{... | collective-permute-start | bytes 393224 | tf_op jit(solution)/shard_map/ppermute | solution.py:43
  127.7 9.0 %collective-permute-start.29 = (bf16[128,512]{1,0:T(8,128)(2,1)}, bf16[128,512]{1,0:T(8,128)(2,1)S(1)}, u32[]{:S(2)}, u32[]{:S(2)}) collective-permute-start(bf16[128,512]{1,0:T(8,128)(2,1)} %get-tuple-element.54), channel_id=1, source_target_pairs={{1,2},{2,1},{3,0},{5,6},{6,5},{7,4},{9,10},{10,9},{11,8},{13,14},{... | collective-permute-start | bytes 393224 | tf_op jit(solution)/shard_map/ppermute | solution.py:43
  137.7 23.5 %collective-permute-start.30 = (bf16[4,128,512]{2,1,0:T(8,128)(2,1)S(1)}, bf16[4,128,512]{2,1,0:T(8,128)(2,1)}, u32[]{:S(2)}, u32[]{:S(2)}) collective-permute-start(bf16[4,128,512]{2,1,0:T(8,128)(2,1)S(1)} %pad_maximum_fusion.5.own), channel_id=1, source_target_pairs={{0,4},{4,0},{8,12},{12,8},{16,20},{20,16},{24,28},{28,24},{1,5},{5... | collective-permute-start | bytes 1572872 | tf_op jit(solution)/shard_map/ppermute | solution.py:37
  142.5 7.6 %collective-permute-start.37 = (bf16[128,512]{1,0:T(8,128)(2,1)}, bf16[128,512]{1,0:T(8,128)(2,1)S(1)}, u32[]{:S(2)}, u32[]{:S(2)}) collective-permute-start(bf16[128,512]{1,0:T(8,128)(2,1)} %get-tuple-element.56), channel_id=1, source_target_pairs={{0,1},{1,0},{2,3},{3,2},{4,5},{5,4},{6,7},{7,6},{8,9},{9,8},{10,11... | collective-permute-start | bytes 393224 | tf_op jit(solution)/shard_map/ppermute | solution.py:43
  143.8 13.1 %collective-permute-start.38 = (bf16[128,512]{1,0:T(8,128)(2,1)}, bf16[128,512]{1,0:T(8,128)(2,1)S(1)}, u32[]{:S(2)}, u32[]{:S(2)}) collective-permute-start(bf16[128,512]{1,0:T(8,128)(2,1)} %get-tuple-element.57), channel_id=1, source_target_pairs={{0,2},{1,3},{2,0},{3,1},{4,6},{5,7},{6,4},{7,5},{8,10},{9,11},{10,... | collective-permute-start | bytes 393224 | tf_op jit(solution)/shard_map/ppermute | solution.py:43
  144.6 12.3 %collective-permute-start.39 = (bf16[128,512]{1,0:T(8,128)(2,1)}, bf16[128,512]{1,0:T(8,128)(2,1)S(1)}, u32[]{:S(2)}, u32[]{:S(2)}) collective-permute-start(bf16[128,512]{1,0:T(8,128)(2,1)} %get-tuple-element.58), channel_id=1, source_target_pairs={{0,3},{1,2},{2,1},{3,0},{4,7},{5,6},{6,5},{7,4},{8,11},{9,10},{10,... | collective-permute-start | bytes 393224 | tf_op jit(solution)/shard_map/ppermute | solution.py:43
  157.7 19.7 %collective-permute-start.41 = (bf16[3,128,512]{2,1,0:T(8,128)(2,1)}, bf16[3,128,512]{2,1,0:T(8,128)(2,1)S(1)}, u32[]{:S(2)}, u32[]{:S(2)}) collective-permute-start(bf16[3,128,512]{2,1,0:T(8,128)(2,1)} %get-tuple-element.69), channel_id=1, source_target_pairs={{0,16},{4,20},{8,24},{12,28},{16,0},{20,4},{24,8},{28,12},{1,17},{... | collective-permute-start | bytes 1179656 | tf_op jit(solution)/shard_map/ppermute | solution.py:37
  158.1 19.3 %collective-permute-start.40 = (bf16[3,128,512]{2,1,0:T(8,128)(2,1)}, bf16[3,128,512]{2,1,0:T(8,128)(2,1)S(1)}, u32[]{:S(2)}, u32[]{:S(2)}) collective-permute-start(bf16[3,128,512]{2,1,0:T(8,128)(2,1)} %get-tuple-element.69), channel_id=1, source_target_pairs={{0,8},{4,12},{8,0},{12,4},{16,24},{20,28},{24,16},{28,20},{1,9},{5... | collective-permute-start | bytes 1179656 | tf_op jit(solution)/shard_map/ppermute | solution.py:37
  159.0 18.4 %collective-permute-start.42 = (bf16[3,128,512]{2,1,0:T(8,128)(2,1)}, bf16[3,128,512]{2,1,0:T(8,128)(2,1)}, u32[]{:S(2)}, u32[]{:S(2)}) collective-permute-start(bf16[3,128,512]{2,1,0:T(8,128)(2,1)} %get-tuple-element.69), channel_id=1, source_target_pairs={{0,24},{4,28},{8,16},{12,20},{16,8},{20,12},{24,0},{28,4},{1,25},{... | collective-permute-start | bytes 1179656 | tf_op jit(solution)/shard_map/ppermute | solution.py:37
  169.0 5.0 %collective-permute-start.31 = (bf16[1,128,256]{2,1,0:T(8,128)(2,1)}, bf16[1,128,256]{2,1,0:T(8,128)(2,1)S(1)}, u32[]{:S(2)}, u32[]{:S(2)}) collective-permute-start(bf16[1,128,256]{2,1,0:T(8,128)(2,1)} %bitcast.75), channel_id=1, source_target_pairs={{0,1},{1,0},{2,3},{3,2},{4,5},{5,4},{6,7},{7,6},{8,9},{9,8},{10,11... | collective-permute-start | bytes 196616 | tf_op jit(solution)/shard_map/ppermute | solution.py:43
  171.6 23.1 %collective-permute-start.26 = (bf16[4,3,128,512]{3,2,1,0:T(8,128)(2,1)S(1)}, bf16[4,3,128,512]{3,2,1,0:T(8,128)(2,1)}, u32[]{:S(2)}, u32[]{:S(2)}) collective-permute-start(bf16[4,3,128,512]{3,2,1,0:T(8,128)(2,1)S(1)} %copy-done), channel_id=1, source_target_pairs={{0,4},{4,0},{8,12},{12,8},{16,20},{20,16},{24,28},{28,24},{1,5},{5... | collective-permute-start | bytes 4718600 | tf_op jit(solution)/shard_map/ppermute | solution.py:37
  175.6 6.2 %collective-permute-start.32 = (bf16[2,128,256]{2,1,0:T(8,128)(2,1)}, bf16[2,128,256]{2,1,0:T(8,128)(2,1)}, u32[]{:S(2)}, u32[]{:S(2)}) collective-permute-start(bf16[2,128,256]{2,1,0:T(8,128)(2,1)} %pad_maximum_fusion.10), channel_id=1, source_target_pairs={{0,2},{1,3},{2,0},{3,1},{4,6},{5,7},{6,4},{7,5},{8,10},{9,11},{10,... | collective-permute-start | bytes 393224 | tf_op jit(solution)/shard_map/ppermute | solution.py:43
  179.7 24.1 %copy-start.1 = (bf16[4,3,128,512]{3,2,1,0:T(8,128)(2,1)}, bf16[4,3,128,512]{3,2,1,0:T(8,128)(2,1)S(1)}, u32[]{:S(2)}) copy-start(bf16[4,3,128,512]{3,2,1,0:T(8,128)(2,1)S(1)} %pad_maximum_fusion.1.own_rows) | copy-start | bytes 4718596
  179.7 24.1 %collective-permute-start.43 = (bf16[4,3,128,512]{3,2,1,0:T(8,128)(2,1)S(1)}, bf16[4,3,128,512]{3,2,1,0:T(8,128)(2,1)}, u32[]{:S(2)}, u32[]{:S(2)}) collective-permute-start(bf16[4,3,128,512]{3,2,1,0:T(8,128)(2,1)S(1)} %pad_maximum_fusion.1.own_rows), channel_id=1, source_target_pairs={{0,4},{4,0},{8,12},{12,8},{16,20},{20,16},{24,28},{28,24},{1,5},{5... | collective-permute-start | bytes 4718600 | tf_op jit(solution)/shard_map/ppermute | solution.py:37
  182.9 7.6 %collective-permute-start.34 = (bf16[3,128,256]{2,1,0:T(8,128)(2,1)S(1)}, bf16[3,128,256]{2,1,0:T(8,128)(2,1)S(1)}, u32[]{:S(2)}, u32[]{:S(2)}) collective-permute-start(bf16[3,128,256]{2,1,0:T(8,128)(2,1)S(1)} %get-tuple-element.78), channel_id=1, source_target_pairs={{0,16},{4,20},{8,24},{12,28},{16,0},{20,4},{24,8},{28,12},{1,17},{... | collective-permute-start | bytes 589832 | tf_op jit(solution)/shard_map/ppermute | solution.py:37
  183.6 7.4 %collective-permute-start.33 = (bf16[3,128,256]{2,1,0:T(8,128)(2,1)S(1)}, bf16[3,128,256]{2,1,0:T(8,128)(2,1)S(1)}, u32[]{:S(2)}, u32[]{:S(2)}) collective-permute-start(bf16[3,128,256]{2,1,0:T(8,128)(2,1)S(1)} %get-tuple-element.78), channel_id=1, source_target_pairs={{0,8},{4,12},{8,0},{12,4},{16,24},{20,28},{24,16},{28,20},{1,9},{5... | collective-permute-start | bytes 589832 | tf_op jit(solution)/shard_map/ppermute | solution.py:37
  184.1 9.6 %collective-permute-start.35 = (bf16[3,128,256]{2,1,0:T(8,128)(2,1)S(1)}, bf16[3,128,256]{2,1,0:T(8,128)(2,1)S(1)}, u32[]{:S(2)}, u32[]{:S(2)}) collective-permute-start(bf16[3,128,256]{2,1,0:T(8,128)(2,1)S(1)} %get-tuple-element.78), channel_id=1, source_target_pairs={{0,24},{4,28},{8,16},{12,20},{16,8},{20,12},{24,0},{28,4},{1,25},{... | collective-permute-start | bytes 589832 | tf_op jit(solution)/shard_map/ppermute | solution.py:37
  194.7 9.1 %collective-permute-start.36 = (bf16[4,3,128,256]{3,2,1,0:T(8,128)(2,1)}, bf16[4,3,128,256]{3,2,1,0:T(8,128)(2,1)}, u32[]{:S(2)}, u32[]{:S(2)}) collective-permute-start(bf16[4,3,128,256]{3,2,1,0:T(8,128)(2,1)} %pad_maximum_fusion.3.own), channel_id=1, source_target_pairs={{0,4},{4,0},{8,12},{12,8},{16,20},{20,16},{24,28},{28,24},{1,5},{5... | collective-permute-start | bytes 2359304 | tf_op jit(solution)/shard_map/ppermute | solution.py:37
  (16 other events, 106.0 us)

commit v2 on v1

--- a/solution.py
+++ b/solution.py
@@ -117,8 +117,9 @@
         tokens = ref.shape[0]
         for part in range(2):
             kind = part
-            if group == 0:
-                kind = 1 - table[AT_Y] if part else table[AT_Y]
+            if group < GROUPS - 1:
+                bit = table[AT_X if group else AT_Y]
+                kind = 1 - bit if part else bit
             at = pl.multiple_of(width + (2 * kind + table[AT_CORE]) * half, half)
             turned[part * half:(part + 1) * half, source * tokens:(source + 1) * tokens] = ref[
                 :, pl.ds(at, half)
@@ -131,8 +132,9 @@
     for group, (mine, sib, out) in enumerate(((mine0, sib0, out0), (mine1, sib1, out1), (mine2, sib2, out2))):
         sources = (mine, sib)
         gradient_rows(table, group, width, half, sources, turned.at[group])
-        for block in range(blocks):
-            span = slice(block * columns, (block + 1) * columns)
+        narrow = min(columns, 256)
+        for start in range(0, width, narrow):
+            span = slice(start, start + narrow)
             values = jnp.concatenate([ref[:, span] for ref in sources], axis=0)
             out[:, span] = dot(turned[group], values, NN)
 
@@ -142,28 +144,27 @@
     columns = width // blocks
     sources = (got, fwd)
     gradient_rows(table, group, width, half, sources, turned)
-    for block in range(blocks):
-        span = slice(block * columns, (block + 1) * columns)
+    narrow = min(columns, 256)
+    for start in range(0, width, narrow):
+        span = slice(start, start + narrow)
+        block, inner = start // columns, slice(start % columns, start % columns + narrow)
         values = jnp.concatenate([ref[:, span] for ref in sources], axis=0)
         terms = (local[:, span] + dot(turned[...], values, NN)).astype(BF16)
-        if group == 0:
-            keep[block] = terms[:half]
-            send[block] = terms[half:]
+        if group < GROUPS - 1:
+            keep[block, :, inner] = terms[:half]
+            send[block, :, inner] = terms[half:]
             continue
-        if group == 1:
-            bit, value, at = table[AT_Z], block % 2, block // 2
-        else:
-            bit, value, at = table[AT_LOW], block // (blocks // 2), block % (blocks // 2)
+        bit, value, at = table[AT_LOW], block // (blocks // 2), block % (blocks // 2)
 
         @pl.when(bit == value)
         def _():
-            keep[0, at] = terms[:half]
-            keep[1, at] = terms[half:]
+            keep[0, at, :, inner] = terms[:half]
+            keep[1, at, :, inner] = terms[half:]
 
         @pl.when(bit != value)
         def _():
-            send[0, at] = terms[:half]
-            send[1, at] = terms[half:]
+            send[0, at, :, inner] = terms[:half]
+            send[1, at, :, inner] = terms[half:]
 
 
 def local_gradients(table, mine, sib, width, blocks, half):
@@ -185,7 +186,7 @@
 def layer_gradient(group, table, local, got, fwd, width, blocks, half):
     columns = width // blocks
     tokens = got.shape[0]
-    shape = (blocks, half, columns) if group == 0 else (2, blocks // 2, half, columns)
+    shape = (blocks, half, columns) if group < GROUPS - 1 else (2, blocks // 2, half, columns)
     return pl.pallas_call(
         functools.partial(gradient_kernel, group, width, blocks),
         in_specs=[SMEM] + [VMEM] * 3,
@@ -199,7 +200,7 @@
     )(table, local, got, fwd)
 
 
-def finish_kernel(scale, table, keep, got, keep_last, got_last, out, last, sums):
+def finish_kernel(scale, table, keep0, got0, keep1, got1, keep2, got2, out, last, sums):
     lane = lax.broadcasted_iota(jnp.int32, sums.shape, 1)
     held = (
         matrix_of(table, 0),
@@ -207,71 +208,73 @@
         2 * CHIPS + 2 * table[AT_Z] + table[AT_X],
     )
     total = jnp.zeros(sums.shape, F32)
-    for unit in range(GROUPS):
-        if unit < GROUPS - 1:
-            values = keep[unit, table[AT_LOW]].astype(F32) + got[unit].astype(F32)
-        else:
-            values = keep_last[...].astype(F32) + got_last[...].astype(F32)
-        values = (values * scale).astype(BF16)
-        if unit < GROUPS - 1:
-            out[unit] = values
-        else:
-            last[...] = values
-        wide = values.astype(F32)
-        total = total + jnp.where(lane == held[unit], jnp.sum(wide * wide), 0.0)
+    half = got0.shape[0]
+    for unit, (keep, at, got) in enumerate(
+        ((keep0, AT_LOW, got0), (keep1, AT_LOW, got1), (keep2, AT_Y, got2))
+    ):
+        partial = jnp.zeros((CHUNK, got.shape[1]), F32)
+        for start in range(0, half, CHUNK):
+            rows = slice(start, start + CHUNK)
+            values = keep[table[at], rows, :].astype(F32) + got[rows, :].astype(F32)
+            values = (values * scale).astype(BF16)
+            if unit < GROUPS - 1:
+                out[unit, rows, :] = values
+            else:
+                last[rows, :] = values
+            wide = values.astype(F32)
+            partial = partial + wide * wide
+        total = total + jnp.where(lane == held[unit], jnp.sum(partial), 0.0)
     sums[...] = total
 
 
-def finish(scale, table, keep, got, keep_last, got_last):
+def finish(scale, table, *pairs):
+    got = pairs[1]
     return pl.pallas_call(
         functools.partial(finish_kernel, scale),
-        in_specs=[SMEM] + [VMEM] * 4,
+        in_specs=[SMEM] + [VMEM] * 6,
         out_specs=[VMEM] * 3,
         out_shape=[
+            jax.ShapeDtypeStruct((GROUPS - 1,) + got.shape, BF16),
             jax.ShapeDtypeStruct(got.shape, BF16),
-            jax.ShapeDtypeStruct(got_last.shape, BF16),
             jax.ShapeDtypeStruct((1, 128), F32),
         ],
         cost_estimate=pl.CostEstimate(flops=1000 * got.size, bytes_accessed=8 * got.size, transcendentals=0),
         name="finish",
-    )(table, keep, got, keep_last, got_last)
-
-
-def momentum_kernel(table, factors, own, sib, momentum, momentum_out, nesterov, buffer, came, left):
+    )(table, *pairs)
+
+
+CHUNK = 16
+
+
+def momentum_kernel(table, factors, own, sib, momentum, momentum_out, nesterov):
     core, chip = table[AT_CORE], table[AT_CHIP]
     half = own.shape[2]
-    mats = buffer.shape[0]
-    ins = [pltpu.make_async_copy(momentum.at[m], buffer.at[m], came.at[m]) for m in range(mats)]
-    outs = [pltpu.make_async_copy(buffer.at[m], momentum_out.at[m], left.at[m]) for m in range(mats)]
-    for copy in ins:
-        copy.start()
-    for matrix in range(mats):
-        ins[matrix].wait()
+    for matrix in range(momentum.shape[0]):
         factor = factors[matrix]
         place, unit = chip_of(matrix) ^ chip, unit_of(matrix)
         for part, ref in ((core, own), (1 - core, sib)):
-            rows = pl.ds(pl.multiple_of(part * half, half), half)
-            step = factor * ref[place, unit].astype(F32)
-            fresh = momentum_rate * buffer[matrix, rows, :] + step
-            buffer[matrix, rows, :] = fresh
-            nesterov[matrix, rows, :] = (step + momentum_rate * fresh).astype(BF16)
-        outs[matrix].start()
-    for copy in outs:
-        copy.wait()
+
+            def chunk(i, carry):
+                source = pl.ds(pl.multiple_of(i * CHUNK, CHUNK), CHUNK)
+                rows = pl.ds(pl.multiple_of(part * half + i * CHUNK, CHUNK), CHUNK)
+                step = factor * ref[place, unit, source, :].astype(F32)
+                fresh = momentum_rate * momentum[matrix, rows, :] + step
+                momentum_out[matrix, rows, :] = fresh
+                nesterov[matrix, rows, :] = (step + momentum_rate * fresh).astype(BF16)
+                return carry
+
+            lax.fori_loop(0, half // CHUNK, chunk, 0, unroll=2)
 
 
 def momentum_step(table, factors, own, sib, momentum):
     mats, rows, columns = momentum.shape
     return pl.pallas_call(
         momentum_kernel,
-        in_specs=[SMEM, SMEM, VMEM, VMEM, ANY],
-        out_specs=[ANY, VMEM],
+        in_specs=[SMEM, SMEM, VMEM, VMEM, VMEM],
+        out_specs=[VMEM, VMEM],
         out_shape=[
             jax.ShapeDtypeStruct(momentum.shape, F32),
             jax.ShapeDtypeStruct(momentum.shape, BF16),
-        ],
-        scratch_shapes=[
-            pltpu.VMEM(momentum.shape, F32), pltpu.SemaphoreType.DMA((mats,)), pltpu.SemaphoreType.DMA((mats,))
         ],
         cost_estimate=pl.CostEstimate(
             flops=mats * rows * columns * 400, bytes_accessed=12 * mats * rows * columns, transcendentals=0
@@ -280,62 +283,49 @@
     )(table, factors, own, sib, momentum)
 
 
-def rows_kernel(table, factors, gradient, old, *outs):
+def input_rows(table, factor, gradient, momentum, matrix, out):
+    half = out.shape[0]
+
+    def chunk(i, carry):
+        source = pl.ds(pl.multiple_of(i * CHUNK, CHUNK), CHUNK)
+        rows = pl.ds(pl.multiple_of(table[AT_CORE] * half + i * CHUNK, CHUNK), CHUNK)
+        step = factor * gradient(source).astype(F32)
+        fresh = momentum_rate * momentum[matrix, rows, :] + step
+        out[source, :] = (step + momentum_rate * fresh).astype(BF16)
+        return carry
+
+    lax.fori_loop(0, half // CHUNK, chunk, 0, unroll=2)
+
+
+def rows_kernel(table, factors, gradient, momentum, *outs):
     for k, out in enumerate(outs):
         unit = jnp.minimum(table[AT_SHARD] ^ k, GROUPS - 1)
-        step = factors[matrix_of(table, unit)] * gradient[unit].astype(F32)
-        fresh = momentum_rate * old[unit] + step
-        out[...] = (step + momentum_rate * fresh).astype(BF16)
-
-
-def newton_rows(table, factors, gradient, old, shard_count):
-    _, half, columns = gradient.shape
-    return pl.pallas_call(
-        rows_kernel,
+        matrix = matrix_of(table, unit)
+        input_rows(
+            table, factors[matrix], lambda rows, u=unit: gradient[u, rows, :], momentum, matrix, out
+        )
+
+
+def carried_kernel(table, factors, own, momentum, *outs):
+    for k, out in enumerate(outs):
+        matrix = table[AT_LISTS + (table[AT_SHARD] ^ (k + 1))]
+        place, unit = chip_of(matrix) ^ table[AT_CHIP], unit_of(matrix)
+        input_rows(
+            table, factors[matrix], lambda rows, p=place, u=unit: own[p, u, rows, :], momentum, matrix, out
+        )
+
+
+def make_rows(kernel, count, table, factors, gradient, momentum):
+    half, columns = gradient.shape[-2:]
+    return pl.pallas_call(
+        kernel,
         in_specs=[SMEM, SMEM, VMEM, VMEM],
-        out_specs=[VMEM] * shard_count,
-        out_shape=[jax.ShapeDtypeStruct((half, columns), BF16)] * shard_count,
-        cost_estimate=pl.CostEstimate(
-            flops=shard_count * half * columns * 100, bytes_accessed=8 * shard_count * half * columns,
-            transcendentals=0,
-        ),
-        name="newton_rows",
-    )(table, factors, gradient, old)
-
-
-def carried_kernel(targets, table, factors, own, *rest):
-    refs, outs, sems = rest[0], rest[1:-2], rest[-2:]
-    buffer, sem = sems
-    core, chip, shard = table[AT_CORE], table[AT_CHIP], table[AT_SHARD]
-    half = own.shape[2]
-    matrices = [table[AT_LISTS + (shard ^ k)] for k in targets]
-    copies = []
-    for i, matrix in enumerate(matrices):
-        rows = pl.ds(pl.multiple_of(core * half, half), half)
-        copies.append(pltpu.make_async_copy(refs.at[matrix, rows, :], buffer.at[i], sem.at[i]))
-        copies[-1].start()
-    for i, matrix in enumerate(matrices):
-        copies[i].wait()
-        step = factors[matrix] * own[chip_of(matrix) ^ chip, unit_of(matrix)].astype(F32)
-        fresh = momentum_rate * buffer[i] + step
-        outs[i][...] = (step + momentum_rate * fresh).astype(BF16)
-
-
-def carried_rows(table, factors, own, momentum, shard_count):
-    half, columns = own.shape[2:]
-    targets = tuple(range(1, shard_count))
-    count = len(targets)
-    return pl.pallas_call(
-        functools.partial(carried_kernel, targets),
-        in_specs=[SMEM, SMEM, VMEM, ANY],
         out_specs=[VMEM] * count,
         out_shape=[jax.ShapeDtypeStruct((half, columns), BF16)] * count,
-        scratch_shapes=[pltpu.VMEM((count, half, columns), F32), pltpu.SemaphoreType.DMA((count,))],
         cost_estimate=pl.CostEstimate(
             flops=count * half * columns * 100, bytes_accessed=8 * count * half * columns, transcendentals=0
         ),
-        name="carried_rows",
-    )(table, factors, own, momentum)
+    )(table, factors, gradient, momentum)
 
 
 def newton_kernel(table, own, sib, out, x, mix):
@@ -526,20 +516,24 @@
         layers = [2 * group + (1 - chosen[group] if other else chosen[group]) for group in range(GROUPS)]
         return load_layers(layers, activations, cotangents)
 
-    gots = [swaps[group](value) for group, value in enumerate(loaded(True))]
+    gots = []
+    for group, value in enumerate(loaded(True)):
+        gots.append(swaps[group](value))
     mine = loaded(False)
     sib = [swap_rep(value, CORE) for value in mine]
-    fwds = [swap_rep(got, CORE) for got in gots]
+    fwds = []
+    for got in gots:
+        fwds.append(swap_rep(got, CORE))
     top = shard_count // 2
     low = (shard // top) & 1
     table = small_table(
         owners, [core, bit_x, bit_y, bit_z, chip, shard, place, low], shard, place, shard_count, slot_count
     )
     local = local_gradients(table, mine, sib, width, shard_count, half)
-    (first, first_sent), (second, second_sent), (third, third_sent) = [
-        layer_gradient(group, table, local[group], gots[group], fwds[group], width, shard_count, half)
-        for group in range(GROUPS)
-    ]
+    gradients = []
+    for group in range(GROUPS):
+        gradients.append(layer_gradient(group, table, local[group], gots[group], fwds[group], width, shard_count, half))
+    (first, first_sent), (second, second_sent), (third, third_sent) = gradients
 
     def over_middle(values):
         bit = 2
@@ -554,26 +548,24 @@
             bit *= 2
         return values
 
-    first_got, second_got, third_got = (
-        swaps[1](first_sent), swaps[2](second_sent), swap_shard(third_sent, top)
-    )
+    first_got = swaps[1](first_sent)
+    second_got = swaps[0](second_sent)
+    third_got = swap_shard(third_sent, top)
     first = add(first, first_got).reshape(shard_count // 2, 2, half, columns)
-    second = add(second, second_got)
     first_got = swaps[2](pick(first, 1 - bit_z, 1))
-    second_got = swaps[0](pick(second, 1 - bit_x))
+    second = add(second, second_got).reshape(shard_count // 2, 2, half, columns)
+    second_got = swaps[2](pick(second, 1 - bit_z, 1))
     third = add(third, third_got)
     third_got = swaps[0](pick(third, 1 - bit_x))
-    first = add(pick(first, bit_z, 1), first_got)
-    second = add(pick(second, bit_x), second_got)
-    terms = jnp.stack([first, second]).reshape(2, 2, shard_count // 4, half, columns)
-    terms = over_middle(terms.reshape(4, shard_count // 4, half, columns)).reshape(2, 2, half, columns)
-    got = swap_shard(pick(terms, 1 - low, 1), top)
+    pairs = []
+    for value, got in ((first, first_got), (second, second_got)):
+        value = add(pick(value, bit_z, 1), got).reshape(2, shard_count // 4, half, columns)
+        value = over_middle(value).reshape(2, half, columns)
+        pairs += [value, swap_shard(pick(value, 1 - low), top)]
     third = add(pick(third, bit_x), third_got).reshape(shard_count // 4, 2, half, columns)
     third = over_middle(jnp.swapaxes(third, 0, 1)).reshape(2, half, columns)
-    third_got = swaps[1](pick(third, 1 - bit_y))
-    terms, last, sums = finish(
-        1.0 / math.sqrt(token_total), table, terms, got, pick(third, bit_y), third_got
-    )
+    pairs += [third, swaps[1](pick(third, 1 - bit_y))]
+    terms, last, sums = finish(1.0 / math.sqrt(token_total), table, *pairs)
 
     turned = [
         (r * shard_count + s, (r ^ BIT_Y) * shard_count + (s ^ 1))
@@ -593,13 +585,7 @@
         bit *= 2
     factors = clip_factors(sums[0, :mats], bucket_starts, rows * width)
 
-    old = jnp.stack(
-        [
-            lax.dynamic_slice(momentum, (matrix, core * half, 0), (1, half, columns)).reshape(half, columns)
-            for matrix in (2 * bit_x + bit_y, CHIPS + chip, 2 * CHIPS + chip)
-        ]
-    )
-    whole = newton_rows(table, factors, gradient, old, shard_count)
+    whole = make_rows(rows_kernel, shard_count, table, factors, gradient, momentum)
     whole = jnp.stack(
         [whole[0]]
         + [
@@ -622,7 +608,7 @@
     all_gradient_sib = swap_rep(all_gradient, CORE)
     momentum_out, nesterov = momentum_step(table, factors, all_gradient, all_gradient_sib, momentum)
 
-    carried = carried_rows(table, factors, all_gradient, momentum, shard_count)
+    carried = make_rows(carried_kernel, shard_count - 1, table, factors, all_gradient, momentum)
     slot_rows = jnp.stack([swap_shard(carried[k - 1], k) for k in range(1, shard_count)])
     slot_rows = jnp.stack(
         [slot_rows] + [swap_rep(slot_rows, BIT_X * k) for k in range(1, slot_count)]

time: 212 us -> 216 us (1.019)
  Pallas kernels: 56 us -> 59.4 us
    ppermute x15 -> x16, waiting for transfers between devices: 49.5 us -> 53.4 us  [swap_shard(): return lax.ppermute(value, 'shard', pairs)]
    pallas_call x3, Pallas kernels: 14.6 us -> 17.8 us  [the longest x1 9.37 us: momentum_step(): pl.pallas_call(momentum_kernel, in_specs=[SMEM, SMEM, VMEM, VMEM, VMEM],...]
    ppermute x15 -> x16, starting transfers between devices: 29.4 us -> 28.8 us  [swap_shard(): return lax.ppermute(value, 'shard', pairs)]
  transfers between devices with their start and end apart: 44 -> 45, of which waited for: 23 -> 24; matrix products, arithmetic and copies ran while one was open for 7% -> 5% of each run, Pallas kernels for 19% -> 19%
where the time goes in v2:
time: 216 us
  waiting for transfers between devices  86.5 us (40%)
  Pallas kernels  59.4 us (28%)
  starting transfers between devices  51.6 us (24%)
  other arithmetic  14 us (6%)
  local copies, waits for them, and re-layouts  3.04 us (1%)
    ppermute x16, waiting for transfers between devices, swap_shard(): return lax.ppermute(value, 'shard', pairs)  53.4 us
    ppermute x28, waiting for transfers between devices, swap_rep(): return lax.ppermute(value, 'rep', [(i, i ^ bit) for i in range(count)])  33 us
    ppermute x16, starting transfers between devices, swap_shard(): return lax.ppermute(value, 'shard', pairs)  28.8 us
    ppermute x28, starting transfers between devices, swap_rep(): return lax.ppermute(value, 'rep', [(i, i ^ bit) for i in range(count)])  22.2 us
    pallas_call x3, Pallas kernels, layer_gradient(): pl.pallas_call(functools.partial(gradient_kernel, group, width, blocks),...  11.5 us
    pallas_call x1, Pallas kernels, momentum_step(): pl.pallas_call(momentum_kernel, in_specs=[SMEM, SMEM, VMEM, VMEM, VMEM],...  9.37 us
    pallas_call x2, Pallas kernels, make_rows(): pl.pallas_call(kernel, in_specs=[SMEM, SMEM, VMEM, VMEM], out_specs=[VMEM...  8.46 us
    pallas_call x1, Pallas kernels, apply_step(): pl.pallas_call(functools.partial(apply_kernel, scale, AT_LISTS + shard_co...  7.84 us
  transfers between devices with their start and end apart: 45, of which 24 were waited for; matrix products, arithmetic and copies ran while one was open for 5% of the time, Pallas kernels for 19%

profile of v2, /device:TPU:0, one launch (start us, length us, event | category | flops | bytes accessed | tf_op | source)
XLA Modules:
  0.0 215.8 jit_solution(14225382162353551772)
XLA Ops:
  1.3 3.5 %load_layers.2 = (bf16[128,2560]{1,0:T(8,128)(2,1)}, bf16[128,2560]{1,0:T(8,128)(2,1)}, bf16[128,2560]{1,0:T(8,128)(2,1)}) custom-call(s32[3]{0:T(128)} %get-tuple-element.74.table, bf16[6,128,2048]{2,1,0:T(8,128)(2,1)} %activations.3, bf16[6,128,512]{2,1,0:T(8,128)(2,1)} %cotangents.3), custom_call_target="tpu_custom_call" | custom-call | flops 78643200 | bytes 3932160 | tf_op jit(solution)/shard_map/load_layers/pallas_call | solution.py:101
  5.3 3.6 %load_layers.3 = (bf16[128,2560]{1,0:T(8,128)(2,1)}, bf16[128,2560]{1,0:T(8,128)(2,1)}, bf16[128,2560]{1,0:T(8,128)(2,1)}) custom-call(s32[3]{0:T(128)} %get-tuple-element.75.table, bf16[6,128,2048]{2,1,0:T(8,128)(2,1)} %activations.3, bf16[6,128,512]{2,1,0:T(8,128)(2,1)} %cotangents.3), custom_call_target="tpu_custom_call" | custom-call | flops 78643200 | bytes 3932160 | tf_op jit(solution)/shard_map/load_layers/pallas_call | solution.py:101
  8.9 2.6 %collective-permute-start.3 = (bf16[128,2560]{1,0:T(8,128)(2,1)}, bf16[128,2560]{1,0:T(8,128)(2,1)}, u32[]{:S(2)}, u32[]{:S(2)}) collective-permute-start(bf16[128,2560]{1,0:T(8,128)(2,1)} %get-tuple-element.36), channel_id=1, source_target_pairs={{0,8},{4,12},{8,0},{12,4},{16,24},{20,28},{24,16},{28,20},{1,9},{5... | collective-permute-start | bytes 1966088 | tf_op jit(solution)/shard_map/ppermute | solution.py:37
  13.6 1.6 collective-permute-start.13
  15.1 12.1 %collective-permute-done.3.got = bf16[128,2560]{1,0:T(8,128)(2,1)} collective-permute-done((bf16[128,2560]{1,0:T(8,128)(2,1)}, bf16[128,2560]{1,0:T(8,128)(2,1)}, u32[]{:S(2)}, u32[]{:S(2)}) %collective-permute-start.3) | collective-permute-done | bytes 655392 | tf_op jit(solution)/shard_map/ppermute | solution.py:37
  28.7 1.8 collective-permute-done.13.got
  31.3 5.3 %local_gradients.1 = (f32[256,2048]{1,0:T(8,128)}, f32[256,2048]{1,0:T(8,128)}, f32[256,2048]{1,0:T(8,128)}) custom-call(s32[20]{0:T(128)} %concatenate.13.table, bf16[128,2560]{1,0:T(8,128)(2,1)} %get-tuple-element.32.mine0, bf16[128,2560]{1,0:T(8,128)(2,1)} %get-tuple-element.33.mine1, bf16[128,2560]{1,0:T(8,128)(2,1)} %get-tuple-element.34.mine2, ...), custom_call_target="tpu_custom_call" | custom-call | flops 805306368 | bytes 9437184 | tf_op jit(solution)/shard_map/local_gradients/pallas_call | solution.py:172
  36.6 3.4 %layer_gradient.3 = (bf16[4,128,512]{2,1,0:T(8,128)(2,1)}, bf16[4,128,512]{2,1,0:T(8,128)(2,1)}) custom-call(s32[20]{0:T(128)} %concatenate.13.table, f32[256,2048]{1,0:T(8,128)} %get-tuple-element.35.local, bf16[128,2560]{1,0:T(8,128)(2,1)} %collective-permute-done.3.got, bf16[128,2560]{1,0:T(8,128)(2,1)} %collective-permute-done.4.fwd), custom_call_target="tpu_custom_call" | custom-call | flops 268435456 | bytes 3145728 | tf_op jit(solution)/shard_map/layer_gradient/pallas_call | solution.py:190
  40.4 3.4 %layer_gradient.4 = (bf16[4,128,512]{2,1,0:T(8,128)(2,1)}, bf16[4,128,512]{2,1,0:T(8,128)(2,1)}) custom-call(s32[20]{0:T(128)} %concatenate.13.table, f32[256,2048]{1,0:T(8,128)} %get-tuple-element.39.local, bf16[128,2560]{1,0:T(8,128)(2,1)} %copy-done.7, bf16[128,2560]{1,0:T(8,128)(2,1)} %collective-permute-done.9.fwd), custom_call_target="tpu_custom_call" | custom-call | flops 268435456 | bytes 3145728 | tf_op jit(solution)/shard_map/layer_gradient/pallas_call | solution.py:190
  44.3 4.8 %layer_gradient.5 = (bf16[2,2,128,512]{3,2,1,0:T(8,128)(2,1)}, bf16[2,2,128,512]{3,2,1,0:T(8,128)(2,1)}) custom-call(s32[20]{0:T(128)} %concatenate.13.table, f32[256,2048]{1,0:T(8,128)} %get-tuple-element.43.local, bf16[128,2560]{1,0:T(8,128)(2,1)} %copy-done.6, bf16[128,2560]{1,0:T(8,128)(2,1)} %collective-permute-done.14.fwd), custom_call_target="tpu_custom_call" | custom-call | flops 268435456 | bytes 3145728 | tf_op jit(solution)/shard_map/layer_gradient/pallas_call | solution.py:190
  49.1 2.6 %collective-permute-start.15 = (bf16[2,2,128,512]{3,2,1,0:T(8,128)(2,1)}, bf16[2,2,128,512]{3,2,1,0:T(8,128)(2,1)S(1)}, u32[]{:S(2)}, u32[]{:S(2)}) collective-permute-start(bf16[2,2,128,512]{3,2,1,0:T(8,128)(2,1)} %get-tuple-element.46), channel_id=1, source_target_pairs={{0,2},{1,3},{2,0},{3,1},{4,6},{5,7},{6,4},{7,5},{8,10},{9,11},{10,... | collective-permute-start | bytes 1572872 | tf_op jit(solution)/shard_map/ppermute | solution.py:43
  51.7 2.8 %collective-permute-done.5 = bf16[4,128,512]{2,1,0:T(8,128)(2,1)S(1)} collective-permute-done((bf16[4,128,512]{2,1,0:T(8,128)(2,1)}, bf16[4,128,512]{2,1,0:T(8,128)(2,1)S(1)}, u32[]{:S(2)}, u32[]{:S(2)}) %collective-permute-start.5) | collective-permute-done | bytes 524320 | tf_op jit(solution)/shard_map/ppermute | solution.py:37
  54.7 1.6 collective-permute-start.6
  56.3 1.8 collective-permute-done.10
  58.2 1.6 collective-permute-start.11
  59.9 15.4 %collective-permute-done.15 = bf16[2,2,128,512]{3,2,1,0:T(8,128)(2,1)S(1)} collective-permute-done((bf16[2,2,128,512]{3,2,1,0:T(8,128)(2,1)}, bf16[2,2,128,512]{3,2,1,0:T(8,128)(2,1)S(1)}, u32[]{:S(2)}, u32[]{:S(2)}) %collective-permute-start.15) | collective-permute-done | bytes 524320 | tf_op jit(solution)/shard_map/ppermute | solution.py:43
  75.5 1.6 collective-permute-start.16
  78.4 2.8 %collective-permute-start.12 = (bf16[128,512]{1,0:T(8,128)(2,1)S(1)}, bf16[128,512]{1,0:T(8,128)(2,1)S(1)}, u32[]{:S(2)}, u32[]{:S(2)}) collective-permute-start(bf16[128,512]{1,0:T(8,128)(2,1)S(1)} %dynamic-slice_bitcast_fusion.4), channel_id=1, source_target_pairs={{0,2},{1,3},{2,0},{3,1},{4,6},{5,7},{6,4},{7,5},{8,10},{9,11},{10,... | collective-permute-start | bytes 393224 | tf_op jit(solution)/shard_map/ppermute | solution.py:43
  82.9 1.6 collective-permute-start.17
  84.5 4.8 %collective-permute-done.7.got0 = bf16[128,512]{1,0:T(8,128)(2,1)S(1)} collective-permute-done((bf16[128,512]{1,0:T(8,128)(2,1)S(1)}, bf16[128,512]{1,0:T(8,128)(2,1)S(1)}, u32[]{:S(2)}, u32[]{:S(2)}) %collective-permute-start.7) | collective-permute-done | bytes 131104 | tf_op jit(solution)/shard_map/ppermute | solution.py:43
  92.1 2.1 finish.1
  96.7 3.1 %collective-permute-done.19 = f32[1,128]{1,0:T(1,128)S(1)} collective-permute-done((f32[1,128]{1,0:T(1,128)S(1)}, f32[1,128]{1,0:T(1,128)S(1)}, u32[]{:S(2)}, u32[]{:S(2)}) %collective-permute-start.19) | collective-permute-done | bytes 544 | tf_op jit(solution)/shard_map/ppermute | solution.py:37
  99.7 1.6 collective-permute-start.20
  101.3 2.0 collective-permute-done.20
  103.3 3.6 %collective-permute-done.21 = f32[1,128]{1,0:T(1,128)S(1)} collective-permute-done((f32[1,128]{1,0:T(1,128)S(1)}, f32[1,128]{1,0:T(1,128)S(1)}, u32[]{:S(2)}, u32[]{:S(2)}) %collective-permute-start.21) | collective-permute-done | bytes 544 | tf_op jit(solution)/shard_map/ppermute | solution.py:43
  107.9 3.5 %collective-permute-done.22 = f32[1,128]{1,0:T(1,128)S(1)} collective-permute-done((f32[1,128]{1,0:T(1,128)S(1)}, f32[1,128]{1,0:T(1,128)S(1)}, u32[]{:S(2)}, u32[]{:S(2)}) %collective-permute-start.22) | collective-permute-done | bytes 544 | tf_op jit(solution)/shard_map/ppermute | solution.py:43
  113.0 1.7 fusion.10
  114.8 4.1 %shard_map.76 = (bf16[128,512]{1,0:T(8,128)(2,1)}, bf16[128,512]{1,0:T(8,128)(2,1)}, bf16[128,512]{1,0:T(8,128)(2,1)}, bf16[128,512]{1,0:T(8,128)(2,1)}) custom-call(s32[20]{0:T(128)} %concatenate.13.table, f32[12]{0:T(128)} %multiply_minimum_fusion.factors, bf16[3,128,512]{2,1,0:T(8,128)(2,1)} %get-tuple-element.68.gradient, f32[12,256,512]{2,1,0:T(8,128)} %momentum.5), custom_call_target="tpu_custom_call" | custom-call | flops 26214400 | bytes 2097152 | tf_op jit(solution)/shard_map/pallas_call | solution.py:320
  118.9 6.1 %collective-permute-start.28 = (bf16[128,512]{1,0:T(8,128)(2,1)}, bf16[128,512]{1,0:T(8,128)(2,1)S(1)}, u32[]{:S(2)}, u32[]{:S(2)}) collective-permute-start(bf16[128,512]{1,0:T(8,128)(2,1)} %get-tuple-element.52), channel_id=1, source_target_pairs={{0,1},{1,0},{3,2},{4,5},{5,4},{7,6},{8,9},{9,8},{11,10},{12,13},{1... | collective-permute-start | bytes 393224 | tf_op jit(solution)/shard_map/ppermute | solution.py:43
  125.1 2.2 %collective-permute-start.25 = (bf16[3,128,512]{2,1,0:T(8,128)(2,1)S(1)}, bf16[3,128,512]{2,1,0:T(8,128)(2,1)S(1)}, u32[]{:S(2)}, u32[]{:S(2)}) collective-permute-start(bf16[3,128,512]{2,1,0:T(8,128)(2,1)S(1)} %copy-done.5), channel_id=1, source_target_pairs={{0,16},{4,20},{8,24},{12,28},{16,0},{20,4},{24,8},{28,12},{1,17},{... | collective-permute-start | bytes 1179656 | tf_op jit(solution)/shard_map/ppermute | solution.py:37
  128.6 1.9 collective-permute-start.29
  132.0 5.4 %collective-permute-done.29 = bf16[128,512]{1,0:T(8,128)(2,1)S(1)} collective-permute-done((bf16[128,512]{1,0:T(8,128)(2,1)}, bf16[128,512]{1,0:T(8,128)(2,1)S(1)}, u32[]{:S(2)}, u32[]{:S(2)}) %collective-permute-start.29) | collective-permute-done | bytes 131104 | tf_op jit(solution)/shard_map/ppermute | solution.py:43
  137.4 2.1 collective-permute-done.30
  141.9 4.3 %shard_map.77 = (bf16[128,512]{1,0:T(8,128)(2,1)}, bf16[128,512]{1,0:T(8,128)(2,1)}, bf16[128,512]{1,0:T(8,128)(2,1)}) custom-call(s32[20]{0:T(128)} %concatenate.13.table, f32[12]{0:T(128)} %multiply_minimum_fusion.factors, bf16[4,3,128,512]{3,2,1,0:T(8,128)(2,1)} %pad_maximum_fusion.own, f32[12,256,512]{2,1,0:T(8,128)} %momentum.5), custom_call_target="tpu_custom_call" | custom-call | flops 19660800 | bytes 1572864 | tf_op jit(solution)/shard_map/pallas_call | solution.py:320
  149.0 1.6 collective-permute-start.40
  150.6 3.2 %collective-permute-done.38 = bf16[128,512]{1,0:T(8,128)(2,1)S(1)} collective-permute-done((bf16[128,512]{1,0:T(8,128)(2,1)}, bf16[128,512]{1,0:T(8,128)(2,1)S(1)}, u32[]{:S(2)}, u32[]{:S(2)}) %collective-permute-start.38) | collective-permute-done | bytes 131104 | tf_op jit(solution)/shard_map/ppermute | solution.py:43
  153.8 6.8 %collective-permute-done.39 = bf16[128,512]{1,0:T(8,128)(2,1)S(1)} collective-permute-done((bf16[128,512]{1,0:T(8,128)(2,1)}, bf16[128,512]{1,0:T(8,128)(2,1)S(1)}, u32[]{:S(2)}, u32[]{:S(2)}) %collective-permute-start.39) | collective-permute-done | bytes 131104 | tf_op jit(solution)/shard_map/ppermute | solution.py:43
  162.7 2.3 %collective-permute-start.43 = (bf16[3,128,512]{2,1,0:T(8,128)(2,1)}, bf16[3,128,512]{2,1,0:T(8,128)(2,1)}, u32[]{:S(2)}, u32[]{:S(2)}) collective-permute-start(bf16[3,128,512]{2,1,0:T(8,128)(2,1)} %get-tuple-element.66), channel_id=1, source_target_pairs={{0,24},{4,28},{8,16},{12,20},{16,8},{20,12},{24,0},{28,4},{1,25},{... | collective-permute-start | bytes 1179656 | tf_op jit(solution)/shard_map/ppermute | solution.py:37
  164.9 7.8 %newton.1 = bf16[128,256]{1,0:T(8,128)(2,1)} custom-call(s32[20]{0:T(128)} %concatenate.13.table, bf16[4,128,512]{2,1,0:T(8,128)(2,1)} %copy-done.14, bf16[4,128,512]{2,1,0:T(8,128)(2,1)} %collective-permute-done.31.sib), custom_call_target="tpu_custom_call" | custom-call | flops 3187671040 | bytes 4194304 | tf_op jit(solution)/shard_map/newton/pallas_call | solution.py:370
  172.8 2.6 %collective-permute-start.32 = (bf16[1,128,256]{2,1,0:T(8,128)(2,1)}, bf16[1,128,256]{2,1,0:T(8,128)(2,1)S(1)}, u32[]{:S(2)}, u32[]{:S(2)}) collective-permute-start(bf16[1,128,256]{2,1,0:T(8,128)(2,1)} %bitcast.76), channel_id=1, source_target_pairs={{0,1},{1,0},{2,3},{3,2},{4,5},{5,4},{6,7},{7,6},{8,9},{9,8},{10,11... | collective-permute-start | bytes 196616 | tf_op jit(solution)/shard_map/ppermute | solution.py:43
  175.3 2.4 %collective-permute-done.32 = bf16[1,128,256]{2,1,0:T(8,128)(2,1)S(1)} collective-permute-done((bf16[1,128,256]{2,1,0:T(8,128)(2,1)}, bf16[1,128,256]{2,1,0:T(8,128)(2,1)S(1)}, u32[]{:S(2)}, u32[]{:S(2)}) %collective-permute-start.32) | collective-permute-done | bytes 65568 | tf_op jit(solution)/shard_map/ppermute | solution.py:43
  179.3 1.8 collective-permute-start.33
  183.5 2.0 collective-permute-done.33
  187.7 2.4 %collective-permute-start.36 = (bf16[3,128,256]{2,1,0:T(8,128)(2,1)S(1)}, bf16[3,128,256]{2,1,0:T(8,128)(2,1)S(1)}, u32[]{:S(2)}, u32[]{:S(2)}) collective-permute-start(bf16[3,128,256]{2,1,0:T(8,128)(2,1)S(1)} %get-tuple-element.73), channel_id=1, source_target_pairs={{0,24},{4,28},{8,16},{12,20},{16,8},{20,12},{24,0},{28,4},{1,25},{... | collective-permute-start | bytes 589832 | tf_op jit(solution)/shard_map/ppermute | solution.py:37
  190.1 4.1 %collective-permute-done.35 = bf16[3,128,256]{2,1,0:T(8,128)(2,1)S(1)} collective-permute-done((bf16[3,128,256]{2,1,0:T(8,128)(2,1)S(1)}, bf16[3,128,256]{2,1,0:T(8,128)(2,1)S(1)}, u32[]{:S(2)}, u32[]{:S(2)}) %collective-permute-start.35) | collective-permute-done | bytes 196640 | tf_op jit(solution)/shard_map/ppermute | solution.py:37
  194.8 2.5 %collective-permute-done.36 = bf16[3,128,256]{2,1,0:T(8,128)(2,1)S(1)} collective-permute-done((bf16[3,128,256]{2,1,0:T(8,128)(2,1)S(1)}, bf16[3,128,256]{2,1,0:T(8,128)(2,1)S(1)}, u32[]{:S(2)}, u32[]{:S(2)}) %collective-permute-start.36) | collective-permute-done | bytes 196640 | tf_op jit(solution)/shard_map/ppermute | solution.py:37
  198.4 9.4 %momentum_step.1 = (f32[12,256,512]{2,1,0:T(8,128)}, bf16[12,256,512]{2,1,0:T(8,128)(2,1)}) custom-call(s32[20]{0:T(128)} %concatenate.13.table, f32[12]{0:T(128)} %multiply_minimum_fusion.factors, bf16[4,3,128,512]{3,2,1,0:T(8,128)(2,1)} %pad_maximum_fusion.own, bf16[4,3,128,512]{3,2,1,0:T(8,128)(2,1)} %collective-permute-done.27.sib, f32[12,256,512]{2,1,0:T(8,128)} %momentum.5), custom_call_target="tpu_custom_call" | custom-call | flops 629145600 | bytes 18874368 | tf_op jit(solution)/shard_map/momentum_step/pallas_call | solution.py:271
  207.8 7.8 %apply_step.1 = (f32[12,256,512]{2,1,0:T(8,128)}, bf16[4,256,2048]{2,1,0:T(8,128)(2,1)}) custom-call(s32[20]{0:T(128)} %concatenate.13.table, bf16[4,3,128,256]{3,2,1,0:T(8,128)(2,1)} %pad_maximum_fusion.2.own, bf16[4,3,128,256]{3,2,1,0:T(8,128)(2,1)} %collective-permute-done.37.sib, bf16[12,256,512]{2,1,0:T(8,128)(2,1)} %get-tuple-element.55.values, ...), custom_call_target="tpu_custom_call" | custom-call | flops 1879048192 | bytes 13631488 | tf_op jit(solution)/shard_map/apply_step/pallas_call | solution.py:430
  (139 shorter events, 35.6 us)
Async XLA Ops:
  4.8 8.8 %collective-permute-start = (bf16[128,2560]{1,0:T(8,128)(2,1)}, bf16[128,2560]{1,0:T(8,128)(2,1)S(1)}, u32[]{:S(2)}, u32[]{:S(2)}) collective-permute-start(bf16[128,2560]{1,0:T(8,128)(2,1)} %get-tuple-element.32.mine0), channel_id=1, source_target_pairs={{0,4},{4,0},{8,12},{12,8},{16,20},{20,16},{24,28},{28,24},{1,5},{5... | collective-permute-start | bytes 1966088 | tf_op jit(solution)/shard_map/ppermute | solution.py:37
  5.3 21.9 %copy-start.21 = (s32[12]{0:T(128)S(1)}, s32[12]{0:T(128)}, u32[]{:S(2)}) copy-start(s32[12]{0:T(128)} %param.8) | copy-start | bytes 148
  8.9 18.3 %collective-permute-start.3 = (bf16[128,2560]{1,0:T(8,128)(2,1)}, bf16[128,2560]{1,0:T(8,128)(2,1)}, u32[]{:S(2)}, u32[]{:S(2)}) collective-permute-start(bf16[128,2560]{1,0:T(8,128)(2,1)} %get-tuple-element.36), channel_id=1, source_target_pairs={{0,8},{4,12},{8,0},{12,4},{16,24},{20,28},{24,16},{28,20},{1,9},{5... | collective-permute-start | bytes 1966088 | tf_op jit(solution)/shard_map/ppermute | solution.py:37
  11.5 17.0 %collective-permute-start.8 = (bf16[128,2560]{1,0:T(8,128)(2,1)}, bf16[128,2560]{1,0:T(8,128)(2,1)S(1)}, u32[]{:S(2)}, u32[]{:S(2)}) collective-permute-start(bf16[128,2560]{1,0:T(8,128)(2,1)} %get-tuple-element.40), channel_id=1, source_target_pairs={{0,16},{4,20},{8,24},{12,28},{16,0},{20,4},{24,8},{28,12},{1,17},{... | collective-permute-start | bytes 1966088 | tf_op jit(solution)/shard_map/ppermute | solution.py:37
  13.0 18.3 %collective-permute-start.1 = (bf16[128,2560]{1,0:T(8,128)(2,1)S(1)}, bf16[128,2560]{1,0:T(8,128)(2,1)}, u32[]{:S(2)}, u32[]{:S(2)}) collective-permute-start(bf16[128,2560]{1,0:T(8,128)(2,1)S(1)} %copy-done.8), channel_id=1, source_target_pairs={{0,4},{4,0},{8,12},{12,8},{16,20},{20,16},{24,28},{28,24},{1,5},{5... | collective-permute-start | bytes 1966088 | tf_op jit(solution)/shard_map/ppermute | solution.py:37
  13.0 18.2 %collective-permute-start.2 = (bf16[128,2560]{1,0:T(8,128)(2,1)S(1)}, bf16[128,2560]{1,0:T(8,128)(2,1)}, u32[]{:S(2)}, u32[]{:S(2)}) collective-permute-start(bf16[128,2560]{1,0:T(8,128)(2,1)S(1)} %copy-done.9), channel_id=1, source_target_pairs={{0,4},{4,0},{8,12},{12,8},{16,20},{20,16},{24,28},{28,24},{1,5},{5... | collective-permute-start | bytes 1966088 | tf_op jit(solution)/shard_map/ppermute | solution.py:37
  13.6 16.9 %collective-permute-start.13 = (bf16[128,2560]{1,0:T(8,128)(2,1)}, bf16[128,2560]{1,0:T(8,128)(2,1)S(1)}, u32[]{:S(2)}, u32[]{:S(2)}) collective-permute-start(bf16[128,2560]{1,0:T(8,128)(2,1)} %get-tuple-element.44), channel_id=1, source_target_pairs={{0,1},{1,0},{2,3},{3,2},{4,5},{5,4},{6,7},{7,6},{8,9},{9,8},{10,11... | collective-permute-start | bytes 1966088 | tf_op jit(solution)/shard_map/ppermute | solution.py:43
  27.2 9.4 %collective-permute-start.4 = (bf16[128,2560]{1,0:T(8,128)(2,1)}, bf16[128,2560]{1,0:T(8,128)(2,1)}, u32[]{:S(2)}, u32[]{:S(2)}) collective-permute-start(bf16[128,2560]{1,0:T(8,128)(2,1)} %collective-permute-done.3.got), channel_id=1, source_target_pairs={{0,4},{4,0},{8,12},{12,8},{16,20},{20,16},{24,28},{28,24},{1,5},{5... | collective-permute-start | bytes 1966088 | tf_op jit(solution)/shard_map/ppermute | solution.py:37
  28.5 11.9 %collective-permute-start.9 = (bf16[128,2560]{1,0:T(8,128)(2,1)S(1)}, bf16[128,2560]{1,0:T(8,128)(2,1)}, u32[]{:S(2)}, u32[]{:S(2)}) collective-permute-start(bf16[128,2560]{1,0:T(8,128)(2,1)S(1)} %collective-permute-done.8.got), channel_id=1, source_target_pairs={{0,4},{4,0},{8,12},{12,8},{16,20},{20,16},{24,28},{28,24},{1,5},{5... | collective-permute-start | bytes 1966088 | tf_op jit(solution)/shard_map/ppermute | solution.py:37
  30.5 13.8 %collective-permute-start.14 = (bf16[128,2560]{1,0:T(8,128)(2,1)S(1)}, bf16[128,2560]{1,0:T(8,128)(2,1)}, u32[]{:S(2)}, u32[]{:S(2)}) collective-permute-start(bf16[128,2560]{1,0:T(8,128)(2,1)S(1)} %collective-permute-done.13.got), channel_id=1, source_target_pairs={{0,4},{4,0},{8,12},{12,8},{16,20},{20,16},{24,28},{28,24},{1,5},{5... | collective-permute-start | bytes 1966088 | tf_op jit(solution)/shard_map/ppermute | solution.py:37
  39.9 14.6 %collective-permute-start.5 = (bf16[4,128,512]{2,1,0:T(8,128)(2,1)}, bf16[4,128,512]{2,1,0:T(8,128)(2,1)S(1)}, u32[]{:S(2)}, u32[]{:S(2)}) collective-permute-start(bf16[4,128,512]{2,1,0:T(8,128)(2,1)} %get-tuple-element.38), channel_id=1, source_target_pairs={{0,16},{4,20},{8,24},{12,28},{16,0},{20,4},{24,8},{28,12},{1,17},{... | collective-permute-start | bytes 1572872 | tf_op jit(solution)/shard_map/ppermute | solution.py:37
  43.8 14.3 %collective-permute-start.10 = (bf16[4,128,512]{2,1,0:T(8,128)(2,1)}, bf16[4,128,512]{2,1,0:T(8,128)(2,1)S(1)}, u32[]{:S(2)}, u32[]{:S(2)}) collective-permute-start(bf16[4,128,512]{2,1,0:T(8,128)(2,1)} %get-tuple-element.42), channel_id=1, source_target_pairs={{0,8},{4,12},{8,0},{12,4},{16,24},{20,28},{24,16},{28,20},{1,9},{5... | collective-permute-start | bytes 1572872 | tf_op jit(solution)/shard_map/ppermute | solution.py:37
  49.1 26.2 %collective-permute-start.15 = (bf16[2,2,128,512]{3,2,1,0:T(8,128)(2,1)}, bf16[2,2,128,512]{3,2,1,0:T(8,128)(2,1)S(1)}, u32[]{:S(2)}, u32[]{:S(2)}) collective-permute-start(bf16[2,2,128,512]{3,2,1,0:T(8,128)(2,1)} %get-tuple-element.46), channel_id=1, source_target_pairs={{0,2},{1,3},{2,0},{3,1},{4,6},{5,7},{6,4},{7,5},{8,10},{9,11},{10,... | collective-permute-start | bytes 1572872 | tf_op jit(solution)/shard_map/ppermute | solution.py:43
  54.7 22.4 %collective-permute-start.6 = (bf16[2,128,512]{2,1,0:T(8,128)(2,1)S(1)}, bf16[2,128,512]{2,1,0:T(8,128)(2,1)S(1)}, u32[]{:S(2)}, u32[]{:S(2)}) collective-permute-start(bf16[2,128,512]{2,1,0:T(8,128)(2,1)S(1)} %dynamic-slice_bitcast_fusion.2), channel_id=1, source_target_pairs={{0,1},{1,0},{2,3},{3,2},{4,5},{5,4},{6,7},{7,6},{8,9},{9,8},{10,11... | collective-permute-start | bytes 786440 | tf_op jit(solution)/shard_map/ppermute | solution.py:43
  58.2 20.1 %collective-permute-start.11 = (bf16[2,128,512]{2,1,0:T(8,128)(2,1)S(1)}, bf16[2,128,512]{2,1,0:T(8,128)(2,1)S(1)}, u32[]{:S(2)}, u32[]{:S(2)}) collective-permute-start(bf16[2,128,512]{2,1,0:T(8,128)(2,1)S(1)} %dynamic-slice_bitcast_fusion.1), channel_id=1, source_target_pairs={{0,1},{1,0},{2,3},{3,2},{4,5},{5,4},{6,7},{7,6},{8,9},{9,8},{10,11... | collective-permute-start | bytes 786440 | tf_op jit(solution)/shard_map/ppermute | solution.py:43
  75.5 7.3 %collective-permute-start.16 = (bf16[2,128,512]{2,1,0:T(8,128)(2,1)S(1)}, bf16[2,128,512]{2,1,0:T(8,128)(2,1)S(1)}, u32[]{:S(2)}, u32[]{:S(2)}) collective-permute-start(bf16[2,128,512]{2,1,0:T(8,128)(2,1)S(1)} %dynamic-slice_bitcast_fusion), channel_id=1, source_target_pairs={{0,8},{4,12},{8,0},{12,4},{16,24},{20,28},{24,16},{28,20},{1,9},{5... | collective-permute-start | bytes 786440 | tf_op jit(solution)/shard_map/ppermute | solution.py:37
  77.2 29.9 %copy-start.22 = (s32[2]{0:T(128)S(1)}, s32[2]{0:T(128)}, u32[]{:S(2)}) copy-start(s32[2]{0:T(128)} %param.9) | copy-start | bytes 28
  77.2 12.2 %collective-permute-start.7 = (bf16[128,512]{1,0:T(8,128)(2,1)S(1)}, bf16[128,512]{1,0:T(8,128)(2,1)S(1)}, u32[]{:S(2)}, u32[]{:S(2)}) collective-permute-start(bf16[128,512]{1,0:T(8,128)(2,1)S(1)} %dynamic-slice_bitcast_fusion.5), channel_id=1, source_target_pairs={{0,2},{1,3},{2,0},{3,1},{4,6},{5,7},{6,4},{7,5},{8,10},{9,11},{10,... | collective-permute-start | bytes 393224 | tf_op jit(solution)/shard_map/ppermute | solution.py:43
  78.4 12.3 %collective-permute-start.12 = (bf16[128,512]{1,0:T(8,128)(2,1)S(1)}, bf16[128,512]{1,0:T(8,128)(2,1)S(1)}, u32[]{:S(2)}, u32[]{:S(2)}) collective-permute-start(bf16[128,512]{1,0:T(8,128)(2,1)S(1)} %dynamic-slice_bitcast_fusion.4), channel_id=1, source_target_pairs={{0,2},{1,3},{2,0},{3,1},{4,6},{5,7},{6,4},{7,5},{8,10},{9,11},{10,... | collective-permute-start | bytes 393224 | tf_op jit(solution)/shard_map/ppermute | solution.py:43
  82.9 7.9 %collective-permute-start.17 = (bf16[128,512]{1,0:T(8,128)(2,1)S(1)}, bf16[128,512]{1,0:T(8,128)(2,1)S(1)}, u32[]{:S(2)}, u32[]{:S(2)}) collective-permute-start(bf16[128,512]{1,0:T(8,128)(2,1)S(1)} %dynamic-slice_bitcast_fusion.3), channel_id=1, source_target_pairs={{0,16},{4,20},{8,24},{12,28},{16,0},{20,4},{24,8},{28,12},{1,17},{... | collective-permute-start | bytes 393224 | tf_op jit(solution)/shard_map/ppermute | solution.py:37
  94.2 1.4 collective-permute-start.18
  96.2 3.6 %collective-permute-start.19 = (f32[1,128]{1,0:T(1,128)S(1)}, f32[1,128]{1,0:T(1,128)S(1)}, u32[]{:S(2)}, u32[]{:S(2)}) collective-permute-start(f32[1,128]{1,0:T(1,128)S(1)} %add.106), channel_id=1, source_target_pairs={{0,8},{4,12},{8,0},{12,4},{16,24},{20,28},{24,16},{28,20},{1,9},{5... | collective-permute-start | bytes 1544 | tf_op jit(solution)/shard_map/ppermute | solution.py:37
  99.7 3.6 %collective-permute-start.20 = (f32[1,128]{1,0:T(1,128)S(1)}, f32[1,128]{1,0:T(1,128)S(1)}, u32[]{:S(2)}, u32[]{:S(2)}) collective-permute-start(f32[1,128]{1,0:T(1,128)S(1)} %add.107), channel_id=1, source_target_pairs={{0,16},{4,20},{8,24},{12,28},{16,0},{20,4},{24,8},{28,12},{1,17},{... | collective-permute-start | bytes 1544 | tf_op jit(solution)/shard_map/ppermute | solution.py:37
  103.3 3.6 %collective-permute-start.21 = (f32[1,128]{1,0:T(1,128)S(1)}, f32[1,128]{1,0:T(1,128)S(1)}, u32[]{:S(2)}, u32[]{:S(2)}) collective-permute-start(f32[1,128]{1,0:T(1,128)S(1)} %add.108), channel_id=1, source_target_pairs={{0,1},{1,0},{2,3},{3,2},{4,5},{5,4},{6,7},{7,6},{8,9},{9,8},{10,11... | collective-permute-start | bytes 1544 | tf_op jit(solution)/shard_map/ppermute | solution.py:43
  106.9 4.5 %collective-permute-start.22 = (f32[1,128]{1,0:T(1,128)S(1)}, f32[1,128]{1,0:T(1,128)S(1)}, u32[]{:S(2)}, u32[]{:S(2)}) collective-permute-start(f32[1,128]{1,0:T(1,128)S(1)} %add.109), channel_id=1, source_target_pairs={{0,2},{1,3},{2,0},{3,1},{4,6},{5,7},{6,4},{7,5},{8,10},{9,11},{10,... | collective-permute-start | bytes 1544 | tf_op jit(solution)/shard_map/ppermute | solution.py:43
  107.2 4.9 %collective-permute-start.23 = (bf16[128,512]{1,0:T(8,128)(2,1)}, bf16[128,512]{1,0:T(8,128)(2,1)S(1)}, u32[]{:S(2)}, u32[]{:S(2)}) collective-permute-start(bf16[128,512]{1,0:T(8,128)(2,1)} %get-tuple-element.49), channel_id=1, source_target_pairs={{1,16},{3,18},{5,20},{7,22},{9,24},{11,26},{13,28},{15,30},{16,1},... | collective-permute-start | bytes 393224 | tf_op jit(solution)/shard_map/ppermute | solution.py:576
  118.9 11.6 %collective-permute-start.28 = (bf16[128,512]{1,0:T(8,128)(2,1)}, bf16[128,512]{1,0:T(8,128)(2,1)S(1)}, u32[]{:S(2)}, u32[]{:S(2)}) collective-permute-start(bf16[128,512]{1,0:T(8,128)(2,1)} %get-tuple-element.52), channel_id=1, source_target_pairs={{0,1},{1,0},{3,2},{4,5},{5,4},{7,6},{8,9},{9,8},{11,10},{12,13},{1... | collective-permute-start | bytes 393224 | tf_op jit(solution)/shard_map/ppermute | solution.py:43
  125.0 15.5 %collective-permute-start.26 = (bf16[3,128,512]{2,1,0:T(8,128)(2,1)S(1)}, bf16[3,128,512]{2,1,0:T(8,128)(2,1)S(1)}, u32[]{:S(2)}, u32[]{:S(2)}) collective-permute-start(bf16[3,128,512]{2,1,0:T(8,128)(2,1)S(1)} %copy-done.5), channel_id=1, source_target_pairs={{0,24},{4,28},{8,16},{12,20},{16,8},{20,12},{24,0},{28,4},{1,25},{... | collective-permute-start | bytes 1179656 | tf_op jit(solution)/shard_map/ppermute | solution.py:37
  125.1 15.5 %collective-permute-start.25 = (bf16[3,128,512]{2,1,0:T(8,128)(2,1)S(1)}, bf16[3,128,512]{2,1,0:T(8,128)(2,1)S(1)}, u32[]{:S(2)}, u32[]{:S(2)}) collective-permute-start(bf16[3,128,512]{2,1,0:T(8,128)(2,1)S(1)} %copy-done.5), channel_id=1, source_target_pairs={{0,16},{4,20},{8,24},{12,28},{16,0},{20,4},{24,8},{28,12},{1,17},{... | collective-permute-start | bytes 1179656 | tf_op jit(solution)/shard_map/ppermute | solution.py:37
  127.3 13.2 %collective-permute-start.24 = (bf16[3,128,512]{2,1,0:T(8,128)(2,1)S(1)}, bf16[3,128,512]{2,1,0:T(8,128)(2,1)S(1)}, u32[]{:S(2)}, u32[]{:S(2)}) collective-permute-start(bf16[3,128,512]{2,1,0:T(8,128)(2,1)S(1)} %copy-done.5), channel_id=1, source_target_pairs={{0,8},{4,12},{8,0},{12,4},{16,24},{20,28},{24,16},{28,20},{1,9},{5... | collective-permute-start | bytes 1179656 | tf_op jit(solution)/shard_map/ppermute | solution.py:37
  128.6 8.8 %collective-permute-start.29 = (bf16[128,512]{1,0:T(8,128)(2,1)}, bf16[128,512]{1,0:T(8,128)(2,1)S(1)}, u32[]{:S(2)}, u32[]{:S(2)}) collective-permute-start(bf16[128,512]{1,0:T(8,128)(2,1)} %get-tuple-element.53), channel_id=1, source_target_pairs={{0,2},{2,0},{3,1},{4,6},{6,4},{7,5},{8,10},{10,8},{11,9},{12,14},{... | collective-permute-start | bytes 393224 | tf_op jit(solution)/shard_map/ppermute | solution.py:43
  130.5 9.0 %collective-permute-start.30 = (bf16[128,512]{1,0:T(8,128)(2,1)}, bf16[128,512]{1,0:T(8,128)(2,1)S(1)}, u32[]{:S(2)}, u32[]{:S(2)}) collective-permute-start(bf16[128,512]{1,0:T(8,128)(2,1)} %get-tuple-element.54), channel_id=1, source_target_pairs={{1,2},{2,1},{3,0},{5,6},{6,5},{7,4},{9,10},{10,9},{11,8},{13,14},{... | collective-permute-start | bytes 393224 | tf_op jit(solution)/shard_map/ppermute | solution.py:43
  140.4 24.5 %collective-permute-start.31 = (bf16[4,128,512]{2,1,0:T(8,128)(2,1)S(1)}, bf16[4,128,512]{2,1,0:T(8,128)(2,1)}, u32[]{:S(2)}, u32[]{:S(2)}) collective-permute-start(bf16[4,128,512]{2,1,0:T(8,128)(2,1)S(1)} %pad_maximum_fusion.3.own), channel_id=1, source_target_pairs={{0,4},{4,0},{8,12},{12,8},{16,20},{20,16},{24,28},{28,24},{1,5},{5... | collective-permute-start | bytes 1572872 | tf_op jit(solution)/shard_map/ppermute | solution.py:37
  146.2 7.5 %collective-permute-start.38 = (bf16[128,512]{1,0:T(8,128)(2,1)}, bf16[128,512]{1,0:T(8,128)(2,1)S(1)}, u32[]{:S(2)}, u32[]{:S(2)}) collective-permute-start(bf16[128,512]{1,0:T(8,128)(2,1)} %get-tuple-element.56), channel_id=1, source_target_pairs={{0,1},{1,0},{2,3},{3,2},{4,5},{5,4},{6,7},{7,6},{8,9},{9,8},{10,11... | collective-permute-start | bytes 393224 | tf_op jit(solution)/shard_map/ppermute | solution.py:43
  147.5 13.1 %collective-permute-start.39 = (bf16[128,512]{1,0:T(8,128)(2,1)}, bf16[128,512]{1,0:T(8,128)(2,1)S(1)}, u32[]{:S(2)}, u32[]{:S(2)}) collective-permute-start(bf16[128,512]{1,0:T(8,128)(2,1)} %get-tuple-element.57), channel_id=1, source_target_pairs={{0,2},{1,3},{2,0},{3,1},{4,6},{5,7},{6,4},{7,5},{8,10},{9,11},{10,... | collective-permute-start | bytes 393224 | tf_op jit(solution)/shard_map/ppermute | solution.py:43
  149.0 11.6 %collective-permute-start.40 = (bf16[128,512]{1,0:T(8,128)(2,1)}, bf16[128,512]{1,0:T(8,128)(2,1)S(1)}, u32[]{:S(2)}, u32[]{:S(2)}) collective-permute-start(bf16[128,512]{1,0:T(8,128)(2,1)} %get-tuple-element.58), channel_id=1, source_target_pairs={{0,3},{1,2},{2,1},{3,0},{4,7},{5,6},{6,5},{7,4},{8,11},{9,10},{10,... | collective-permute-start | bytes 393224 | tf_op jit(solution)/shard_map/ppermute | solution.py:43
  161.4 19.7 %collective-permute-start.42 = (bf16[3,128,512]{2,1,0:T(8,128)(2,1)}, bf16[3,128,512]{2,1,0:T(8,128)(2,1)S(1)}, u32[]{:S(2)}, u32[]{:S(2)}) collective-permute-start(bf16[3,128,512]{2,1,0:T(8,128)(2,1)} %get-tuple-element.66), channel_id=1, source_target_pairs={{0,16},{4,20},{8,24},{12,28},{16,0},{20,4},{24,8},{28,12},{1,17},{... | collective-permute-start | bytes 1179656 | tf_op jit(solution)/shard_map/ppermute | solution.py:37
  161.7 19.4 %collective-permute-start.41 = (bf16[3,128,512]{2,1,0:T(8,128)(2,1)}, bf16[3,128,512]{2,1,0:T(8,128)(2,1)S(1)}, u32[]{:S(2)}, u32[]{:S(2)}) collective-permute-start(bf16[3,128,512]{2,1,0:T(8,128)(2,1)} %get-tuple-element.66), channel_id=1, source_target_pairs={{0,8},{4,12},{8,0},{12,4},{16,24},{20,28},{24,16},{28,20},{1,9},{5... | collective-permute-start | bytes 1179656 | tf_op jit(solution)/shard_map/ppermute | solution.py:37
  162.7 18.5 %collective-permute-start.43 = (bf16[3,128,512]{2,1,0:T(8,128)(2,1)}, bf16[3,128,512]{2,1,0:T(8,128)(2,1)}, u32[]{:S(2)}, u32[]{:S(2)}) collective-permute-start(bf16[3,128,512]{2,1,0:T(8,128)(2,1)} %get-tuple-element.66), channel_id=1, source_target_pairs={{0,24},{4,28},{8,16},{12,20},{16,8},{20,12},{24,0},{28,4},{1,25},{... | collective-permute-start | bytes 1179656 | tf_op jit(solution)/shard_map/ppermute | solution.py:37
  172.8 5.0 %collective-permute-start.32 = (bf16[1,128,256]{2,1,0:T(8,128)(2,1)}, bf16[1,128,256]{2,1,0:T(8,128)(2,1)S(1)}, u32[]{:S(2)}, u32[]{:S(2)}) collective-permute-start(bf16[1,128,256]{2,1,0:T(8,128)(2,1)} %bitcast.76), channel_id=1, source_target_pairs={{0,1},{1,0},{2,3},{3,2},{4,5},{5,4},{6,7},{7,6},{8,9},{9,8},{10,11... | collective-permute-start | bytes 196616 | tf_op jit(solution)/shard_map/ppermute | solution.py:43
  175.3 23.0 %collective-permute-start.27 = (bf16[4,3,128,512]{3,2,1,0:T(8,128)(2,1)S(1)}, bf16[4,3,128,512]{3,2,1,0:T(8,128)(2,1)}, u32[]{:S(2)}, u32[]{:S(2)}) collective-permute-start(bf16[4,3,128,512]{3,2,1,0:T(8,128)(2,1)S(1)} %copy-done), channel_id=1, source_target_pairs={{0,4},{4,0},{8,12},{12,8},{16,20},{20,16},{24,28},{28,24},{1,5},{5... | collective-permute-start | bytes 4718600 | tf_op jit(solution)/shard_map/ppermute | solution.py:37
  179.3 6.2 %collective-permute-start.33 = (bf16[2,128,256]{2,1,0:T(8,128)(2,1)}, bf16[2,128,256]{2,1,0:T(8,128)(2,1)}, u32[]{:S(2)}, u32[]{:S(2)}) collective-permute-start(bf16[2,128,256]{2,1,0:T(8,128)(2,1)} %pad_maximum_fusion.8), channel_id=1, source_target_pairs={{0,2},{1,3},{2,0},{3,1},{4,6},{5,7},{6,4},{7,5},{8,10},{9,11},{10,... | collective-permute-start | bytes 393224 | tf_op jit(solution)/shard_map/ppermute | solution.py:43
  183.4 24.3 %copy-start.1 = (bf16[4,3,128,512]{3,2,1,0:T(8,128)(2,1)}, bf16[4,3,128,512]{3,2,1,0:T(8,128)(2,1)S(1)}, u32[]{:S(2)}) copy-start(bf16[4,3,128,512]{3,2,1,0:T(8,128)(2,1)S(1)} %pad_maximum_fusion.1.own_rows) | copy-start | bytes 4718596
  183.4 24.3 %collective-permute-start.44 = (bf16[4,3,128,512]{3,2,1,0:T(8,128)(2,1)S(1)}, bf16[4,3,128,512]{3,2,1,0:T(8,128)(2,1)}, u32[]{:S(2)}, u32[]{:S(2)}) collective-permute-start(bf16[4,3,128,512]{3,2,1,0:T(8,128)(2,1)S(1)} %pad_maximum_fusion.1.own_rows), channel_id=1, source_target_pairs={{0,4},{4,0},{8,12},{12,8},{16,20},{20,16},{24,28},{28,24},{1,5},{5... | collective-permute-start | bytes 4718600 | tf_op jit(solution)/shard_map/ppermute | solution.py:37
  186.5 7.6 %collective-permute-start.35 = (bf16[3,128,256]{2,1,0:T(8,128)(2,1)S(1)}, bf16[3,128,256]{2,1,0:T(8,128)(2,1)S(1)}, u32[]{:S(2)}, u32[]{:S(2)}) collective-permute-start(bf16[3,128,256]{2,1,0:T(8,128)(2,1)S(1)} %get-tuple-element.73), channel_id=1, source_target_pairs={{0,16},{4,20},{8,24},{12,28},{16,0},{20,4},{24,8},{28,12},{1,17},{... | collective-permute-start | bytes 589832 | tf_op jit(solution)/shard_map/ppermute | solution.py:37
  187.3 7.5 %collective-permute-start.34 = (bf16[3,128,256]{2,1,0:T(8,128)(2,1)S(1)}, bf16[3,128,256]{2,1,0:T(8,128)(2,1)S(1)}, u32[]{:S(2)}, u32[]{:S(2)}) collective-permute-start(bf16[3,128,256]{2,1,0:T(8,128)(2,1)S(1)} %get-tuple-element.73), channel_id=1, source_target_pairs={{0,8},{4,12},{8,0},{12,4},{16,24},{20,28},{24,16},{28,20},{1,9},{5... | collective-permute-start | bytes 589832 | tf_op jit(solution)/shard_map/ppermute | solution.py:37
  187.7 9.6 %collective-permute-start.36 = (bf16[3,128,256]{2,1,0:T(8,128)(2,1)S(1)}, bf16[3,128,256]{2,1,0:T(8,128)(2,1)S(1)}, u32[]{:S(2)}, u32[]{:S(2)}) collective-permute-start(bf16[3,128,256]{2,1,0:T(8,128)(2,1)S(1)} %get-tuple-element.73), channel_id=1, source_target_pairs={{0,24},{4,28},{8,16},{12,20},{16,8},{20,12},{24,0},{28,4},{1,25},{... | collective-permute-start | bytes 589832 | tf_op jit(solution)/shard_map/ppermute | solution.py:37
  198.4 9.4 %collective-permute-start.37 = (bf16[4,3,128,256]{3,2,1,0:T(8,128)(2,1)}, bf16[4,3,128,256]{3,2,1,0:T(8,128)(2,1)}, u32[]{:S(2)}, u32[]{:S(2)}) collective-permute-start(bf16[4,3,128,256]{3,2,1,0:T(8,128)(2,1)} %pad_maximum_fusion.2.own), channel_id=1, source_target_pairs={{0,4},{4,0},{8,12},{12,8},{16,20},{20,16},{24,28},{28,24},{1,5},{5... | collective-permute-start | bytes 2359304 | tf_op jit(solution)/shard_map/ppermute | solution.py:37
  (20 other events, 154.3 us)

commit v3 on v2

--- a/solution.py
+++ b/solution.py
@@ -52,8 +52,11 @@
 
 
 VMEM = pl.BlockSpec(memory_space=pltpu.VMEM)
-ANY = pl.BlockSpec(memory_space=pl.ANY)
+HBM = pl.BlockSpec(memory_space=pltpu.HBM)
 SMEM = pl.BlockSpec(memory_space=pltpu.SMEM)
+CHUNK = 16
+SMALL = pltpu.CompilerParams(vmem_limit_bytes=16 << 20)
+LARGE = pltpu.CompilerParams(vmem_limit_bytes=32 << 20)
 
 AT_CORE, AT_X, AT_Y, AT_Z, AT_CHIP, AT_SHARD, AT_PLACE, AT_LOW, AT_LISTS = range(9)
 
@@ -100,7 +103,7 @@
     terms = cotangents.shape[2]
     return pl.pallas_call(
         load_kernel,
-        in_specs=[SMEM, ANY, ANY],
+        in_specs=[SMEM, HBM, HBM],
         out_specs=[VMEM] * GROUPS,
         out_shape=[jax.ShapeDtypeStruct((tokens, width + terms), BF16)] * GROUPS,
         scratch_shapes=[pltpu.SemaphoreType.DMA((2 * GROUPS,))],
@@ -108,6 +111,7 @@
             flops=GROUPS * tokens * width * 100, bytes_accessed=4 * GROUPS * tokens * (width + terms),
             transcendentals=0,
         ),
+        compiler_params=SMALL,
         name="load_layers",
     )(jnp.stack(layers), activations, cotangents)
 
@@ -179,6 +183,7 @@
             flops=GROUPS * 2 * 2 * tokens * 2 * half * width, bytes_accessed=GROUPS * 12 * tokens * width,
             transcendentals=0,
         ),
+        compiler_params=LARGE,
         name="local_gradients",
     )(table, *mine, *sib)
 
@@ -196,6 +201,7 @@
         cost_estimate=pl.CostEstimate(
             flops=2 * 2 * tokens * 2 * half * width, bytes_accessed=12 * tokens * width, transcendentals=0
         ),
+        compiler_params=SMALL,
         name="layer_gradient",
     )(table, local, got, fwd)
 
@@ -239,17 +245,22 @@
             jax.ShapeDtypeStruct((1, 128), F32),
         ],
         cost_estimate=pl.CostEstimate(flops=1000 * got.size, bytes_accessed=8 * got.size, transcendentals=0),
+        compiler_params=SMALL,
         name="finish",
     )(table, *pairs)
 
 
-CHUNK = 16
-
-
-def momentum_kernel(table, factors, own, sib, momentum, momentum_out, nesterov):
+def momentum_kernel(table, factors, own, sib, momentum, momentum_out, nesterov, buffer, inputs, came, left, gone):
     core, chip = table[AT_CORE], table[AT_CHIP]
     half = own.shape[2]
-    for matrix in range(momentum.shape[0]):
+    mats = buffer.shape[0]
+    ins = [pltpu.make_async_copy(momentum.at[m], buffer.at[m], came.at[m]) for m in range(mats)]
+    outs = [pltpu.make_async_copy(buffer.at[m], momentum_out.at[m], left.at[m]) for m in range(mats)]
+    outs += [pltpu.make_async_copy(inputs.at[m], nesterov.at[m], gone.at[m]) for m in range(mats)]
+    for copy in ins:
+        copy.start()
+    for matrix in range(mats):
+        ins[matrix].wait()
         factor = factors[matrix]
         place, unit = chip_of(matrix) ^ chip, unit_of(matrix)
         for part, ref in ((core, own), (1 - core, sib)):
@@ -258,24 +269,36 @@
                 source = pl.ds(pl.multiple_of(i * CHUNK, CHUNK), CHUNK)
                 rows = pl.ds(pl.multiple_of(part * half + i * CHUNK, CHUNK), CHUNK)
                 step = factor * ref[place, unit, source, :].astype(F32)
-                fresh = momentum_rate * momentum[matrix, rows, :] + step
-                momentum_out[matrix, rows, :] = fresh
-                nesterov[matrix, rows, :] = (step + momentum_rate * fresh).astype(BF16)
+                fresh = momentum_rate * buffer[matrix, rows, :] + step
+                buffer[matrix, rows, :] = fresh
+                inputs[matrix, rows, :] = (step + momentum_rate * fresh).astype(BF16)
                 return carry
 
-            lax.fori_loop(0, half // CHUNK, chunk, 0, unroll=2)
+            lax.fori_loop(0, half // CHUNK, chunk, 0, unroll=4)
+        outs[matrix].start()
+        outs[mats + matrix].start()
+    for copy in outs:
+        copy.wait()
 
 
 def momentum_step(table, factors, own, sib, momentum):
     mats, rows, columns = momentum.shape
     return pl.pallas_call(
         momentum_kernel,
-        in_specs=[SMEM, SMEM, VMEM, VMEM, VMEM],
-        out_specs=[VMEM, VMEM],
+        in_specs=[SMEM, SMEM, VMEM, VMEM, HBM],
+        out_specs=[HBM, HBM],
         out_shape=[
             jax.ShapeDtypeStruct(momentum.shape, F32),
             jax.ShapeDtypeStruct(momentum.shape, BF16),
         ],
+        scratch_shapes=[
+            pltpu.VMEM(momentum.shape, F32),
+            pltpu.VMEM(momentum.shape, BF16),
+            pltpu.SemaphoreType.DMA((mats,)),
+            pltpu.SemaphoreType.DMA((mats,)),
+            pltpu.SemaphoreType.DMA((mats,)),
+        ],
+        compiler_params=LARGE,
         cost_estimate=pl.CostEstimate(
             flops=mats * rows * columns * 400, bytes_accessed=12 * mats * rows * columns, transcendentals=0
         ),
@@ -283,45 +306,57 @@
     )(table, factors, own, sib, momentum)
 
 
-def input_rows(table, factor, gradient, momentum, matrix, out):
-    half = out.shape[0]
-
-    def chunk(i, carry):
-        source = pl.ds(pl.multiple_of(i * CHUNK, CHUNK), CHUNK)
-        rows = pl.ds(pl.multiple_of(table[AT_CORE] * half + i * CHUNK, CHUNK), CHUNK)
-        step = factor * gradient(source).astype(F32)
-        fresh = momentum_rate * momentum[matrix, rows, :] + step
-        out[source, :] = (step + momentum_rate * fresh).astype(BF16)
-        return carry
-
-    lax.fori_loop(0, half // CHUNK, chunk, 0, unroll=2)
-
-
-def rows_kernel(table, factors, gradient, momentum, *outs):
-    for k, out in enumerate(outs):
-        unit = jnp.minimum(table[AT_SHARD] ^ k, GROUPS - 1)
-        matrix = matrix_of(table, unit)
-        input_rows(
-            table, factors[matrix], lambda rows, u=unit: gradient[u, rows, :], momentum, matrix, out
-        )
-
-
-def carried_kernel(table, factors, own, momentum, *outs):
-    for k, out in enumerate(outs):
-        matrix = table[AT_LISTS + (table[AT_SHARD] ^ (k + 1))]
-        place, unit = chip_of(matrix) ^ table[AT_CHIP], unit_of(matrix)
-        input_rows(
-            table, factors[matrix], lambda rows, p=place, u=unit: own[p, u, rows, :], momentum, matrix, out
-        )
+def input_rows(table, factors, gradients, matrices, momentum, outs, buffer, sems):
+    half = outs[0].shape[0]
+    part = pl.ds(pl.multiple_of(table[AT_CORE] * half, half), half)
+    copies = [
+        pltpu.make_async_copy(momentum.at[matrix, part, :], buffer.at[k], sems.at[k])
+        for k, matrix in enumerate(matrices)
+    ]
+    for copy in copies:
+        copy.start()
+    for k, (gradient, matrix, out) in enumerate(zip(gradients, matrices, outs)):
+        copies[k].wait()
+        factor = factors[matrix]
+
+        def chunk(i, carry):
+            rows = pl.ds(pl.multiple_of(i * CHUNK, CHUNK), CHUNK)
+            step = factor * gradient(rows).astype(F32)
+            fresh = momentum_rate * buffer[k, rows, :] + step
+            out[rows, :] = (step + momentum_rate * fresh).astype(BF16)
+            return carry
+
+        lax.fori_loop(0, half // CHUNK, chunk, 0, unroll=4)
+
+
+def rows_kernel(table, factors, gradient, momentum, *rest):
+    outs, (buffer, sems) = rest[:-2], rest[-2:]
+    units = [jnp.minimum(table[AT_SHARD] ^ k, GROUPS - 1) for k in range(len(outs))]
+    gradients = [lambda rows, u=unit: gradient[u, rows, :] for unit in units]
+    input_rows(
+        table, factors, gradients, [matrix_of(table, unit) for unit in units], momentum, outs, buffer, sems
+    )
+
+
+def carried_kernel(table, factors, own, momentum, *rest):
+    outs, (buffer, sems) = rest[:-2], rest[-2:]
+    matrices = [table[AT_LISTS + (table[AT_SHARD] ^ (k + 1))] for k in range(len(outs))]
+    gradients = [
+        lambda rows, p=chip_of(matrix) ^ table[AT_CHIP], u=unit_of(matrix): own[p, u, rows, :]
+        for matrix in matrices
+    ]
+    input_rows(table, factors, gradients, matrices, momentum, outs, buffer, sems)
 
 
 def make_rows(kernel, count, table, factors, gradient, momentum):
     half, columns = gradient.shape[-2:]
     return pl.pallas_call(
         kernel,
-        in_specs=[SMEM, SMEM, VMEM, VMEM],
+        in_specs=[SMEM, SMEM, VMEM, HBM],
         out_specs=[VMEM] * count,
         out_shape=[jax.ShapeDtypeStruct((half, columns), BF16)] * count,
+        scratch_shapes=[pltpu.VMEM((count, half, columns), F32), pltpu.SemaphoreType.DMA((count,))],
+        compiler_params=SMALL,
         cost_estimate=pl.CostEstimate(
             flops=count * half * columns * 100, bytes_accessed=8 * count * half * columns, transcendentals=0
         ),
@@ -377,6 +412,7 @@
             flops=ITERS * 2 * size * size * (2 * parts * columns + 3 * size),
             bytes_accessed=8 * size * parts * columns, transcendentals=0,
         ),
+        compiler_params=SMALL,
         name="newton",
     )(table, own, sib)
 
@@ -430,7 +466,7 @@
     return pl.pallas_call(
         functools.partial(apply_kernel, scale, AT_LISTS + shard_count),
         in_specs=[SMEM] + [VMEM] * 5,
-        out_specs=[ANY, ANY],
+        out_specs=[HBM, HBM],
         out_shape=[
             jax.ShapeDtypeStruct(values.shape, F32),
             jax.ShapeDtypeStruct((slots, rows, width), BF16),
@@ -446,6 +482,7 @@
             flops=2 * rows * rows * (mats * columns + slots * width),
             bytes_accessed=6 * mats * rows * columns + 2 * slots * rows * width, transcendentals=0,
         ),
+        compiler_params=LARGE,
         name="apply_step",
     )(table, own, sib, values, own_rows, sib_rows)
 

time: 216 us -> 203 us (0.940)
  Pallas kernels: 59.4 us -> 34 us
  local copies, waits for them, and re-layouts: 3.04 us -> 17.1 us
  other arithmetic: 14 us -> 6.39 us
  starting transfers between devices: 51.6 us -> 58.5 us
  waiting for transfers between devices: 86.5 us -> 84.1 us
    unnamed x46 -> x44, local copies, waits for them, and re-layouts: 2.2 us -> 16.9 us
    pallas_call x5, Pallas kernels: 24.9 us -> 10.4 us  [the longest x1 5.09 us: momentum_step(): pl.pallas_call(momentum_kernel, in_specs=[SMEM, SMEM, VMEM, VMEM, HBM], o...]
    ppermute x16, starting transfers between devices: 28.8 us -> 38 us  [swap_shard(): return lax.ppermute(value, 'shard', pairs)]
    ppermute x16, waiting for transfers between devices: 53.4 us -> 47.1 us  [swap_shard(): return lax.ppermute(value, 'shard', pairs)]
    ppermute x28, waiting for transfers between devices: 33 us -> 37 us  [swap_rep(): return lax.ppermute(value, 'rep', [(i, i ^ bit) for i in range(count)])]
    pallas_call x3, Pallas kernels: 11.5 us -> 7.96 us  [layer_gradient(): pl.pallas_call(functools.partial(gradient_kernel, group, width, blocks),...]
    pallas_call x1, Pallas kernels: 5.26 us -> 2.32 us  [local_gradients(): pl.pallas_call(functools.partial(local_kernel, width, blocks), in_specs=[...]
    another operation x4, other arithmetic: 4.16 us -> 1.53 us  [over_chips(): jnp.stack([value] + [swap_rep(value, BIT_X * k) for k in range(1, CHIPS)])]
  transfers between devices with their start and end apart: 45 -> 45, of which waited for: 24 -> 26; matrix products, arithmetic and copies ran while one was open for 5% -> 3% of each run, Pallas kernels for 19% -> 13%
where the time goes in v3:
time: 203 us; the launch traced here: 201 us
  waiting for transfers between devices  84.1 us (41%)
  starting transfers between devices  58.5 us (29%)
  Pallas kernels  34 us (17%)
  local copies, waits for them, and re-layouts  17.1 us (8%)
  other arithmetic  6.39 us (3%)
    ppermute x16, waiting for transfers between devices, swap_shard(): return lax.ppermute(value, 'shard', pairs)  47.1 us
    ppermute x16, starting transfers between devices, swap_shard(): return lax.ppermute(value, 'shard', pairs)  38 us
    ppermute x28, waiting for transfers between devices, swap_rep(): return lax.ppermute(value, 'rep', [(i, i ^ bit) for i in range(count)])  37 us
    ppermute x28, starting transfers between devices, swap_rep(): return lax.ppermute(value, 'rep', [(i, i ^ bit) for i in range(count)])  19.8 us
    unnamed x44, local copies, waits for them, and re-layouts  16.9 us
    pallas_call x3, Pallas kernels, layer_gradient(): pl.pallas_call(functools.partial(gradient_kernel, group, width, blocks),...  7.96 us
    pallas_call x1, Pallas kernels, newton(): pl.pallas_call(newton_kernel, in_specs=[SMEM, VMEM, VMEM], out_specs=VMEM...  6.52 us
    pallas_call x1, Pallas kernels, apply_step(): pl.pallas_call(functools.partial(apply_kernel, scale, AT_LISTS + shard_co...  5.98 us
  transfers between devices with their start and end apart: 45, of which 26 were waited for; matrix products, arithmetic and copies ran while one was open for 3% of the time, Pallas kernels for 13%

profile of v3, /device:TPU:0, one launch (start us, length us, event | category | flops | bytes accessed | tf_op | source)
XLA Modules:
  0.0 201.5 jit_solution(14842573635856500051)
XLA Ops:
  0.7 1.9 copy-done.2
  6.5 1.8 load_layers.3
  8.4 3.0 %collective-permute-start.3 = (bf16[128,2560]{1,0:T(8,128)(2,1)S(1)}, bf16[128,2560]{1,0:T(8,128)(2,1)}, u32[]{:S(2)}, u32[]{:S(2)}) collective-permute-start(bf16[128,2560]{1,0:T(8,128)(2,1)S(1)} %get-tuple-element.36), channel_id=1, source_target_pairs={{0,8},{4,12},{8,0},{12,4},{16,24},{20,28},{24,16},{28,20},{1,9},{5... | collective-permute-start | bytes 1966088 | tf_op jit(solution)/shard_map/ppermute | solution.py:37
  14.3 1.6 collective-permute-start.13
  15.9 10.4 %collective-permute-done.3.got = bf16[128,2560]{1,0:T(8,128)(2,1)} collective-permute-done((bf16[128,2560]{1,0:T(8,128)(2,1)S(1)}, bf16[128,2560]{1,0:T(8,128)(2,1)}, u32[]{:S(2)}, u32[]{:S(2)}) %collective-permute-start.3) | collective-permute-done | bytes 655392 | tf_op jit(solution)/shard_map/ppermute | solution.py:37
  28.0 3.3 %collective-permute-done.13.got = bf16[128,2560]{1,0:T(8,128)(2,1)S(1)} collective-permute-done((bf16[128,2560]{1,0:T(8,128)(2,1)}, bf16[128,2560]{1,0:T(8,128)(2,1)S(1)}, u32[]{:S(2)}, u32[]{:S(2)}) %collective-permute-start.13) | collective-permute-done | bytes 655392 | tf_op jit(solution)/shard_map/ppermute | solution.py:43
  35.8 2.3 %local_gradients.1 = (f32[256,2048]{1,0:T(8,128)S(1)}, f32[256,2048]{1,0:T(8,128)S(1)}, f32[256,2048]{1,0:T(8,128)S(1)}) custom-call(s32[20]{0:T(128)S(1)} %concatenate.13.table, bf16[128,2560]{1,0:T(8,128)(2,1)S(1)} %copy-done.7, bf16[128,2560]{1,0:T(8,128)(2,1)S(1)} %copy-done.9, bf16[128,2560]{1,0:T(8,128)(2,1)S(1)} %copy-done.11, ...), custom_call_target="tpu_custom_call" | custom-call | flops 805306368 | bytes 9437184 | tf_op jit(solution)/shard_map/local_gradients/pallas_call | solution.py:176
  38.2 2.6 %layer_gradient.3 = (bf16[4,128,512]{2,1,0:T(8,128)(2,1)S(1)}, bf16[4,128,512]{2,1,0:T(8,128)(2,1)}) custom-call(s32[20]{0:T(128)S(1)} %concatenate.13.table, f32[256,2048]{1,0:T(8,128)S(1)} %get-tuple-element.35.local, bf16[128,2560]{1,0:T(8,128)(2,1)} %collective-permute-done.3.got, bf16[128,2560]{1,0:T(8,128)(2,1)} %collective-permute-done.4.fwd), custom_call_target="tpu_custom_call" | custom-call | flops 268435456 | bytes 3145728 | tf_op jit(solution)/shard_map/layer_gradient/pallas_call | solution.py:195
  42.0 2.4 %layer_gradient.4 = (bf16[4,128,512]{2,1,0:T(8,128)(2,1)S(1)}, bf16[4,128,512]{2,1,0:T(8,128)(2,1)}) custom-call(s32[20]{0:T(128)S(1)} %concatenate.13.table, f32[256,2048]{1,0:T(8,128)S(1)} %get-tuple-element.39.local, bf16[128,2560]{1,0:T(8,128)(2,1)S(1)} %collective-permute-done.8.got, bf16[128,2560]{1,0:T(8,128)(2,1)} %collective-permute-done.9.fwd), custom_call_target="tpu_custom_call" | custom-call | flops 268435456 | bytes 3145728 | tf_op jit(solution)/shard_map/layer_gradient/pallas_call | solution.py:195
  45.6 3.0 %layer_gradient.5 = (bf16[2,2,128,512]{3,2,1,0:T(8,128)(2,1)S(1)}, bf16[2,2,128,512]{3,2,1,0:T(8,128)(2,1)S(1)}) custom-call(s32[20]{0:T(128)S(1)} %concatenate.13.table, f32[256,2048]{1,0:T(8,128)S(1)} %get-tuple-element.43.local, bf16[128,2560]{1,0:T(8,128)(2,1)S(1)} %collective-permute-done.13.got, bf16[128,2560]{1,0:T(8,128)(2,1)} %collective-permute-done.14.fwd), custom_call_target="tpu_custom_call" | custom-call | flops 268435456 | bytes 3145728 | tf_op jit(solution)/shard_map/layer_gradient/pallas_call | solution.py:195
  48.6 2.8 %collective-permute-start.15 = (bf16[2,2,128,512]{3,2,1,0:T(8,128)(2,1)S(1)}, bf16[2,2,128,512]{3,2,1,0:T(8,128)(2,1)S(1)}, u32[]{:S(2)}, u32[]{:S(2)}) collective-permute-start(bf16[2,2,128,512]{3,2,1,0:T(8,128)(2,1)S(1)} %get-tuple-element.46), channel_id=1, source_target_pairs={{0,2},{1,3},{2,0},{3,1},{4,6},{5,7},{6,4},{7,5},{8,10},{9,11},{10,... | collective-permute-start | bytes 1572872 | tf_op jit(solution)/shard_map/ppermute | solution.py:43
  51.4 4.8 %collective-permute-done.5 = bf16[4,128,512]{2,1,0:T(8,128)(2,1)} collective-permute-done((bf16[4,128,512]{2,1,0:T(8,128)(2,1)}, bf16[4,128,512]{2,1,0:T(8,128)(2,1)}, u32[]{:S(2)}, u32[]{:S(2)}) %collective-permute-start.5) | collective-permute-done | bytes 524320 | tf_op jit(solution)/shard_map/ppermute | solution.py:37
  57.4 1.6 collective-permute-start.6
  60.8 1.6 collective-permute-start.11
  62.5 12.3 %collective-permute-done.15 = bf16[2,2,128,512]{3,2,1,0:T(8,128)(2,1)S(1)} collective-permute-done((bf16[2,2,128,512]{3,2,1,0:T(8,128)(2,1)S(1)}, bf16[2,2,128,512]{3,2,1,0:T(8,128)(2,1)S(1)}, u32[]{:S(2)}, u32[]{:S(2)}) %collective-permute-start.15) | collective-permute-done | bytes 524320 | tf_op jit(solution)/shard_map/ppermute | solution.py:43
  75.0 1.6 collective-permute-start.16
  76.9 2.8 %collective-permute-start.7 = (bf16[128,512]{1,0:T(8,128)(2,1)S(1)}, bf16[128,512]{1,0:T(8,128)(2,1)S(1)}, u32[]{:S(2)}, u32[]{:S(2)}) collective-permute-start(bf16[128,512]{1,0:T(8,128)(2,1)S(1)} %dynamic-slice_bitcast_fusion.5), channel_id=1, source_target_pairs={{0,2},{1,3},{2,0},{3,1},{4,6},{5,7},{6,4},{7,5},{8,10},{9,11},{10,... | collective-permute-start | bytes 393224 | tf_op jit(solution)/shard_map/ppermute | solution.py:43
  79.7 3.8 %collective-permute-done.11 = bf16[2,128,512]{2,1,0:T(8,128)(2,1)S(1)} collective-permute-done((bf16[2,128,512]{2,1,0:T(8,128)(2,1)S(1)}, bf16[2,128,512]{2,1,0:T(8,128)(2,1)S(1)}, u32[]{:S(2)}, u32[]{:S(2)}) %collective-permute-start.11) | collective-permute-done | bytes 262176 | tf_op jit(solution)/shard_map/ppermute | solution.py:43
  83.6 3.3 %collective-permute-start.12 = (bf16[128,512]{1,0:T(8,128)(2,1)S(1)}, bf16[128,512]{1,0:T(8,128)(2,1)S(1)}, u32[]{:S(2)}, u32[]{:S(2)}) collective-permute-start(bf16[128,512]{1,0:T(8,128)(2,1)S(1)} %dynamic-slice_bitcast_fusion.4), channel_id=1, source_target_pairs={{0,2},{1,3},{2,0},{3,1},{4,6},{5,7},{6,4},{7,5},{8,10},{9,11},{10,... | collective-permute-start | bytes 393224 | tf_op jit(solution)/shard_map/ppermute | solution.py:43
  87.0 2.7 %collective-permute-done.12.got1 = bf16[128,512]{1,0:T(8,128)(2,1)S(1)} collective-permute-done((bf16[128,512]{1,0:T(8,128)(2,1)S(1)}, bf16[128,512]{1,0:T(8,128)(2,1)S(1)}, u32[]{:S(2)}, u32[]{:S(2)}) %collective-permute-start.12) | collective-permute-done | bytes 131104 | tf_op jit(solution)/shard_map/ppermute | solution.py:43
  89.8 2.2 %collective-permute-done.17.got2 = bf16[128,512]{1,0:T(8,128)(2,1)S(1)} collective-permute-done((bf16[128,512]{1,0:T(8,128)(2,1)S(1)}, bf16[128,512]{1,0:T(8,128)(2,1)S(1)}, u32[]{:S(2)}, u32[]{:S(2)}) %collective-permute-start.17) | collective-permute-done | bytes 131104 | tf_op jit(solution)/shard_map/ppermute | solution.py:37
  94.5 3.0 %collective-permute-done.19 = f32[1,128]{1,0:T(1,128)S(1)} collective-permute-done((f32[1,128]{1,0:T(1,128)S(1)}, f32[1,128]{1,0:T(1,128)S(1)}, u32[]{:S(2)}, u32[]{:S(2)}) %collective-permute-start.19) | collective-permute-done | bytes 544 | tf_op jit(solution)/shard_map/ppermute | solution.py:37
  97.8 3.4 %collective-permute-done.20 = f32[1,128]{1,0:T(1,128)S(1)} collective-permute-done((f32[1,128]{1,0:T(1,128)S(1)}, f32[1,128]{1,0:T(1,128)S(1)}, u32[]{:S(2)}, u32[]{:S(2)}) %collective-permute-start.20) | collective-permute-done | bytes 544 | tf_op jit(solution)/shard_map/ppermute | solution.py:37
  101.2 2.4 %collective-permute-start.21 = (f32[1,128]{1,0:T(1,128)S(1)}, f32[1,128]{1,0:T(1,128)S(1)}, u32[]{:S(2)}, u32[]{:S(2)}) collective-permute-start(f32[1,128]{1,0:T(1,128)S(1)} %add.108), channel_id=1, source_target_pairs={{0,1},{1,0},{2,3},{3,2},{4,5},{5,4},{6,7},{7,6},{8,9},{9,8},{10,11... | collective-permute-start | bytes 1544 | tf_op jit(solution)/shard_map/ppermute | solution.py:43
  107.0 2.6 %collective-permute-done.22 = f32[1,128]{1,0:T(1,128)S(1)} collective-permute-done((f32[1,128]{1,0:T(1,128)S(1)}, f32[1,128]{1,0:T(1,128)S(1)}, u32[]{:S(2)}, u32[]{:S(2)}) %collective-permute-start.22) | collective-permute-done | bytes 544 | tf_op jit(solution)/shard_map/ppermute | solution.py:43
  109.9 2.8 %copy-done = f32[12,256,512]{2,1,0:T(8,128)S(1)} copy-done((f32[12,256,512]{2,1,0:T(8,128)S(1)}, f32[12,256,512]{2,1,0:T(8,128)}, u32[]{:S(2)}) %copy-start) | copy-done | bytes 6291480
  113.7 8.4 %collective-permute-start.28 = (bf16[128,512]{1,0:T(8,128)(2,1)S(1)}, bf16[128,512]{1,0:T(8,128)(2,1)S(1)}, u32[]{:S(2)}, u32[]{:S(2)}) collective-permute-start(bf16[128,512]{1,0:T(8,128)(2,1)S(1)} %get-tuple-element.52), channel_id=1, source_target_pairs={{0,1},{1,0},{3,2},{4,5},{5,4},{7,6},{8,9},{9,8},{11,10},{12,13},{1... | collective-permute-start | bytes 393224 | tf_op jit(solution)/shard_map/ppermute | solution.py:43
  122.1 2.0 collective-permute-start.25
  125.6 1.9 collective-permute-start.29
  129.0 5.2 %collective-permute-done.29 = bf16[128,512]{1,0:T(8,128)(2,1)S(1)} collective-permute-done((bf16[128,512]{1,0:T(8,128)(2,1)S(1)}, bf16[128,512]{1,0:T(8,128)(2,1)S(1)}, u32[]{:S(2)}, u32[]{:S(2)}) %collective-permute-start.29) | collective-permute-done | bytes 131104 | tf_op jit(solution)/shard_map/ppermute | solution.py:43
  134.2 2.1 %collective-permute-done.30 = bf16[128,512]{1,0:T(8,128)(2,1)S(1)} collective-permute-done((bf16[128,512]{1,0:T(8,128)(2,1)S(1)}, bf16[128,512]{1,0:T(8,128)(2,1)S(1)}, u32[]{:S(2)}, u32[]{:S(2)}) %collective-permute-start.30) | collective-permute-done | bytes 131104 | tf_op jit(solution)/shard_map/ppermute | solution.py:43
  138.0 1.8 shard_map.77
  142.1 2.1 %collective-permute-start.40 = (bf16[128,512]{1,0:T(8,128)(2,1)S(1)}, bf16[128,512]{1,0:T(8,128)(2,1)S(1)}, u32[]{:S(2)}, u32[]{:S(2)}) collective-permute-start(bf16[128,512]{1,0:T(8,128)(2,1)S(1)} %get-tuple-element.58), channel_id=1, source_target_pairs={{0,3},{1,2},{2,1},{3,0},{4,7},{5,6},{6,5},{7,4},{8,11},{9,10},{10,... | collective-permute-start | bytes 393224 | tf_op jit(solution)/shard_map/ppermute | solution.py:43
  144.2 2.8 %collective-permute-done.38 = bf16[128,512]{1,0:T(8,128)(2,1)S(1)} collective-permute-done((bf16[128,512]{1,0:T(8,128)(2,1)S(1)}, bf16[128,512]{1,0:T(8,128)(2,1)S(1)}, u32[]{:S(2)}, u32[]{:S(2)}) %collective-permute-start.38) | collective-permute-done | bytes 131104 | tf_op jit(solution)/shard_map/ppermute | solution.py:43
  147.0 6.8 %collective-permute-done.39 = bf16[128,512]{1,0:T(8,128)(2,1)S(1)} collective-permute-done((bf16[128,512]{1,0:T(8,128)(2,1)S(1)}, bf16[128,512]{1,0:T(8,128)(2,1)S(1)}, u32[]{:S(2)}, u32[]{:S(2)}) %collective-permute-start.39) | collective-permute-done | bytes 131104 | tf_op jit(solution)/shard_map/ppermute | solution.py:43
  154.7 2.8 %collective-permute-start.43 = (bf16[3,128,512]{2,1,0:T(8,128)(2,1)S(1)}, bf16[3,128,512]{2,1,0:T(8,128)(2,1)S(1)}, u32[]{:S(2)}, u32[]{:S(2)}) collective-permute-start(bf16[3,128,512]{2,1,0:T(8,128)(2,1)S(1)} %get-tuple-element.66), channel_id=1, source_target_pairs={{0,24},{4,28},{8,16},{12,20},{16,8},{20,12},{24,0},{28,4},{1,25},{... | collective-permute-start | bytes 1179656 | tf_op jit(solution)/shard_map/ppermute | solution.py:37
  157.4 6.5 %newton.1 = bf16[128,256]{1,0:T(8,128)(2,1)S(1)} custom-call(s32[20]{0:T(128)S(1)} %concatenate.13.table, bf16[4,128,512]{2,1,0:T(8,128)(2,1)S(1)} %pad_maximum_fusion.3.own, bf16[4,128,512]{2,1,0:T(8,128)(2,1)S(1)} %collective-permute-done.31.sib), custom_call_target="tpu_custom_call" | custom-call | flops 3187671040 | bytes 4194304 | tf_op jit(solution)/shard_map/newton/pallas_call | solution.py:405
  164.0 2.7 %collective-permute-start.32 = (bf16[1,128,256]{2,1,0:T(8,128)(2,1)S(1)}, bf16[1,128,256]{2,1,0:T(8,128)(2,1)S(1)}, u32[]{:S(2)}, u32[]{:S(2)}) collective-permute-start(bf16[1,128,256]{2,1,0:T(8,128)(2,1)S(1)} %bitcast.69), channel_id=1, source_target_pairs={{0,1},{1,0},{2,3},{3,2},{4,5},{5,4},{6,7},{7,6},{8,9},{9,8},{10,11... | collective-permute-start | bytes 196616 | tf_op jit(solution)/shard_map/ppermute | solution.py:43
  166.6 2.2 %collective-permute-done.32 = bf16[1,128,256]{2,1,0:T(8,128)(2,1)S(1)} collective-permute-done((bf16[1,128,256]{2,1,0:T(8,128)(2,1)S(1)}, bf16[1,128,256]{2,1,0:T(8,128)(2,1)S(1)}, u32[]{:S(2)}, u32[]{:S(2)}) %collective-permute-start.32) | collective-permute-done | bytes 65568 | tf_op jit(solution)/shard_map/ppermute | solution.py:43
  168.9 1.9 collective-permute-start.33
  170.8 2.4 %collective-permute-done.43 = bf16[3,128,512]{2,1,0:T(8,128)(2,1)S(1)} collective-permute-done((bf16[3,128,512]{2,1,0:T(8,128)(2,1)S(1)}, bf16[3,128,512]{2,1,0:T(8,128)(2,1)S(1)}, u32[]{:S(2)}, u32[]{:S(2)}) %collective-permute-start.43) | collective-permute-done | bytes 393248 | tf_op jit(solution)/shard_map/ppermute | solution.py:37
  173.5 1.6 collective-permute-done.33
  177.2 2.4 %collective-permute-start.36 = (bf16[3,128,256]{2,1,0:T(8,128)(2,1)S(1)}, bf16[3,128,256]{2,1,0:T(8,128)(2,1)S(1)}, u32[]{:S(2)}, u32[]{:S(2)}) collective-permute-start(bf16[3,128,256]{2,1,0:T(8,128)(2,1)S(1)} %get-tuple-element.73), channel_id=1, source_target_pairs={{0,24},{4,28},{8,16},{12,20},{16,8},{20,12},{24,0},{28,4},{1,25},{... | collective-permute-start | bytes 589832 | tf_op jit(solution)/shard_map/ppermute | solution.py:37
  179.6 3.4 %collective-permute-done.35 = bf16[3,128,256]{2,1,0:T(8,128)(2,1)S(1)} collective-permute-done((bf16[3,128,256]{2,1,0:T(8,128)(2,1)S(1)}, bf16[3,128,256]{2,1,0:T(8,128)(2,1)S(1)}, u32[]{:S(2)}, u32[]{:S(2)}) %collective-permute-start.35) | collective-permute-done | bytes 196640 | tf_op jit(solution)/shard_map/ppermute | solution.py:37
  184.4 2.8 %collective-permute-done.36 = bf16[3,128,256]{2,1,0:T(8,128)(2,1)S(1)} collective-permute-done((bf16[3,128,256]{2,1,0:T(8,128)(2,1)S(1)}, bf16[3,128,256]{2,1,0:T(8,128)(2,1)S(1)}, u32[]{:S(2)}, u32[]{:S(2)}) %collective-permute-start.36) | collective-permute-done | bytes 196640 | tf_op jit(solution)/shard_map/ppermute | solution.py:37
  187.4 2.8 %copy-done.1 = f32[12,256,512]{2,1,0:T(8,128)S(1)} copy-done((f32[12,256,512]{2,1,0:T(8,128)S(1)}, f32[12,256,512]{2,1,0:T(8,128)}, u32[]{:S(2)}) %copy-start.1) | copy-done | bytes 6291480
  190.2 5.1 %momentum_step.1 = (f32[12,256,512]{2,1,0:T(8,128)}, bf16[12,256,512]{2,1,0:T(8,128)(2,1)S(1)}) custom-call(s32[20]{0:T(128)S(1)} %concatenate.13.table, f32[12]{0:T(128)S(1)} %multiply_minimum_fusion.factors, bf16[4,3,128,512]{3,2,1,0:T(8,128)(2,1)} %pad_maximum_fusion.own, bf16[4,3,128,512]{3,2,1,0:T(8,128)(2,1)S(1)} %collective-permute-done.27.sib, ...), custom_call_target="tpu_custom_call" | custom-call | flops 629145600 | bytes 18874368 | tf_op jit(solution)/shard_map/momentum_step/pallas_call | solution.py:286
  195.3 6.0 %apply_step.1 = (f32[12,256,512]{2,1,0:T(8,128)}, bf16[4,256,2048]{2,1,0:T(8,128)(2,1)}) custom-call(s32[20]{0:T(128)S(1)} %concatenate.13.table, bf16[4,3,128,256]{3,2,1,0:T(8,128)(2,1)S(1)} %pad_maximum_fusion.2.own, bf16[4,3,128,256]{3,2,1,0:T(8,128)(2,1)S(1)} %collective-permute-done.37.sib, bf16[12,256,512]{2,1,0:T(8,128)(2,1)S(1)} %get-tuple-element.55.values, ...), custom_call_target="tpu_custom_call" | custom-call | flops 1879048192 | bytes 13631488 | tf_op jit(solution)/shard_map/apply_step/pallas_call | solution.py:466
  (138 shorter events, 38.6 us)
Async XLA Ops:
  4.5 8.9 %collective-permute-start = (bf16[128,2560]{1,0:T(8,128)(2,1)S(1)}, bf16[128,2560]{1,0:T(8,128)(2,1)S(1)}, u32[]{:S(2)}, u32[]{:S(2)}) collective-permute-start(bf16[128,2560]{1,0:T(8,128)(2,1)S(1)} %get-tuple-element.32.mine0), channel_id=1, source_target_pairs={{0,4},{4,0},{8,12},{12,8},{16,20},{20,16},{24,28},{28,24},{1,5},{5... | collective-permute-start | bytes 1966088 | tf_op jit(solution)/shard_map/ppermute | solution.py:37
  8.4 17.9 %collective-permute-start.3 = (bf16[128,2560]{1,0:T(8,128)(2,1)S(1)}, bf16[128,2560]{1,0:T(8,128)(2,1)}, u32[]{:S(2)}, u32[]{:S(2)}) collective-permute-start(bf16[128,2560]{1,0:T(8,128)(2,1)S(1)} %get-tuple-element.36), channel_id=1, source_target_pairs={{0,8},{4,12},{8,0},{12,4},{16,24},{20,28},{24,16},{28,20},{1,9},{5... | collective-permute-start | bytes 1966088 | tf_op jit(solution)/shard_map/ppermute | solution.py:37
  11.4 16.4 %collective-permute-start.8 = (bf16[128,2560]{1,0:T(8,128)(2,1)}, bf16[128,2560]{1,0:T(8,128)(2,1)S(1)}, u32[]{:S(2)}, u32[]{:S(2)}) collective-permute-start(bf16[128,2560]{1,0:T(8,128)(2,1)} %get-tuple-element.40), channel_id=1, source_target_pairs={{0,16},{4,20},{8,24},{12,28},{16,0},{20,4},{24,8},{28,12},{1,17},{... | collective-permute-start | bytes 1966088 | tf_op jit(solution)/shard_map/ppermute | solution.py:37
  12.9 18.5 %collective-permute-start.1 = (bf16[128,2560]{1,0:T(8,128)(2,1)S(1)}, bf16[128,2560]{1,0:T(8,128)(2,1)}, u32[]{:S(2)}, u32[]{:S(2)}) collective-permute-start(bf16[128,2560]{1,0:T(8,128)(2,1)S(1)} %get-tuple-element.33.mine1), channel_id=1, source_target_pairs={{0,4},{4,0},{8,12},{12,8},{16,20},{20,16},{24,28},{28,24},{1,5},{5... | collective-permute-start | bytes 1966088 | tf_op jit(solution)/shard_map/ppermute | solution.py:37
  13.0 18.5 %collective-permute-start.2 = (bf16[128,2560]{1,0:T(8,128)(2,1)S(1)}, bf16[128,2560]{1,0:T(8,128)(2,1)}, u32[]{:S(2)}, u32[]{:S(2)}) collective-permute-start(bf16[128,2560]{1,0:T(8,128)(2,1)S(1)} %get-tuple-element.34.mine2), channel_id=1, source_target_pairs={{0,4},{4,0},{8,12},{12,8},{16,20},{20,16},{24,28},{28,24},{1,5},{5... | collective-permute-start | bytes 1966088 | tf_op jit(solution)/shard_map/ppermute | solution.py:37
  14.3 16.9 %collective-permute-start.13 = (bf16[128,2560]{1,0:T(8,128)(2,1)}, bf16[128,2560]{1,0:T(8,128)(2,1)S(1)}, u32[]{:S(2)}, u32[]{:S(2)}) collective-permute-start(bf16[128,2560]{1,0:T(8,128)(2,1)} %get-tuple-element.44), channel_id=1, source_target_pairs={{0,1},{1,0},{2,3},{3,2},{4,5},{5,4},{6,7},{7,6},{8,9},{9,8},{10,11... | collective-permute-start | bytes 1966088 | tf_op jit(solution)/shard_map/ppermute | solution.py:43
  26.3 11.9 %collective-permute-start.4 = (bf16[128,2560]{1,0:T(8,128)(2,1)}, bf16[128,2560]{1,0:T(8,128)(2,1)}, u32[]{:S(2)}, u32[]{:S(2)}) collective-permute-start(bf16[128,2560]{1,0:T(8,128)(2,1)} %collective-permute-done.3.got), channel_id=1, source_target_pairs={{0,4},{4,0},{8,12},{12,8},{16,20},{20,16},{24,28},{28,24},{1,5},{5... | collective-permute-start | bytes 1966088 | tf_op jit(solution)/shard_map/ppermute | solution.py:37
  27.8 14.2 %collective-permute-start.9 = (bf16[128,2560]{1,0:T(8,128)(2,1)S(1)}, bf16[128,2560]{1,0:T(8,128)(2,1)}, u32[]{:S(2)}, u32[]{:S(2)}) collective-permute-start(bf16[128,2560]{1,0:T(8,128)(2,1)S(1)} %collective-permute-done.8.got), channel_id=1, source_target_pairs={{0,4},{4,0},{8,12},{12,8},{16,20},{20,16},{24,28},{28,24},{1,5},{5... | collective-permute-start | bytes 1966088 | tf_op jit(solution)/shard_map/ppermute | solution.py:37
  31.2 14.4 %collective-permute-start.14 = (bf16[128,2560]{1,0:T(8,128)(2,1)S(1)}, bf16[128,2560]{1,0:T(8,128)(2,1)}, u32[]{:S(2)}, u32[]{:S(2)}) collective-permute-start(bf16[128,2560]{1,0:T(8,128)(2,1)S(1)} %collective-permute-done.13.got), channel_id=1, source_target_pairs={{0,4},{4,0},{8,12},{12,8},{16,20},{20,16},{24,28},{28,24},{1,5},{5... | collective-permute-start | bytes 1966088 | tf_op jit(solution)/shard_map/ppermute | solution.py:37
  41.5 14.6 %collective-permute-start.5 = (bf16[4,128,512]{2,1,0:T(8,128)(2,1)}, bf16[4,128,512]{2,1,0:T(8,128)(2,1)}, u32[]{:S(2)}, u32[]{:S(2)}) collective-permute-start(bf16[4,128,512]{2,1,0:T(8,128)(2,1)} %get-tuple-element.38), channel_id=1, source_target_pairs={{0,16},{4,20},{8,24},{12,28},{16,0},{20,4},{24,8},{28,12},{1,17},{... | collective-permute-start | bytes 1572872 | tf_op jit(solution)/shard_map/ppermute | solution.py:37
  45.2 14.4 %collective-permute-start.10 = (bf16[4,128,512]{2,1,0:T(8,128)(2,1)}, bf16[4,128,512]{2,1,0:T(8,128)(2,1)}, u32[]{:S(2)}, u32[]{:S(2)}) collective-permute-start(bf16[4,128,512]{2,1,0:T(8,128)(2,1)} %get-tuple-element.42), channel_id=1, source_target_pairs={{0,8},{4,12},{8,0},{12,4},{16,24},{20,28},{24,16},{28,20},{1,9},{5... | collective-permute-start | bytes 1572872 | tf_op jit(solution)/shard_map/ppermute | solution.py:37
  48.6 26.2 %collective-permute-start.15 = (bf16[2,2,128,512]{3,2,1,0:T(8,128)(2,1)S(1)}, bf16[2,2,128,512]{3,2,1,0:T(8,128)(2,1)S(1)}, u32[]{:S(2)}, u32[]{:S(2)}) collective-permute-start(bf16[2,2,128,512]{3,2,1,0:T(8,128)(2,1)S(1)} %get-tuple-element.46), channel_id=1, source_target_pairs={{0,2},{1,3},{2,0},{3,1},{4,6},{5,7},{6,4},{7,5},{8,10},{9,11},{10,... | collective-permute-start | bytes 1572872 | tf_op jit(solution)/shard_map/ppermute | solution.py:43
  57.4 19.3 %collective-permute-start.6 = (bf16[2,128,512]{2,1,0:T(8,128)(2,1)S(1)}, bf16[2,128,512]{2,1,0:T(8,128)(2,1)S(1)}, u32[]{:S(2)}, u32[]{:S(2)}) collective-permute-start(bf16[2,128,512]{2,1,0:T(8,128)(2,1)S(1)} %dynamic-slice_bitcast_fusion.2), channel_id=1, source_target_pairs={{0,1},{1,0},{2,3},{3,2},{4,5},{5,4},{6,7},{7,6},{8,9},{9,8},{10,11... | collective-permute-start | bytes 786440 | tf_op jit(solution)/shard_map/ppermute | solution.py:43
  60.8 22.6 %collective-permute-start.11 = (bf16[2,128,512]{2,1,0:T(8,128)(2,1)S(1)}, bf16[2,128,512]{2,1,0:T(8,128)(2,1)S(1)}, u32[]{:S(2)}, u32[]{:S(2)}) collective-permute-start(bf16[2,128,512]{2,1,0:T(8,128)(2,1)S(1)} %dynamic-slice_bitcast_fusion.1), channel_id=1, source_target_pairs={{0,1},{1,0},{2,3},{3,2},{4,5},{5,4},{6,7},{7,6},{8,9},{9,8},{10,11... | collective-permute-start | bytes 786440 | tf_op jit(solution)/shard_map/ppermute | solution.py:43
  75.0 11.8 %collective-permute-start.16 = (bf16[2,128,512]{2,1,0:T(8,128)(2,1)S(1)}, bf16[2,128,512]{2,1,0:T(8,128)(2,1)S(1)}, u32[]{:S(2)}, u32[]{:S(2)}) collective-permute-start(bf16[2,128,512]{2,1,0:T(8,128)(2,1)S(1)} %dynamic-slice_bitcast_fusion), channel_id=1, source_target_pairs={{0,8},{4,12},{8,0},{12,4},{16,24},{20,28},{24,16},{28,20},{1,9},{5... | collective-permute-start | bytes 786440 | tf_op jit(solution)/shard_map/ppermute | solution.py:37
  76.8 29.5 %copy-start.19 = (s32[2]{0:T(128)S(1)}, s32[2]{0:T(128)}, u32[]{:S(2)}) copy-start(s32[2]{0:T(128)} %param.9) | copy-start | bytes 28
  76.9 10.2 %collective-permute-start.7 = (bf16[128,512]{1,0:T(8,128)(2,1)S(1)}, bf16[128,512]{1,0:T(8,128)(2,1)S(1)}, u32[]{:S(2)}, u32[]{:S(2)}) collective-permute-start(bf16[128,512]{1,0:T(8,128)(2,1)S(1)} %dynamic-slice_bitcast_fusion.5), channel_id=1, source_target_pairs={{0,2},{1,3},{2,0},{3,1},{4,6},{5,7},{6,4},{7,5},{8,10},{9,11},{10,... | collective-permute-start | bytes 393224 | tf_op jit(solution)/shard_map/ppermute | solution.py:43
  83.6 6.2 %collective-permute-start.12 = (bf16[128,512]{1,0:T(8,128)(2,1)S(1)}, bf16[128,512]{1,0:T(8,128)(2,1)S(1)}, u32[]{:S(2)}, u32[]{:S(2)}) collective-permute-start(bf16[128,512]{1,0:T(8,128)(2,1)S(1)} %dynamic-slice_bitcast_fusion.4), channel_id=1, source_target_pairs={{0,2},{1,3},{2,0},{3,1},{4,6},{5,7},{6,4},{7,5},{8,10},{9,11},{10,... | collective-permute-start | bytes 393224 | tf_op jit(solution)/shard_map/ppermute | solution.py:43
  86.8 51.2 %slice-start = ((s8[6291456]{0:T(1024)(128)(4,1)}), s8[2097152]{0:T(1024)(128)(4,1)S(1)}, s32[]{:S(2)}) async-start(s8[6291456]{0:T(1024)(128)(4,1)} %bitcast.67), calls=%async_computation | async-start | bytes 4194304
  86.9 5.0 %collective-permute-start.17 = (bf16[128,512]{1,0:T(8,128)(2,1)S(1)}, bf16[128,512]{1,0:T(8,128)(2,1)S(1)}, u32[]{:S(2)}, u32[]{:S(2)}) collective-permute-start(bf16[128,512]{1,0:T(8,128)(2,1)S(1)} %dynamic-slice_bitcast_fusion.3), channel_id=1, source_target_pairs={{0,16},{4,20},{8,24},{12,28},{16,0},{20,4},{24,8},{28,12},{1,17},{... | collective-permute-start | bytes 393224 | tf_op jit(solution)/shard_map/ppermute | solution.py:37
  92.8 1.2 collective-permute-start.18
  94.0 3.6 %collective-permute-start.19 = (f32[1,128]{1,0:T(1,128)S(1)}, f32[1,128]{1,0:T(1,128)S(1)}, u32[]{:S(2)}, u32[]{:S(2)}) collective-permute-start(f32[1,128]{1,0:T(1,128)S(1)} %add.106), channel_id=1, source_target_pairs={{0,8},{4,12},{8,0},{12,4},{16,24},{20,28},{24,16},{28,20},{1,9},{5... | collective-permute-start | bytes 1544 | tf_op jit(solution)/shard_map/ppermute | solution.py:37
  97.6 3.6 %collective-permute-start.20 = (f32[1,128]{1,0:T(1,128)S(1)}, f32[1,128]{1,0:T(1,128)S(1)}, u32[]{:S(2)}, u32[]{:S(2)}) collective-permute-start(f32[1,128]{1,0:T(1,128)S(1)} %add.107), channel_id=1, source_target_pairs={{0,16},{4,20},{8,24},{12,28},{16,0},{20,4},{24,8},{28,12},{1,17},{... | collective-permute-start | bytes 1544 | tf_op jit(solution)/shard_map/ppermute | solution.py:37
  101.2 4.0 %collective-permute-start.21 = (f32[1,128]{1,0:T(1,128)S(1)}, f32[1,128]{1,0:T(1,128)S(1)}, u32[]{:S(2)}, u32[]{:S(2)}) collective-permute-start(f32[1,128]{1,0:T(1,128)S(1)} %add.108), channel_id=1, source_target_pairs={{0,1},{1,0},{2,3},{3,2},{4,5},{5,4},{6,7},{7,6},{8,9},{9,8},{10,11... | collective-permute-start | bytes 1544 | tf_op jit(solution)/shard_map/ppermute | solution.py:43
  105.2 4.5 %collective-permute-start.22 = (f32[1,128]{1,0:T(1,128)S(1)}, f32[1,128]{1,0:T(1,128)S(1)}, u32[]{:S(2)}, u32[]{:S(2)}) collective-permute-start(f32[1,128]{1,0:T(1,128)S(1)} %add.109), channel_id=1, source_target_pairs={{0,2},{1,3},{2,0},{3,1},{4,6},{5,7},{6,4},{7,5},{8,10},{9,11},{10,... | collective-permute-start | bytes 1544 | tf_op jit(solution)/shard_map/ppermute | solution.py:43
  106.4 3.4 %collective-permute-start.23 = (bf16[128,512]{1,0:T(8,128)(2,1)S(1)}, bf16[128,512]{1,0:T(8,128)(2,1)S(1)}, u32[]{:S(2)}, u32[]{:S(2)}) collective-permute-start(bf16[128,512]{1,0:T(8,128)(2,1)S(1)} %get-tuple-element.49), channel_id=1, source_target_pairs={{1,16},{3,18},{5,20},{7,22},{9,24},{11,26},{13,28},{15,30},{16,1},... | collective-permute-start | bytes 393224 | tf_op jit(solution)/shard_map/ppermute | solution.py:613
  112.7 25.3 %slice-start.1 = ((s8[6291456]{0:T(1024)(128)(4,1)}), s8[4194304]{0:T(1024)(128)(4,1)S(1)}, s32[]{:S(2)}) async-start(s8[6291456]{0:T(1024)(128)(4,1)} %bitcast.67), calls=%async_computation.1 | async-start | bytes 8388608
  113.7 13.8 %collective-permute-start.28 = (bf16[128,512]{1,0:T(8,128)(2,1)S(1)}, bf16[128,512]{1,0:T(8,128)(2,1)S(1)}, u32[]{:S(2)}, u32[]{:S(2)}) collective-permute-start(bf16[128,512]{1,0:T(8,128)(2,1)S(1)} %get-tuple-element.52), channel_id=1, source_target_pairs={{0,1},{1,0},{3,2},{4,5},{5,4},{7,6},{8,9},{9,8},{11,10},{12,13},{1... | collective-permute-start | bytes 393224 | tf_op jit(solution)/shard_map/ppermute | solution.py:43
  122.0 14.4 %collective-permute-start.26 = (bf16[3,128,512]{2,1,0:T(8,128)(2,1)S(1)}, bf16[3,128,512]{2,1,0:T(8,128)(2,1)S(1)}, u32[]{:S(2)}, u32[]{:S(2)}) collective-permute-start(bf16[3,128,512]{2,1,0:T(8,128)(2,1)S(1)} %get-tuple-element.68.gradient), channel_id=1, source_target_pairs={{0,24},{4,28},{8,16},{12,20},{16,8},{20,12},{24,0},{28,4},{1,25},{... | collective-permute-start | bytes 1179656 | tf_op jit(solution)/shard_map/ppermute | solution.py:37
  122.1 14.5 %collective-permute-start.25 = (bf16[3,128,512]{2,1,0:T(8,128)(2,1)S(1)}, bf16[3,128,512]{2,1,0:T(8,128)(2,1)S(1)}, u32[]{:S(2)}, u32[]{:S(2)}) collective-permute-start(bf16[3,128,512]{2,1,0:T(8,128)(2,1)S(1)} %get-tuple-element.68.gradient), channel_id=1, source_target_pairs={{0,16},{4,20},{8,24},{12,28},{16,0},{20,4},{24,8},{28,12},{1,17},{... | collective-permute-start | bytes 1179656 | tf_op jit(solution)/shard_map/ppermute | solution.py:37
  124.1 12.5 %collective-permute-start.24 = (bf16[3,128,512]{2,1,0:T(8,128)(2,1)S(1)}, bf16[3,128,512]{2,1,0:T(8,128)(2,1)S(1)}, u32[]{:S(2)}, u32[]{:S(2)}) collective-permute-start(bf16[3,128,512]{2,1,0:T(8,128)(2,1)S(1)} %get-tuple-element.68.gradient), channel_id=1, source_target_pairs={{0,8},{4,12},{8,0},{12,4},{16,24},{20,28},{24,16},{28,20},{1,9},{5... | collective-permute-start | bytes 1179656 | tf_op jit(solution)/shard_map/ppermute | solution.py:37
  125.6 8.6 %collective-permute-start.29 = (bf16[128,512]{1,0:T(8,128)(2,1)S(1)}, bf16[128,512]{1,0:T(8,128)(2,1)S(1)}, u32[]{:S(2)}, u32[]{:S(2)}) collective-permute-start(bf16[128,512]{1,0:T(8,128)(2,1)S(1)} %get-tuple-element.53), channel_id=1, source_target_pairs={{0,2},{2,0},{3,1},{4,6},{6,4},{7,5},{8,10},{10,8},{11,9},{12,14},{... | collective-permute-start | bytes 393224 | tf_op jit(solution)/shard_map/ppermute | solution.py:43
  127.5 8.8 %collective-permute-start.30 = (bf16[128,512]{1,0:T(8,128)(2,1)S(1)}, bf16[128,512]{1,0:T(8,128)(2,1)S(1)}, u32[]{:S(2)}, u32[]{:S(2)}) collective-permute-start(bf16[128,512]{1,0:T(8,128)(2,1)S(1)} %get-tuple-element.54), channel_id=1, source_target_pairs={{1,2},{2,1},{3,0},{5,6},{6,5},{7,4},{9,10},{10,9},{11,8},{13,14},{... | collective-permute-start | bytes 393224 | tf_op jit(solution)/shard_map/ppermute | solution.py:43
  136.4 21.1 %collective-permute-start.31 = (bf16[4,128,512]{2,1,0:T(8,128)(2,1)S(1)}, bf16[4,128,512]{2,1,0:T(8,128)(2,1)S(1)}, u32[]{:S(2)}, u32[]{:S(2)}) collective-permute-start(bf16[4,128,512]{2,1,0:T(8,128)(2,1)S(1)} %pad_maximum_fusion.3.own), channel_id=1, source_target_pairs={{0,4},{4,0},{8,12},{12,8},{16,20},{20,16},{24,28},{28,24},{1,5},{5... | collective-permute-start | bytes 1572872 | tf_op jit(solution)/shard_map/ppermute | solution.py:37
  139.8 7.2 %collective-permute-start.38 = (bf16[128,512]{1,0:T(8,128)(2,1)S(1)}, bf16[128,512]{1,0:T(8,128)(2,1)S(1)}, u32[]{:S(2)}, u32[]{:S(2)}) collective-permute-start(bf16[128,512]{1,0:T(8,128)(2,1)S(1)} %get-tuple-element.56), channel_id=1, source_target_pairs={{0,1},{1,0},{2,3},{3,2},{4,5},{5,4},{6,7},{7,6},{8,9},{9,8},{10,11... | collective-permute-start | bytes 393224 | tf_op jit(solution)/shard_map/ppermute | solution.py:43
  140.9 12.9 %collective-permute-start.39 = (bf16[128,512]{1,0:T(8,128)(2,1)S(1)}, bf16[128,512]{1,0:T(8,128)(2,1)S(1)}, u32[]{:S(2)}, u32[]{:S(2)}) collective-permute-start(bf16[128,512]{1,0:T(8,128)(2,1)S(1)} %get-tuple-element.57), channel_id=1, source_target_pairs={{0,2},{1,3},{2,0},{3,1},{4,6},{5,7},{6,4},{7,5},{8,10},{9,11},{10,... | collective-permute-start | bytes 393224 | tf_op jit(solution)/shard_map/ppermute | solution.py:43
  142.1 11.7 %collective-permute-start.40 = (bf16[128,512]{1,0:T(8,128)(2,1)S(1)}, bf16[128,512]{1,0:T(8,128)(2,1)S(1)}, u32[]{:S(2)}, u32[]{:S(2)}) collective-permute-start(bf16[128,512]{1,0:T(8,128)(2,1)S(1)} %get-tuple-element.58), channel_id=1, source_target_pairs={{0,3},{1,2},{2,1},{3,0},{4,7},{5,6},{6,5},{7,4},{8,11},{9,10},{10,... | collective-permute-start | bytes 393224 | tf_op jit(solution)/shard_map/ppermute | solution.py:43
  153.9 16.9 %collective-permute-start.42 = (bf16[3,128,512]{2,1,0:T(8,128)(2,1)S(1)}, bf16[3,128,512]{2,1,0:T(8,128)(2,1)S(1)}, u32[]{:S(2)}, u32[]{:S(2)}) collective-permute-start(bf16[3,128,512]{2,1,0:T(8,128)(2,1)S(1)} %get-tuple-element.66), channel_id=1, source_target_pairs={{0,16},{4,20},{8,24},{12,28},{16,0},{20,4},{24,8},{28,12},{1,17},{... | collective-permute-start | bytes 1179656 | tf_op jit(solution)/shard_map/ppermute | solution.py:37
  154.2 16.6 %collective-permute-start.41 = (bf16[3,128,512]{2,1,0:T(8,128)(2,1)S(1)}, bf16[3,128,512]{2,1,0:T(8,128)(2,1)S(1)}, u32[]{:S(2)}, u32[]{:S(2)}) collective-permute-start(bf16[3,128,512]{2,1,0:T(8,128)(2,1)S(1)} %get-tuple-element.66), channel_id=1, source_target_pairs={{0,8},{4,12},{8,0},{12,4},{16,24},{20,28},{24,16},{28,20},{1,9},{5... | collective-permute-start | bytes 1179656 | tf_op jit(solution)/shard_map/ppermute | solution.py:37
  154.7 18.5 %collective-permute-start.43 = (bf16[3,128,512]{2,1,0:T(8,128)(2,1)S(1)}, bf16[3,128,512]{2,1,0:T(8,128)(2,1)S(1)}, u32[]{:S(2)}, u32[]{:S(2)}) collective-permute-start(bf16[3,128,512]{2,1,0:T(8,128)(2,1)S(1)} %get-tuple-element.66), channel_id=1, source_target_pairs={{0,24},{4,28},{8,16},{12,20},{16,8},{20,12},{24,0},{28,4},{1,25},{... | collective-permute-start | bytes 1179656 | tf_op jit(solution)/shard_map/ppermute | solution.py:37
  164.0 4.9 %collective-permute-start.32 = (bf16[1,128,256]{2,1,0:T(8,128)(2,1)S(1)}, bf16[1,128,256]{2,1,0:T(8,128)(2,1)S(1)}, u32[]{:S(2)}, u32[]{:S(2)}) collective-permute-start(bf16[1,128,256]{2,1,0:T(8,128)(2,1)S(1)} %bitcast.69), channel_id=1, source_target_pairs={{0,1},{1,0},{2,3},{3,2},{4,5},{5,4},{6,7},{7,6},{8,9},{9,8},{10,11... | collective-permute-start | bytes 196616 | tf_op jit(solution)/shard_map/ppermute | solution.py:43
  166.6 20.8 %collective-permute-start.27 = (bf16[4,3,128,512]{3,2,1,0:T(8,128)(2,1)}, bf16[4,3,128,512]{3,2,1,0:T(8,128)(2,1)S(1)}, u32[]{:S(2)}, u32[]{:S(2)}) collective-permute-start(bf16[4,3,128,512]{3,2,1,0:T(8,128)(2,1)} %pad_maximum_fusion.own), channel_id=1, source_target_pairs={{0,4},{4,0},{8,12},{12,8},{16,20},{20,16},{24,28},{28,24},{1,5},{5... | collective-permute-start | bytes 4718600 | tf_op jit(solution)/shard_map/ppermute | solution.py:37
  168.9 6.2 %collective-permute-start.33 = (bf16[2,128,256]{2,1,0:T(8,128)(2,1)S(1)}, bf16[2,128,256]{2,1,0:T(8,128)(2,1)}, u32[]{:S(2)}, u32[]{:S(2)}) collective-permute-start(bf16[2,128,256]{2,1,0:T(8,128)(2,1)S(1)} %pad_maximum_fusion.8), channel_id=1, source_target_pairs={{0,2},{1,3},{2,0},{3,1},{4,6},{5,7},{6,4},{7,5},{8,10},{9,11},{10,... | collective-permute-start | bytes 393224 | tf_op jit(solution)/shard_map/ppermute | solution.py:43
  173.4 21.9 %collective-permute-start.44 = (bf16[4,3,128,512]{3,2,1,0:T(8,128)(2,1)S(1)}, bf16[4,3,128,512]{3,2,1,0:T(8,128)(2,1)}, u32[]{:S(2)}, u32[]{:S(2)}) collective-permute-start(bf16[4,3,128,512]{3,2,1,0:T(8,128)(2,1)S(1)} %pad_maximum_fusion.1.own_rows), channel_id=1, source_target_pairs={{0,4},{4,0},{8,12},{12,8},{16,20},{20,16},{24,28},{28,24},{1,5},{5... | collective-permute-start | bytes 4718600 | tf_op jit(solution)/shard_map/ppermute | solution.py:37
  176.1 6.9 %collective-permute-start.35 = (bf16[3,128,256]{2,1,0:T(8,128)(2,1)S(1)}, bf16[3,128,256]{2,1,0:T(8,128)(2,1)S(1)}, u32[]{:S(2)}, u32[]{:S(2)}) collective-permute-start(bf16[3,128,256]{2,1,0:T(8,128)(2,1)S(1)} %get-tuple-element.73), channel_id=1, source_target_pairs={{0,16},{4,20},{8,24},{12,28},{16,0},{20,4},{24,8},{28,12},{1,17},{... | collective-permute-start | bytes 589832 | tf_op jit(solution)/shard_map/ppermute | solution.py:37
  176.7 7.8 %collective-permute-start.34 = (bf16[3,128,256]{2,1,0:T(8,128)(2,1)S(1)}, bf16[3,128,256]{2,1,0:T(8,128)(2,1)S(1)}, u32[]{:S(2)}, u32[]{:S(2)}) collective-permute-start(bf16[3,128,256]{2,1,0:T(8,128)(2,1)S(1)} %get-tuple-element.73), channel_id=1, source_target_pairs={{0,8},{4,12},{8,0},{12,4},{16,24},{20,28},{24,16},{28,20},{1,9},{5... | collective-permute-start | bytes 589832 | tf_op jit(solution)/shard_map/ppermute | solution.py:37
  177.2 10.0 %collective-permute-start.36 = (bf16[3,128,256]{2,1,0:T(8,128)(2,1)S(1)}, bf16[3,128,256]{2,1,0:T(8,128)(2,1)S(1)}, u32[]{:S(2)}, u32[]{:S(2)}) collective-permute-start(bf16[3,128,256]{2,1,0:T(8,128)(2,1)S(1)} %get-tuple-element.73), channel_id=1, source_target_pairs={{0,24},{4,28},{8,16},{12,20},{16,8},{20,12},{24,0},{28,4},{1,25},{... | collective-permute-start | bytes 589832 | tf_op jit(solution)/shard_map/ppermute | solution.py:37
  187.3 8.0 %collective-permute-start.37 = (bf16[4,3,128,256]{3,2,1,0:T(8,128)(2,1)S(1)}, bf16[4,3,128,256]{3,2,1,0:T(8,128)(2,1)S(1)}, u32[]{:S(2)}, u32[]{:S(2)}) collective-permute-start(bf16[4,3,128,256]{3,2,1,0:T(8,128)(2,1)S(1)} %pad_maximum_fusion.2.own), channel_id=1, source_target_pairs={{0,4},{4,0},{8,12},{12,8},{16,20},{20,16},{24,28},{28,24},{1,5},{5... | collective-permute-start | bytes 2359304 | tf_op jit(solution)/shard_map/ppermute | solution.py:37
  (19 other events, 82.5 us)
